TPU v7x, 128 devices: a whole 4x4x4 slice. The times are simulated.
128 devices in a mesh: wide: 8 (over z, x_hi), narrow: 4 (over y), depth: 4 (over x_lo, core).
Axes of the slice: x: 4 (x_hi: 2, x_lo: 2; x = x_hi * 2 + x_lo), y: 4, z: 4, core: 2. Of those that a mesh axis runs over, the one named last changes fastest.
Arguments:
- hidden_in: bfloat16 [2048, 4096], P(('wide', 'narrow'), 'depth'), may hold values from -36 to 36
- queries: bfloat16 [2048, 4096], P('wide', ('narrow', 'depth')), may hold values from -8 to 8
- lang_ids: int32 [2048], replicated, may hold values from 0 to 7
- owner_slot: int32 [8], replicated, may hold values from 0 to 7, each once
- enc_kv: bfloat16 [8, 2, 768, 4096], P('wide', None, None, ('narrow', 'depth')), may hold values from -7 to 7
- attn_proj: bfloat16 [4096, 4096], P(('narrow', 'depth')), may hold values from -0.09375 to 0.09375
- norm_gain: float32 [4096], replicated, may hold values from 0.25 to 1.75
- router_proj: float32 [4096, 4], replicated, may hold values from -0.09375 to 0.09375
- expert_ids: int32 [2048, 2], P('wide'), may hold values from 0 to 3, all different within a row; in each aligned block of 64 rows (0 to 63, 64 to 127, ...) at most 48 rows name the same one
- proj_in: bfloat16 [4, 4096, 5120], P('narrow', None, 'depth'), may hold values from -0.09375 to 0.09375
- proj_out: bfloat16 [4, 5120, 4096], P('narrow', 'depth'), may hold values from -0.078125 to 0.078125
Outputs:
- layer_out: bfloat16 [2048, 4096], P(('wide', 'narrow'), 'depth')
Inputs may be any that keep to these rules, and one draw needn't show every extreme that they name: `owner_slot`: every slot once. `expert_ids`: each row names two different experts. Within each aligned block of 64 rows (the rows of one index of wide+narrow) no expert is named more than 48 times, a bound that some block reaches.
All inputs are finite; a program needn't handle non-finite values.
Results may differ from a plain program's by a relative error of at most 0.017.
Values may be sent and summed in bfloat16 or wider, within the bound.
No kernel may reach another device: no remote copies, remote signals or barrier semaphores. Data moves between devices by JAX's collectives and lax.ppermute only.
A program may use at most 128 MiB of HBM per device.

v0:
```python
import math

import jax
import jax.numpy as jnp
from jax import lax
from jax.sharding import PartitionSpec as P

HEAD_DIM = 64
CAP = 48


neg_big = -1e30
norm_eps = 1e-06


def in_order(blocks, dim):
    shape = list(blocks.shape[1:])
    shape[dim] *= blocks.shape[0]
    return jnp.moveaxis(blocks, 0, dim).reshape(shape)


def sent_to_all(value, axis):
    peers = lax.axis_size(axis)
    return lax.all_to_all(
        jnp.broadcast_to(value[None], (peers, *value.shape)), axis, 0, 0, tiled=True
    )


def collect(value, axis, dim):
    return in_order(sent_to_all(value, axis), dim)


def in_blocks(value, dim, peers):
    before, after = (value.shape[:dim], value.shape[dim + 1 :])
    return jnp.moveaxis(value.reshape(*before, peers, -1, *after), dim, 0)


def sum_at_owner(value, axis, dim):
    blocks = in_blocks(value, dim, lax.axis_size(axis))
    arrived = lax.all_to_all(blocks, axis, split_axis=0, concat_axis=0, tiled=True)
    return arrived.astype(jnp.float32).sum(axis=0)


def empty_state(row_count, head_count):
    return (
        jnp.full((row_count, head_count), neg_big, jnp.float32),
        jnp.zeros((row_count, head_count), jnp.float32),
        jnp.zeros((row_count, head_count, HEAD_DIM), jnp.float32),
    )


def slot_update(running, query_rows, key_rows, value_rows, is_live):
    run_max, run_sum, run_acc = running
    scores = jnp.einsum(
        "rhd,khd->rhk", query_rows, key_rows, preferred_element_type=jnp.float32
    ) * HEAD_DIM ** (-0.5)
    new_max = jnp.where(is_live[:, None], jnp.maximum(run_max, jnp.max(scores, axis=2)), run_max)
    weights = jnp.where(is_live[:, None, None], jnp.exp(scores - new_max[:, :, None]), 0.0)
    shrink = jnp.exp(run_max - new_max)
    run_sum = run_sum * shrink + jnp.sum(weights, axis=2)
    taken_sum = jnp.einsum(
        "rhk,khd->rhd", weights.astype(jnp.bfloat16), value_rows, preferred_element_type=jnp.float32
    )
    return (new_max, run_sum, run_acc * shrink[:, :, None] + taken_sum)


def slot_scan(running, kv_block, first_slot, query_rows, slot_tags):
    head_count = query_rows.shape[1]

    def visit_slot(carried, element):
        kv_pair, position = element
        key_rows = kv_pair[0].reshape(kv_pair.shape[1], head_count, HEAD_DIM)
        value_rows = kv_pair[1].reshape(kv_pair.shape[1], head_count, HEAD_DIM)
        return (slot_update(carried, query_rows, key_rows, value_rows, slot_tags == position), None)

    positions = first_slot + jnp.arange(kv_block.shape[0], dtype=jnp.int32)
    running, _ = lax.scan(visit_slot, running, (kv_block, positions))
    return running


def finish(running):
    run_max, run_sum, run_acc = running
    safe_sum = jnp.where(run_sum > 0.0, run_sum, 1.0)
    return (run_acc / safe_sum[:, :, None]).reshape(run_acc.shape[0], -1)


def assign_slots(choice_ids, experts):
    pick_flags = (
        choice_ids[:, :, None] == jnp.arange(experts, dtype=jnp.int32)[None, None, :]
    ).astype(jnp.int32)
    flat_flags = pick_flags.reshape(-1, experts)
    before = jnp.cumsum(flat_flags, axis=0) - flat_flags
    slot_rank = jnp.sum(before * flat_flags, axis=1).reshape(choice_ids.shape)
    return choice_ids * CAP + slot_rank


def make_worker(proj_in, proj_out, depth_count, quarter):
    experts_here = proj_in.shape[0]
    out_blocks = proj_out.reshape(experts_here, proj_out.shape[1], depth_count, quarter)

    def expert_ffn(arrived):
        sources = arrived.shape[0] // experts_here
        slot_count = arrived.shape[1]
        grid_rows = arrived.reshape(sources, experts_here, slot_count, arrived.shape[2])
        hidden_act = jnp.einsum(
            "secd,edf->secf", grid_rows, proj_in, preferred_element_type=jnp.float32
        )
        hidden_act = jax.nn.gelu(hidden_act, approximate=True).astype(jnp.bfloat16)
        expert_part = jnp.einsum(
            "secf,efgq->gsecq", hidden_act, out_blocks, preferred_element_type=jnp.float32
        )
        expert_part = expert_part.reshape(depth_count, sources * experts_here, slot_count, quarter)
        return expert_part

    return expert_ffn


def shards(
    hidden_in,
    queries,
    lang_ids,
    owner_slot,
    enc_kv,
    attn_proj,
    norm_gain,
    router_proj,
    expert_ids,
    proj_in,
    proj_out,
):
    narrow_count = lax.axis_size("narrow")
    depth_count = lax.axis_size("depth")
    tok_rows = hidden_in.shape[0]
    quarter = hidden_in.shape[1]
    head_count = queries.shape[1] // HEAD_DIM
    lang_count = owner_slot.shape[0]
    experts_here = proj_in.shape[0]
    experts = experts_here * narrow_count
    lang_match = lang_ids[:, None] == jnp.arange(lang_count, dtype=jnp.int32)[None, :]
    holder = jnp.sum(jnp.where(lang_match, owner_slot[None, :], 0), axis=1)
    first_slot = lax.axis_index("wide") * enc_kv.shape[0]
    segment = collect(queries, "wide", 0)
    row_count = segment.shape[0]
    block_rows = math.gcd(row_count, 512)

    def one_block(element):
        part_rows, part_tags = element
        running = slot_scan(
            empty_state(block_rows, head_count),
            enc_kv,
            first_slot,
            part_rows.reshape(block_rows, head_count, HEAD_DIM),
            part_tags,
        )
        return finish(running)

    blocks_out = lax.map(
        one_block,
        (
            segment.reshape(row_count // block_rows, block_rows, segment.shape[1]),
            holder.reshape(row_count // block_rows, block_rows),
        ),
    )
    partial_context = blocks_out.reshape(row_count, segment.shape[1])
    context = sum_at_owner(partial_context.astype(jnp.bfloat16), "wide", 0).astype(jnp.bfloat16)
    context_blocks = context.reshape(narrow_count, tok_rows, context.shape[1])
    proj_blocks = attn_proj.reshape(attn_proj.shape[0], depth_count, quarter)

    def pair_term(pair_index):
        row_block = lax.dynamic_index_in_dim(
            context_blocks, pair_index // depth_count, 0, keepdims=False
        )
        col_block = lax.dynamic_index_in_dim(
            proj_blocks, pair_index % depth_count, 1, keepdims=False
        )
        return jnp.dot(row_block, col_block, preferred_element_type=jnp.float32)

    pair_ids = jnp.arange(
        tok_rows * lax.axis_size(("narrow", "depth")) // tok_rows, dtype=jnp.int32
    )
    attn_out = sum_at_owner(
        lax.map(pair_term, pair_ids)
        .reshape(tok_rows * lax.axis_size(("narrow", "depth")), quarter)
        .astype(jnp.bfloat16),
        ("narrow", "depth"),
        0,
    )
    residual = (hidden_in.astype(jnp.float32) + attn_out).astype(jnp.bfloat16)
    full_rows = lax.all_gather(residual, "depth", axis=1, tiled=True).astype(jnp.float32)
    inv_norm = lax.rsqrt(jnp.mean(full_rows * full_rows, axis=1) + norm_eps)
    normed = (full_rows * inv_norm[:, None] * norm_gain[None, :]).astype(jnp.bfloat16)
    narrow_at = lax.axis_index("narrow")
    own_ids = lax.dynamic_slice_in_dim(expert_ids, narrow_at * tok_rows, tok_rows, 0)
    targets = assign_slots(own_ids, experts)
    lane_ids = jnp.arange(experts * CAP, dtype=jnp.int32)
    dispatch_mask = jnp.any(lane_ids[:, None, None] == targets[None, :, :], axis=2).astype(
        jnp.bfloat16
    )
    outbox = jnp.dot(dispatch_mask, normed, preferred_element_type=jnp.float32).astype(jnp.bfloat16)
    outbox = outbox.reshape(experts, CAP, normed.shape[1])
    worker = make_worker(proj_in, proj_out, depth_count, quarter)
    arrived_out = worker(lax.all_to_all(outbox, "narrow", split_axis=0, concat_axis=0, tiled=True))
    summed = sum_at_owner(arrived_out.astype(jnp.bfloat16), "depth", 0)
    returned = lax.all_to_all(
        summed.astype(jnp.bfloat16), "narrow", split_axis=1, concat_axis=1, tiled=True
    ).astype(summed.dtype)
    logits = jnp.dot(normed.astype(jnp.float32), router_proj, precision=lax.Precision.HIGHEST)
    pick_mask = own_ids[:, :, None] == jnp.arange(experts, dtype=jnp.int32)[None, None, :]
    own_logit = jnp.sum(jnp.where(pick_mask, logits[:, None, :], 0.0), axis=2)
    gates = jax.nn.sigmoid(own_logit - own_logit[:, ::-1])
    picked = jnp.take(
        returned.reshape(experts * CAP, quarter), targets.reshape(-1), axis=0
    ).reshape(tok_rows, 2, quarter)
    combined = jnp.sum(gates[:, :, None] * picked, axis=1)
    return (residual.astype(jnp.float32) + combined).astype(jnp.bfloat16)


def solution(mesh):
    return jax.shard_map(
        shards,
        mesh=mesh,
        in_specs=(
            P(("wide", "narrow"), "depth"),
            P("wide", ("narrow", "depth")),
            P(),
            P(),
            P("wide", None, None, ("narrow", "depth")),
            P(("narrow", "depth"), None),
            P(),
            P(),
            P("wide", None),
            P("narrow", None, "depth"),
            P("narrow", "depth", None),
        ),
        out_specs=P(("wide", "narrow"), "depth"),
        check_vma=False,
    )
```

profile of v0, /device:TPU:0, one launch (start us, length us, event | category | flops | bytes accessed | tf_op | source)
XLA Modules:
  0.0 258.0 jit_solution(7034597366299841906)
XLA Ops:
  0.0 2.0 broadcast_in_dim.114
  2.0 7.9 %all-to-all-start = ((bf16[8,256,256]{2,1,0:T(8,128)(2,1)}), bf16[8,256,256]{2,1,0:T(8,128)(2,1)S(1)}, u32[]{:S(2)}, u32[]{:S(2)}) async-start(bf16[8,256,256]{2,1,0:T(8,128)(2,1)} %broadcast_in_dim.114), calls=%async_computation | async-start | bytes 2097152 | tf_op jit(solution)/shard_map/all_to_all | solution.py:24
  12.1 15.0 %all-to-all-done = bf16[8,256,256]{2,1,0:T(8,128)(2,1)S(1)} async-done(((bf16[8,256,256]{2,1,0:T(8,128)(2,1)}), bf16[8,256,256]{2,1,0:T(8,128)(2,1)S(1)}, u32[]{:S(2)}, u32[]{:S(2)}) %all-to-all-start) | async-done | bytes 1048608 | tf_op jit(solution)/shard_map/all_to_all | solution.py:24
  27.1 20.3 %while.28 = (s32[]{:T(128)}, bf16[4,512,256]{2,1,0:T(8,128)(2,1)S(1)}, s32[4,512]{1,0:T(4,128)S(1)}, s32[]{:T(128)}, bf16[4,512,256]{2,1,0:T(8,128)(2,1)S(1)}, /*index=5*/bf16[1,2,768,256]{2,3,1,0:T(8,128)(2,1)S(1)}, s32[]{:T(128)}) while((s32[]{:T(128)}, bf16[4,512,256]{2,1,0:T(8,128)(2,1)S(1)}, s32[4,512]{1,0:T(4,128)S(1)}, s32[]{:T(128)}, ...), condition=%wide.region_4.5_spmd, body=%wide.region_1.4_spmd.sunk | while | flops 418789888 | bytes 23957604 | solution.py:157
  30.2 1.8 fusion.95
  35.3 1.8 fusion.95
  40.3 1.8 fusion.95
  48.4 3.6 %all-to-all-start.1 = ((bf16[8,256,256]{2,1,0:T(8,128)(2,1)}), bf16[8,256,256]{2,1,0:T(8,128)(2,1)S(1)}, u32[]{:S(2)}, u32[]{:S(2)}) async-start(bf16[8,256,256]{2,1,0:T(8,128)(2,1)} %bitcast.143), calls=%async_computation.1 | async-start | bytes 2097152 | tf_op jit(solution)/shard_map/all_to_all | solution.py:40
  51.9 3.3 %copy.53 = bf16[256,4096]{0,1:T(8,128)(2,1)S(1)} copy(bf16[256,4096]{1,0:T(8,128)(2,1)} %param.20) | data formatting | bytes 4194304 | tf_op args[5]
  55.2 13.2 %all-to-all-done.1 = bf16[8,256,256]{2,1,0:T(8,128)(2,1)S(1)} async-done(((bf16[8,256,256]{2,1,0:T(8,128)(2,1)}), bf16[8,256,256]{2,1,0:T(8,128)(2,1)S(1)}, u32[]{:S(2)}, u32[]{:S(2)}) %all-to-all-start.1) | async-done | bytes 1048608 | tf_op jit(solution)/shard_map/all_to_all | solution.py:40
  68.6 64.6 %while.29 = (s32[]{:T(128)}, bf16[16,64,1024]{2,1,0:T(8,128)(2,1)}, s32[16]{0:T(128)S(1)}, bf16[4,64,256]{2,1,0:T(8,128)(2,1)S(1)}, bf16[256,4,1024]{0,2,1:T(8,1...) while((s32[]{:T(128)}, bf16[16,64,1024]{2,1,0:T(8,128)(2,1)}, ...), condition=%wide.region_7.8_spmd, body=%wide.region_6.7_spmd.sunk | while | flops 33554456 | bytes 819596 | solution.py:182
  133.3 4.6 %all-to-all-start.2 = ((bf16[16,64,1024]{2,1,0:T(8,128)(2,1)}), bf16[16,64,1024]{2,1,0:T(8,128)(2,1)S(1)}, u32[]{:S(2)}, u32[]{:S(2)}) async-start(bf16[16,64,1024]{2,1,0:T(8,128)(2,1)} %get-tuple-element.130), calls=%async_computation.2 | async-start | bytes 4194304 | tf_op jit(solution)/shard_map/all_to_all | solution.py:40
  139.1 26.6 %all-to-all-done.2 = bf16[16,64,1024]{2,1,0:T(8,128)(2,1)S(1)} async-done(((bf16[16,64,1024]{2,1,0:T(8,128)(2,1)}), bf16[16,64,1024]{2,1,0:T(8,128)(2,1)S(1)}, u32[]{:S(2)}, u32[]{:S(2)}) %all-to-all-start.2) | async-done | bytes 2097184 | tf_op jit(solution)/shard_map/all_to_all | solution.py:40
  166.1 6.5 %all_gather.3 = bf16[64,4096]{1,0:T(8,128)(2,1)S(1)} all-gather(bf16[64,1024]{1,0:T(8,128)(2,1)S(1)} %add_convert_fusion.1), channel_id=1, replica_groups=mesh['wide'=8,'narrow'=4,'depth'=4] {'depth'}, dimensions={1}, use_global_device_ids=true | all-gather | bytes 655360 | tf_op jit(solution)/shard_map/all_gather | solution.py:189
  172.8 1.8 convolution_convert_fusion
  174.6 3.7 %all-to-all-start.3 = ((bf16[4,48,4096]{2,1,0:T(8,128)(2,1)}), bf16[4,48,4096]{2,1,0:T(8,128)(2,1)S(1)}, u32[]{:S(2)}, u32[]{:S(2)}) async-start(bf16[4,48,4096]{2,1,0:T(8,128)(2,1)} %bitcast.14), calls=%async_computation.3 | async-start | bytes 3145728 | tf_op jit(solution)/shard_map/all_to_all | solution.py:202
  178.4 17.8 %reshape.205 = bf16[1280,4,1024]{2,1,0:T(4,128)(2,1)} reshape(bf16[1,1280,4096]{2,1,0:T(8,128)(2,1)} %param.25) | data formatting | bytes 20971520 | tf_op jit(solution)/shard_map/reshape.14
  196.2 3.5 %all-to-all-done.3 = bf16[4,48,4096]{2,1,0:T(8,128)(2,1)S(1)} async-done(((bf16[4,48,4096]{2,1,0:T(8,128)(2,1)}), bf16[4,48,4096]{2,1,0:T(8,128)(2,1)S(1)}, u32[]{:S(2)}, u32[]{:S(2)}) %all-to-all-start.3) | async-done | bytes 1572896 | tf_op jit(solution)/shard_map/all_to_all | solution.py:202
  199.7 16.7 %fusion.35 = bf16[4,1,4,48,1024]{4,3,0,2,1:T(8,128)(2,1)} fusion(bf16[1280,4,1024]{2,1,0:T(4,128)(2,1)} %reshape.205, bf16[4,48,4096]{2,1,0:T(8,128)(2,1)S(1)} %all-to-all-done.3, bf16[1,4096,1280]{2,1,0:T(8,128)(2,1)} %param.24), kind=kOutput, calls=%fused_computation.36 | convolution fusion | flops 4029530112 | bytes 24117248 | tf_op jit(solution)/shard_map/secf,efgq->gsecq/dot_general | solution.py:109
  216.4 2.7 %copy.60 = bf16[4,1,4,48,1024]{4,3,2,1,0:T(8,128)(2,1)} copy(bf16[4,1,4,48,1024]{4,3,0,2,1:T(8,128)(2,1)} %fusion.35) | data formatting | bytes 3145728 | tf_op jit(solution)/shard_map/convert_element_type | solution.py:203
  219.1 3.6 %all-to-all-start.4 = ((bf16[4,1,4,48,1024]{4,3,2,1,0:T(8,128)(2,1)}), bf16[4,1,4,48,1024]{4,3,2,1,0:T(8,128)(2,1)S(1)}, u32[]{:S(2)}, u32[]{:S(2)}) async-start(bf16[4,1,4,48,1024]{4,3,2,1,0:T(8,128)(2,1)} %copy.60), calls=%async_computation.4 | async-start | bytes 3145728 | tf_op jit(solution)/shard_map/all_to_all | solution.py:40
  223.6 19.0 %all-to-all-done.4 = bf16[4,1,4,48,1024]{4,3,2,1,0:T(8,128)(2,1)S(1)} async-done(((bf16[4,1,4,48,1024]{4,3,2,1,0:T(8,128)(2,1)}), bf16[4,1,4,48,1024]{4,3,2,1,0:T(8,128)(2,1)S(1)}, u32[]{:S(2)}, u32[]{:S(2)}) %all-to-all-start.4) | async-done | bytes 1572896 | tf_op jit(solution)/shard_map/all_to_all | solution.py:40
  243.8 3.5 %all-to-all-start.5 = ((bf16[1,4,48,1024]{3,2,0,1:T(8,128)(2,1)}), bf16[1,4,48,1024]{3,2,0,1:T(8,128)(2,1)S(1)}, u32[]{:S(2)}, u32[]{:S(2)}) async-start(bf16[1,4,48,1024]{3,2,0,1:T(8,128)(2,1)} %bitcast.30), calls=%async_computation.5 | async-start | bytes 786432 | tf_op jit(solution)/shard_map/all_to_all | solution.py:204
  247.4 7.9 %all-to-all-done.5 = bf16[1,4,48,1024]{3,2,0,1:T(8,128)(2,1)S(1)} async-done(((bf16[1,4,48,1024]{3,2,0,1:T(8,128)(2,1)}), bf16[1,4,48,1024]{3,2,0,1:T(8,128)(2,1)S(1)}, u32[]{:S(2)}, u32[]{:S(2)}) %all-to-all-start.5) | async-done | bytes 393248 | tf_op jit(solution)/shard_map/all_to_all | solution.py:204
  (120 shorter events, 49.3 us)
Async XLA Ops:
  0.0 223.0 %copy-start = (f32[4096,4]{0,1:T(4,128)S(1)}, f32[4096,4]{0,1:T(4,128)}, u32[]{:S(2)}) copy-start(f32[4096,4]{0,1:T(4,128)} %param.22) | copy-start | bytes 196612
  2.0 25.1 %all-to-all-start = ((bf16[8,256,256]{2,1,0:T(8,128)(2,1)}), bf16[8,256,256]{2,1,0:T(8,128)(2,1)S(1)}, u32[]{:S(2)}, u32[]{:S(2)}) async-start(bf16[8,256,256]{2,1,0:T(8,128)(2,1)} %broadcast_in_dim.114), calls=%async_computation | async-start | bytes 2097152 | tf_op jit(solution)/shard_map/all_to_all | solution.py:24
  47.4 1.0 copy-start.1
  48.4 20.1 %all-to-all-start.1 = ((bf16[8,256,256]{2,1,0:T(8,128)(2,1)}), bf16[8,256,256]{2,1,0:T(8,128)(2,1)S(1)}, u32[]{:S(2)}, u32[]{:S(2)}) async-start(bf16[8,256,256]{2,1,0:T(8,128)(2,1)} %bitcast.143), calls=%async_computation.1 | async-start | bytes 2097152 | tf_op jit(solution)/shard_map/all_to_all | solution.py:40
  51.9 85.9 %copy-start.4 = (s32[256,2]{0,1:T(2,128)S(1)}, s32[256,2]{0,1:T(2,128)}, u32[]{:S(2)}) copy-start(s32[256,2]{0,1:T(2,128)} %param.23) | copy-start | bytes 6148
  55.2 110.8 %copy-start.2 = (bf16[64,1024]{1,0:T(8,128)(2,1)S(1)}, bf16[64,1024]{1,0:T(8,128)(2,1)}, u32[]{:S(2)}) copy-start(bf16[64,1024]{1,0:T(8,128)(2,1)} %param.15) | copy-start | bytes 393220
  68.6 104.2 %copy-start.3 = (f32[4096]{0:T(1024)S(1)}, f32[4096]{0:T(1024)}, u32[]{:S(2)}) copy-start(f32[4096]{0:T(1024)} %param.21) | copy-start | bytes 49156
  133.3 32.4 %all-to-all-start.2 = ((bf16[16,64,1024]{2,1,0:T(8,128)(2,1)}), bf16[16,64,1024]{2,1,0:T(8,128)(2,1)S(1)}, u32[]{:S(2)}, u32[]{:S(2)}) async-start(bf16[16,64,1024]{2,1,0:T(8,128)(2,1)} %get-tuple-element.130), calls=%async_computation.2 | async-start | bytes 4194304 | tf_op jit(solution)/shard_map/all_to_all | solution.py:40
  174.6 25.0 %all-to-all-start.3 = ((bf16[4,48,4096]{2,1,0:T(8,128)(2,1)}), bf16[4,48,4096]{2,1,0:T(8,128)(2,1)S(1)}, u32[]{:S(2)}, u32[]{:S(2)}) async-start(bf16[4,48,4096]{2,1,0:T(8,128)(2,1)} %bitcast.14), calls=%async_computation.3 | async-start | bytes 3145728 | tf_op jit(solution)/shard_map/all_to_all | solution.py:202
  219.1 23.6 %all-to-all-start.4 = ((bf16[4,1,4,48,1024]{4,3,2,1,0:T(8,128)(2,1)}), bf16[4,1,4,48,1024]{4,3,2,1,0:T(8,128)(2,1)S(1)}, u32[]{:S(2)}, u32[]{:S(2)}) async-start(bf16[4,1,4,48,1024]{4,3,2,1,0:T(8,128)(2,1)} %copy.60), calls=%async_computation.4 | async-start | bytes 3145728 | tf_op jit(solution)/shard_map/all_to_all | solution.py:40
  243.8 11.5 %all-to-all-start.5 = ((bf16[1,4,48,1024]{3,2,0,1:T(8,128)(2,1)}), bf16[1,4,48,1024]{3,2,0,1:T(8,128)(2,1)S(1)}, u32[]{:S(2)}, u32[]{:S(2)}) async-start(bf16[1,4,48,1024]{3,2,0,1:T(8,128)(2,1)} %bitcast.30), calls=%async_computation.5 | async-start | bytes 786432 | tf_op jit(solution)/shard_map/all_to_all | solution.py:204
where the time goes:
time: 260 us; the launch traced here: 258 us
  waiting for transfers between devices  85.2 us (33%)
  matrix products  45.8 us (18%)
  local copies, waits for them, and re-layouts  41.3 us (16%)
  loops' own time  40.3 us (15%)
  starting transfers between devices  26.8 us (10%)
  other arithmetic  11.9 us (5%)
  blocking collectives  6.5 us (2%)
    all_to_all x3, waiting for transfers between devices, sum_at_owner(): lax.all_to_all(blocks, axis, split_axis=0, concat_axis=0, tiled=True)  58.9 us
    another operation x1, loops' own time, shards(): lax.map(pair_term, pair_ids)  40.1 us
    another operation x1, local copies, waits for them, and re-layouts  17.8 us
    dot_general x1, matrix products, expert_ffn(): jnp.einsum('secf,efgq->gsecq', hidden_act, out_blocks, preferred_element_...  16.7 us
    dot_general x16, matrix products, pair_term(): return jnp.dot(row_block, col_block, preferred_element_type=jnp.float32)  15.1 us
    all_to_all x1, waiting for transfers between devices, sent_to_all(): lax.all_to_all(jnp.broadcast_to(value[None], (peers, *value.shape)), axis...  15 us
    all_to_all x3, starting transfers between devices, sum_at_owner(): lax.all_to_all(blocks, axis, split_axis=0, concat_axis=0, tiled=True)  11.7 us
    dynamic_slice x16, local copies, waits for them, and re-layouts, shards(): lax.map(pair_term, pair_ids)  9.44 us
  transfers between devices with their start and end apart: 6, of which 6 were waited for; matrix products, arithmetic and copies ran while one was open for 10% of the time, Pallas kernels for 0%

commit v1 on v0

v1 whole, which is shorter than its diff:
```python
import functools

import jax
import jax.numpy as jnp
from jax import lax
from jax.experimental import pallas as pl
from jax.experimental.pallas import tpu as pltpu
from jax.sharding import PartitionSpec as P

HEAD_DIM = 64
CAP = 48
norm_eps = 1e-06
F32 = jnp.float32
BF16 = jnp.bfloat16
ROWS_BLOCK = 256
LIMIT = 60 * 1024 * 1024


def dot(a, b):
    return jnp.dot(a, b, preferred_element_type=F32)


def iota(shape, dim):
    return lax.broadcasted_iota(jnp.int32, shape, dim)


def one_hot(flags):
    return jnp.where(flags, 1.0, 0.0).astype(BF16)


def vmem(*shape_dtype):
    return pltpu.VMEM(*shape_dtype)


def attend_kernel(place, slot_of, lang_ref, q_ref, kt_ref, v_ref, out_ref, packed, attended):
    sources, rows, width = q_ref.shape
    heads = width // HEAD_DIM
    span = rows + 16
    wide_span = rows + 128
    langs = lang_ref[...]
    holder = jnp.zeros_like(langs)
    for lang in range(slot_of.shape[0]):
        holder = jnp.where(langs == lang, slot_of[lang], holder)
    mine = holder == place[0]
    upto = one_hot(iota((rows, rows), 0) <= iota((rows, rows), 1))
    within = dot(one_hot(mine), upto)
    counts = within[:, rows - 1 :]
    begins = [jnp.int32(0)]
    before = jnp.zeros((sources, 1), F32)
    for source in range(sources):
        count = counts[source : source + 1, :]
        before = before + jnp.where(iota((sources, 1), 0) > source, count, 0.0)
        begins.append(begins[-1] + jnp.sum(count).astype(jnp.int32))
    pos = jnp.where(mine, within - 1.0 + before, -1.0)
    pos_row = pos.astype(jnp.int32)
    pos_col = pos.T.astype(jnp.int32)
    packed[...] = jnp.zeros_like(packed)
    attended[...] = jnp.zeros_like(attended)
    for source in range(sources):
        at = pl.multiple_of((begins[source] // 16) * 16, 16)
        pick = one_hot(iota((span, rows), 0) + at == pos_row[source : source + 1, :])
        moved = dot(pick, q_ref[source]).astype(BF16)
        packed[pl.ds(at, span), :] += moved

    head_of = iota((1, width), 1) // HEAD_DIM

    def block(index, _):
        here = pl.ds(pl.multiple_of(index * ROWS_BLOCK, ROWS_BLOCK), ROWS_BLOCK)
        query = packed[here, :] * jnp.asarray(HEAD_DIM**-0.5, BF16)
        total = jnp.zeros((ROWS_BLOCK, width), F32)
        for head in range(heads):
            mine = head_of == head
            scores = dot(jnp.where(mine, query, jnp.zeros_like(query)), kt_ref[...])
            weights = jnp.exp(scores - jnp.max(scores, axis=1, keepdims=True))
            norm = jnp.sum(weights, axis=1, keepdims=True)
            taken = dot(weights.astype(BF16), v_ref[...])
            total = jnp.where(mine, taken / norm, total)
        attended[here, :] = total.astype(BF16)
        return 0

    lax.fori_loop(0, (begins[sources] + ROWS_BLOCK - 1) // ROWS_BLOCK, block, 0)
    for source in range(sources):
        at = pl.multiple_of((begins[source] // 16) * 16, 16)
        put = one_hot(iota((rows, wide_span), 1) + at == pos_col[:, source : source + 1])
        out_ref[source] = dot(put, attended[pl.ds(at, wide_span), :]).astype(BF16)


def attend(wide_at, owner_slot, langs, queries, keys_t, values):
    sources, rows, width = queries.shape
    capacity = sources * rows + 2 * ROWS_BLOCK
    in_vmem = pl.BlockSpec(memory_space=pltpu.VMEM)
    in_smem = pl.BlockSpec(memory_space=pltpu.SMEM)
    return pl.pallas_call(
        attend_kernel,
        out_shape=jax.ShapeDtypeStruct(queries.shape, BF16),
        in_specs=[in_smem] * 2 + [in_vmem] * 4,
        out_specs=in_vmem,
        scratch_shapes=[pltpu.VMEM((capacity, width), BF16)] * 2,
        cost_estimate=pl.CostEstimate(flops=10**9, bytes_accessed=4 * 10**6, transcendentals=10**6),
        compiler_params=pltpu.CompilerParams(vmem_limit_bytes=32 * 1024 * 1024),
        name="attend",
    )(wide_at, owner_slot, langs, queries, keys_t, values)


def project_kernel(place, *refs):
    parts = (len(refs) - 3) // 2
    ctx_refs, proj_refs = refs[:parts], refs[parts : 2 * parts]
    send_ref, keep_ref, full = refs[2 * parts :]
    rows = send_ref.shape[1]
    acc = dot(ctx_refs[0][...], proj_refs[0][...])
    for part in range(1, parts):
        acc = acc + dot(ctx_refs[part][...], proj_refs[part][...])
    full[...] = acc
    core = place[0]
    for far in range(2):
        gone = pl.multiple_of((far * 2 + 1 - core) * rows, rows)
        kept = pl.multiple_of((far * 2 + core) * rows, rows)
        send_ref[far] = full[pl.ds(gone, rows), :].astype(BF16)
        keep_ref[far] = full[pl.ds(kept, rows), :]


def project(core, contexts, projs):
    rows, width = contexts[0].shape
    cols = projs[0].shape[1]
    in_vmem = pl.BlockSpec(memory_space=pltpu.VMEM)
    return pl.pallas_call(
        project_kernel,
        out_shape=(
            jax.ShapeDtypeStruct((2, rows // 4, cols), BF16),
            jax.ShapeDtypeStruct((2, rows // 4, cols), F32),
        ),
        in_specs=[pl.BlockSpec(memory_space=pltpu.SMEM)] + [in_vmem] * (len(contexts) + len(projs)),
        out_specs=(in_vmem, in_vmem),
        scratch_shapes=[pltpu.VMEM((rows, cols), F32)],
        cost_estimate=pl.CostEstimate(flops=10**9, bytes_accessed=4 * 10**6, transcendentals=0),
        compiler_params=pltpu.CompilerParams(vmem_limit_bytes=24 * 1024 * 1024),
        name="project",
    )(core, *contexts, *projs)


def dispatch_kernel(near_ref, got_ref, hidden_ref, slot_ref, resid_ref, *box_refs):
    for far in range(2):
        summed = near_ref[far].astype(F32) + got_ref[far].astype(F32)
        residual = (hidden_ref[far].astype(F32) + summed).astype(BF16)
        resid_ref[far] = residual
        for step, box_ref in enumerate(box_refs):
            index = step * 2 + far
            pick = one_hot(iota((CAP, residual.shape[0]), 0) == slot_ref[index : index + 1, :])
            box_ref[far] = dot(pick, residual).astype(BF16)


def dispatch(near, got, hidden, slots):
    _, rows, cols = near.shape
    steps = slots.shape[0] // 2
    in_vmem = pl.BlockSpec(memory_space=pltpu.VMEM)
    return pl.pallas_call(
        dispatch_kernel,
        out_shape=(jax.ShapeDtypeStruct(near.shape, BF16),)
        + (jax.ShapeDtypeStruct((2, CAP, cols), BF16),) * steps,
        in_specs=[in_vmem] * 4,
        out_specs=(in_vmem,) * (1 + steps),
        cost_estimate=pl.CostEstimate(flops=10**8, bytes_accessed=2 * 10**6, transcendentals=0),
        compiler_params=pltpu.CompilerParams(vmem_limit_bytes=16 * 1024 * 1024),
        name="dispatch",
    )(near, got, hidden, slots)


def hold_kernel(from_ref, _, held_ref, sems):
    pieces = sems.shape[0]
    rows = from_ref.shape[0] // pieces
    copies = [
        pltpu.make_async_copy(
            from_ref.at[pl.ds(piece * rows, rows)], held_ref.at[pl.ds(piece * rows, rows)], sems.at[piece]
        )
        for piece in range(pieces)
    ]
    for copy in copies:
        copy.start()
    for copy in copies:
        copy.wait()


def hold(weight, after, grant):
    in_vmem = pl.BlockSpec(memory_space=pltpu.VMEM)
    return pl.pallas_call(
        hold_kernel,
        out_shape=jax.ShapeDtypeStruct(weight.shape, weight.dtype),
        in_specs=[pl.BlockSpec(memory_space=pltpu.HBM), in_vmem],
        out_specs=in_vmem,
        scratch_shapes=[pltpu.SemaphoreType.DMA((8,))],
        cost_estimate=pl.CostEstimate(flops=4 * 10**9, bytes_accessed=10**7, transcendentals=0),
        compiler_params=pltpu.CompilerParams(vmem_limit_bytes=grant * 1024 * 1024),
        name="hold",
    )(weight, after)


IN_COLS = 640
OUT_COLS = 1024


def expert_kernel(place, *refs):
    parts = 4
    row_refs = refs[: 2 * parts]
    gain_ref, router_ref, choose_ref, w_in, w_out, send_ref, keep_ref = refs[2 * parts : 2 * parts + 7]
    rows_all, hidden = refs[2 * parts + 7 :]
    narrow_at, core = place[0], place[1]
    features, hidden_units = w_in.shape
    _, slots, quarter = row_refs[0].shape
    blocks = [lax.rem(narrow_at + parts - step, parts) for step in range(parts)]

    for which, side in ((0, core), (1, 1 - core)):
        for far in range(2):
            squares = jnp.zeros((slots, 1), F32)
            for part in range(parts):
                rows = row_refs[which * parts + part][far].astype(F32)
                squares = squares + jnp.sum(rows * rows, axis=1, keepdims=True)
            inverse = lax.rsqrt(squares / features + norm_eps)
            at = pl.multiple_of((far * 2 + side) * slots, 16)
            for part in range(parts):
                rows = row_refs[which * parts + part][far].astype(F32)
                normed = rows * inverse * gain_ref[blocks[part]]
                rows_all[part, pl.ds(at, slots), :] = normed.astype(BF16)
    logits = dot(rows_all[0], router_ref[blocks[0]])
    for part in range(1, parts):
        logits = logits + dot(rows_all[part], router_ref[blocks[part]])
    differ = jnp.sum(logits * choose_ref[...], axis=1, keepdims=True)
    gate = 1.0 / (1.0 + jnp.exp(-differ))
    for step in range(hidden_units // IN_COLS):
        cols = slice(step * IN_COLS, (step + 1) * IN_COLS)
        acc = None
        for part in range(parts):
            at = pl.multiple_of(blocks[part] * quarter, quarter)
            term = dot(rows_all[part], w_in[pl.ds(at, quarter), cols])
            acc = term if acc is None else acc + term
        hidden[:, cols] = jax.nn.gelu(acc, approximate=True).astype(BF16)
    for kept in range(2):
        side = core if kept else 1 - core
        for far in range(2):
            for step in range(quarter // OUT_COLS):
                at = pl.multiple_of((far * 2 + side) * quarter + step * OUT_COLS, OUT_COLS)
                acc = dot(hidden[...], w_out[:, pl.ds(at, OUT_COLS)]) * gate
                cols = slice(step * OUT_COLS, (step + 1) * OUT_COLS)
                if kept:
                    keep_ref[far, :, cols] = acc
                else:
                    send_ref[far, :, cols] = acc.astype(BF16)


def expert(place, own, other, gain, router, choose, w_in, w_out):
    _, slots, quarter = own[0].shape
    parts = len(own)
    rows = 4 * slots
    features, units = w_in.shape
    in_vmem = pl.BlockSpec(memory_space=pltpu.VMEM)
    return pl.pallas_call(
        expert_kernel,
        out_shape=(
            jax.ShapeDtypeStruct((2, rows, quarter), BF16),
            jax.ShapeDtypeStruct((2, rows, quarter), F32),
        ),
        in_specs=[pl.BlockSpec(memory_space=pltpu.SMEM)]
        + [in_vmem] * (2 * parts + 5),
        out_specs=(in_vmem, in_vmem),
        scratch_shapes=[
            pltpu.VMEM((parts, rows, quarter), BF16),
            pltpu.VMEM((rows, units), BF16),
        ],
        cost_estimate=pl.CostEstimate(flops=4 * 10**9, bytes_accessed=24 * 10**6, transcendentals=10**5),
        compiler_params=pltpu.CompilerParams(vmem_limit_bytes=12 * 1024 * 1024),
        name="expert",
    )(place, *own, *other, gain, router, choose, w_in, w_out)


def share_kernel(place, keep_ref, got_ref, *box_refs):
    slots = box_refs[0].shape[1]
    for step, box_ref in enumerate(box_refs):
        block = lax.rem(place[0] + step, len(box_refs))
        at = pl.ds(pl.multiple_of(block * slots, 16), slots)
        for far in range(2):
            box_ref[far] = (keep_ref[far, at, :] + got_ref[far, at, :].astype(F32)).astype(BF16)


def share(place, keep, got, peers):
    _, rows, cols = keep.shape
    in_vmem = pl.BlockSpec(memory_space=pltpu.VMEM)
    return pl.pallas_call(
        share_kernel,
        out_shape=(jax.ShapeDtypeStruct((2, rows // peers, cols), BF16),) * peers,
        in_specs=[pl.BlockSpec(memory_space=pltpu.SMEM), in_vmem, in_vmem],
        out_specs=(in_vmem,) * peers,
        cost_estimate=pl.CostEstimate(flops=10**7, bytes_accessed=4 * 10**6, transcendentals=0),
        compiler_params=pltpu.CompilerParams(vmem_limit_bytes=16 * 1024 * 1024),
        name="share",
    )(place, keep, got)


def combine_kernel(place, slot_ref, resid_ref, *refs):
    box_refs, (send_ref, keep_ref, both) = refs[:-3], refs[-3:]
    tokens = slot_ref.shape[1]
    for far in range(2):
        acc = jnp.zeros(both.shape[1:], F32)
        for step, box_ref in enumerate(box_refs):
            pick = one_hot(iota((tokens, CAP), 1) == slot_ref[step])
            acc = acc + dot(pick, box_ref[far])
        both[far] = acc
    send_ref[...] = both[1 - place[0]].astype(BF16)
    keep_ref[...] = both[place[0]] + resid_ref[...].astype(F32)


def combine(place, slots, resid, boxes):
    in_vmem = pl.BlockSpec(memory_space=pltpu.VMEM)
    return pl.pallas_call(
        combine_kernel,
        out_shape=(
            jax.ShapeDtypeStruct(resid.shape, BF16),
            jax.ShapeDtypeStruct(resid.shape, F32),
        ),
        in_specs=[pl.BlockSpec(memory_space=pltpu.SMEM)] + [in_vmem] * (2 + len(boxes)),
        out_specs=(in_vmem, in_vmem),
        scratch_shapes=[pltpu.VMEM((2, *resid.shape), F32)],
        cost_estimate=pl.CostEstimate(flops=10**8, bytes_accessed=2 * 10**6, transcendentals=0),
        compiler_params=pltpu.CompilerParams(vmem_limit_bytes=16 * 1024 * 1024),
        name="combine",
    )(place, slots, resid, *boxes)


def ring(count, step):
    return [(i, (i + step) % count) for i in range(count)]


def pick_at(values, index, axis=0):
    return lax.dynamic_index_in_dim(values, index, axis, keepdims=False)


def to_all(value, axis):
    peers = lax.axis_size(axis)
    return lax.all_to_all(
        jnp.broadcast_to(value[None], (peers, *value.shape)), axis, 0, 0, tiled=True
    )


def shards(
    hidden_in,
    queries,
    lang_ids,
    owner_slot,
    enc_kv,
    attn_proj,
    norm_gain,
    router_proj,
    expert_ids,
    proj_in,
    proj_out,
):
    narrow_count = lax.axis_size("narrow")
    depth_count = lax.axis_size("depth")
    wide_count = lax.axis_size("wide")
    tok_rows, quarter = hidden_in.shape
    seg_rows, width = queries.shape
    experts = narrow_count
    peers = range(narrow_count)
    wide_at = lax.axis_index("wide")
    narrow_at = lax.axis_index("narrow")
    depth_at = lax.axis_index("depth")
    core, far = depth_at % 2, depth_at // 2
    core_perm = [(i, i ^ 1) for i in range(depth_count)]
    far_perm = [(i, i ^ 2) for i in range(depth_count)]

    def swap_perm(flip):
        return [
            (n * depth_count + d, d * narrow_count + (n ^ flip))
            for n in range(narrow_count)
            for d in range(depth_count)
        ]

    def around(values):
        return [values[0]] + [
            lax.ppermute(values[step], "narrow", ring(narrow_count, step)) for step in peers if step
        ]

    def to_core(value):
        return lax.ppermute(value, "depth", core_perm)

    def to_far(value):
        return lax.ppermute(value, "depth", far_perm)

    segment = to_all(queries, "wide")

    id_blocks = expert_ids.reshape(-1, tok_rows, 2)
    names = id_blocks[:, :, :, None] == jnp.arange(experts, dtype=jnp.int32)
    named = jnp.any(names, axis=2)
    ranks = jnp.where(named, jnp.cumsum(named.astype(jnp.int32), axis=1) - 1, -1)
    ranks = jnp.moveaxis(ranks, 2, 0)
    my_blocks = jnp.stack([core, 2 + core])
    around_to = (narrow_at + jnp.arange(narrow_count)) % narrow_count
    around_from = (narrow_at - jnp.arange(narrow_count)) % narrow_count
    send_slots = ranks[around_to][:, my_blocks].reshape(2 * narrow_count, tok_rows)
    get_slots = pick_at(ranks, narrow_at, 1)[around_from][:, :, None]
    my_ranks = pick_at(ranks, narrow_at)
    filled = my_ranks[:, None, :] == jnp.arange(CAP, dtype=jnp.int32)[None, :, None]
    here = jnp.arange(experts, dtype=jnp.int32) == narrow_at
    weigh = jnp.where(here[None, None, :], 1.0, -1.0) * named
    choose = jnp.sum(jnp.where(filled[:, :, :, None], weigh[:, None, :, :], 0.0), axis=2)
    choose = choose.reshape(-1, experts)
    choose = jnp.pad(jnp.concatenate([choose] * 3, axis=1), ((0, 0), (0, 128 - 3 * experts)))
    high = router_proj.astype(BF16)
    rest = router_proj - high.astype(F32)
    middle = rest.astype(BF16)
    low = (rest - middle.astype(F32)).astype(BF16)
    router = jnp.pad(
        jnp.concatenate([high, middle, low], axis=1), ((0, 0), (0, 128 - 3 * experts))
    )

    projs = around(
        [
            lax.dynamic_slice_in_dim(attn_proj, around_to[step] * quarter, quarter, 1)
            for step in peers
        ]
    )
    hidden_blocks = [
        lax.ppermute(hidden_in, ("narrow", "depth"), swap_perm(flip)) for flip in (0, 2)
    ]
    near_hidden = jnp.where(far == 0, hidden_blocks[0], hidden_blocks[1])
    far_hidden = jnp.where(far == 0, hidden_blocks[1], hidden_blocks[0])
    hidden_swapped = jnp.stack([near_hidden, far_hidden])
    router = router.reshape(narrow_count, quarter, 128)
    gain = norm_gain.reshape(narrow_count, 1, quarter)
    keys_t = enc_kv[0, 0].T
    values = enc_kv[0, 1]

    partial = attend(
        wide_at[None], owner_slot, lang_ids.reshape(wide_count, seg_rows), segment, keys_t, values
    )
    returned = lax.all_to_all(partial, "wide", split_axis=0, concat_axis=0, tiled=True)
    returned, projs, hidden_swapped, send_slots, get_slots, choose, router, gain = (
        lax.optimization_barrier(
            (returned, projs, hidden_swapped, send_slots, get_slots, choose, router, gain)
        )
    )
    context = jnp.sum(returned, axis=0, dtype=BF16)
    contexts = around([context] * narrow_count)

    send, keep = project(core[None], contexts, projs)
    near = (keep + to_core(send).astype(F32)).astype(BF16)
    w_in = hold(proj_in[0], send[0, :16, :128], 2)
    got, w_in = lax.optimization_barrier((to_far(near), w_in))
    residual, *boxes = dispatch(near, got, hidden_swapped, send_slots)
    own_rows = around(boxes)
    w_out = hold(proj_out[0], residual[0, :16, :128], 2)
    own_rows[1], w_out = lax.optimization_barrier((own_rows[1], w_out))
    other_rows = [to_core(part) for part in own_rows]
    own_resid = lax.ppermute(pick_at(residual, far), ("narrow", "depth"), swap_perm(0))

    out_send, out_keep = expert(
        jnp.stack([narrow_at, core]),
        own_rows,
        other_rows,
        gain,
        router,
        choose,
        w_in,
        w_out,
    )
    arrived = around(share(narrow_at[None], out_keep, to_core(out_send), narrow_count))
    far_send, own_sum = combine(far[None], get_slots, own_resid, arrived)
    return (own_sum + to_far(far_send).astype(F32)).astype(BF16)


def solution(mesh):
    return jax.shard_map(
        shards,
        mesh=mesh,
        in_specs=(
            P(("wide", "narrow"), "depth"),
            P("wide", ("narrow", "depth")),
            P(),
            P(),
            P("wide", None, None, ("narrow", "depth")),
            P(("narrow", "depth"), None),
            P(),
            P(),
            P("wide", None),
            P("narrow", None, "depth"),
            P("narrow", "depth", None),
        ),
        out_specs=P(("wide", "narrow"), "depth"),
        check_vma=False,
    )
```

time: 260 us -> 134 us (0.52)
  matrix products: 45.8 us -> 0 us
  loops' own time: 40.3 us -> 0 us
  waiting for transfers between devices: 85.2 us -> 45.8 us
  local copies, waits for them, and re-layouts: 41.3 us -> 19.5 us
  starting transfers between devices: 26.8 us -> 44.4 us
  Pallas kernels: 0 us -> 17.3 us
  other arithmetic: 11.9 us -> 3.84 us
  blocking collectives: 6.5 us -> 0 us
  between operations: 0.25 us -> 2.85 us
    all_to_all x6 -> x2, waiting for transfers between devices: 85.2 us -> 9.81 us  [the longest x1 9.8 us: shards(): lax.all_to_all(partial, 'wide', split_axis=0, concat_axis=0, tiled=True)]
    dot_general x27 -> x0, matrix products: 45.8 us -> none  [the longest x1 16.7 us: expert_ffn(): jnp.einsum('secf,efgq->gsecq', hidden_act, out_blocks, preferred_element_...]
    another operation x2 -> x0, loops' own time: 40.3 us -> none  [the longest x1 40.1 us: shards(): lax.map(pair_term, pair_ids)]
    ppermute x0 -> x23, waiting for transfers between devices: none -> 36 us  [the longest x12 23.8 us: around(): lax.ppermute(values[step], 'narrow', ring(narrow_count, step))]
    ppermute x0 -> x23, starting transfers between devices: none -> 28.3 us  [the longest x12 20.8 us: around(): lax.ppermute(values[step], 'narrow', ring(narrow_count, step))]
    another operation x1, local copies, waits for them, and re-layouts: 17.8 us -> 0.23 us
    pallas_call x0 -> x8, Pallas kernels: none -> 17.3 us  [the longest x1 7.24 us: expert(): pl.pallas_call(expert_kernel, out_shape=(jax.ShapeDtypeStruct((2, rows, q...]
    all_to_all x6 -> x2, starting transfers between devices: 26.8 us -> 16.1 us  [the longest x1 8.64 us: shards(): lax.all_to_all(partial, 'wide', split_axis=0, concat_axis=0, tiled=True)]
  transfers between devices with their start and end apart: 6 -> 25, of which waited for: 6 -> 16; matrix products, arithmetic and copies ran while one was open for 10% -> 13% of each run, Pallas kernels for 0% -> 5%
where the time goes in v1:
time: 134 us
  waiting for transfers between devices  45.8 us (34%)
  starting transfers between devices  44.4 us (33%)
  local copies, waits for them, and re-layouts  19.5 us (15%)
  Pallas kernels  17.3 us (13%)
  other arithmetic  3.84 us (3%)
  between operations  2.85 us (2%)
    ppermute x12, waiting for transfers between devices, around(): lax.ppermute(values[step], 'narrow', ring(narrow_count, step))  23.8 us
    ppermute x12, starting transfers between devices, around(): lax.ppermute(values[step], 'narrow', ring(narrow_count, step))  20.8 us
    all_to_all x1, waiting for transfers between devices, shards(): lax.all_to_all(partial, 'wide', split_axis=0, concat_axis=0, tiled=True)  9.8 us
    all_to_all x1, starting transfers between devices, shards(): lax.all_to_all(partial, 'wide', split_axis=0, concat_axis=0, tiled=True)  8.64 us
    all_to_all x1, starting transfers between devices, to_all(): lax.all_to_all(jnp.broadcast_to(value[None], (peers, *value.shape)), axis...  7.48 us
    ppermute x2, waiting for transfers between devices, to_far(): return lax.ppermute(value, 'depth', far_perm)  7.28 us
    pallas_call x1, Pallas kernels, expert(): pl.pallas_call(expert_kernel, out_shape=(jax.ShapeDtypeStruct((2, rows, q...  7.24 us
    unnamed x14, local copies, waits for them, and re-layouts  6.57 us
  transfers between devices with their start and end apart: 25, of which 16 were waited for; matrix products, arithmetic and copies ran while one was open for 13% of the time, Pallas kernels for 5%

profile of v1, /device:TPU:0, one launch (start us, length us, event | category | flops | bytes accessed | tf_op | source)
XLA Modules:
  0.0 133.6 jit_solution(17327804123945550577)
XLA Ops:
  3.2 1.9 %broadcast_in_dim.60 = bf16[8,256,256]{2,1,0:T(8,128)(2,1)} broadcast(bf16[256,256]{1,0:T(8,128)(2,1)} %param.12), dimensions={1,2} | broadcast | bytes 1179648 | tf_op jit(solution)/shard_map/broadcast_in_dim | solution.py:338
  5.1 7.5 %all-to-all-start = ((bf16[8,256,256]{2,1,0:T(8,128)(2,1)}), bf16[8,256,256]{2,1,0:T(8,128)(2,1)S(1)}, u32[]{:S(2)}, u32[]{:S(2)}) async-start(bf16[8,256,256]{2,1,0:T(8,128)(2,1)} %broadcast_in_dim.60), calls=%async_computation | async-start | bytes 2097152 | tf_op jit(solution)/shard_map/all_to_all | solution.py:337
  15.7 2.7 %constant_dynamic-slice_fusion = (bf16[256,1024]{1,0:T(8,128)(2,1)}, bf16[256,1024]{1,0:T(8,128)(2,1)}, bf16[256,1024]{1,0:T(8,128)(2,1)S(1)}, bf16[256,1024]{1,0:T(8,128)(2,1)}) fusion(bf16[256,4096]{1,0:T(8,128)(2,1)} %param.16, s32[]{:T(128)S(6)} %select_n.127, s32[]{:T(128)S(6)} %select_n.125, s32[]{:T(128)S(6)} %select_n.124, s32[]{:T(128)S(6)} %select_n.126), kind=kLoop, calls=%fused_computation.41 | loop fusion | bytes 4194320 | tf_op jit(solution)/shard_map/dynamic_slice | solution.py:416
  18.5 5.8 %collective-permute-start.2 = (bf16[256,1024]{1,0:T(8,128)(2,1)}, bf16[256,1024]{1,0:T(8,128)(2,1)S(1)}, u32[]{:S(2)}, u32[]{:S(2)}) collective-permute-start(bf16[256,1024]{1,0:T(8,128)(2,1)} %get-tuple-element.65), channel_id=1, source_target_pairs={{0,12},{4,0},{8,4},{12,8},{1,13},{5,1},{9,5},{13,9},{2,14},{6,2},{... | collective-permute-start | bytes 1572872 | tf_op jit(solution)/shard_map/ppermute | solution.py:378
  24.2 2.8 %collective-permute-start.1 = (bf16[256,1024]{1,0:T(8,128)(2,1)}, bf16[256,1024]{1,0:T(8,128)(2,1)}, u32[]{:S(2)}, u32[]{:S(2)}) collective-permute-start(bf16[256,1024]{1,0:T(8,128)(2,1)} %get-tuple-element.68), channel_id=1, source_target_pairs={{0,8},{4,12},{8,0},{12,4},{1,9},{5,13},{9,1},{13,5},{2,10},{6,14},... | collective-permute-start | bytes 1572872 | tf_op jit(solution)/shard_map/ppermute | solution.py:378
  29.0 1.9 %slice_bitcast_fusion = (bf16[768,256]{1,0:T(8,128)(2,1)S(1)}, bf16[1,1,768,256]{3,2,1,0:T(8,128)(2,1)}) fusion(bf16[1,2,768,256]{3,2,1,0:T(8,128)(2,1)} %param.15), kind=kLoop, calls=%fused_computation.5 | loop fusion | bytes 1572864 | tf_op jit(solution)/shard_map/squeeze | solution.py:429
  33.8 4.7 %attend.1 = bf16[8,256,256]{2,1,0:T(8,128)(2,1)} custom-call(s32[1]{0:T(128)} %bitcast.1.place, s32[8]{0:T(128)S(1)} %copy-done.2, s32[8,256]{1,0:T(8,128)S(1)} %reshape.224.lang_ref, bf16[8,256,256]{2,1,0:T(8,128)(2,1)S(1)} %all-to-all-done.q_ref, bf16[256,768]{1,0:T(8,128)(2,1)S(1)} %bitcast.52, bf16[768,256]{1,0:T(8,128)(2,1)S(1)} %get-tuple-element.69.v_ref), custom_call_target="tpu_custom_call" | custom-call | flops 1000000000 | bytes 4000000 | tf_op jit(solution)/shard_map/attend/pallas_call | solution.py:93
  38.5 8.6 %all-to-all-start.1 = ((bf16[8,256,256]{2,1,0:T(8,128)(2,1)}), bf16[8,256,256]{2,1,0:T(8,128)(2,1)}, u32[]{:S(2)}, u32[]{:S(2)}) async-start(bf16[8,256,256]{2,1,0:T(8,128)(2,1)} %attend.1), calls=%async_computation.1 | async-start | bytes 2097152 | tf_op jit(solution)/shard_map/all_to_all | solution.py:434
  52.2 9.8 %all-to-all-done.1 = bf16[8,256,256]{2,1,0:T(8,128)(2,1)} async-done(((bf16[8,256,256]{2,1,0:T(8,128)(2,1)}), bf16[8,256,256]{2,1,0:T(8,128)(2,1)}, u32[]{:S(2)}, u32[]{:S(2)}) %all-to-all-start.1) | async-done | bytes 1048608 | tf_op jit(solution)/shard_map/all_to_all | solution.py:434
  65.2 2.6 %collective-permute-start.6 = (bf16[256,256]{1,0:T(8,128)(2,1)S(1)}, bf16[256,256]{1,0:T(8,128)(2,1)S(1)}, u32[]{:S(2)}, u32[]{:S(2)}) collective-permute-start(bf16[256,256]{1,0:T(8,128)(2,1)S(1)} %reduce_sum.19.refs_0_), channel_id=1, source_target_pairs={{0,8},{4,12},{8,0},{12,4},{1,9},{5,13},{9,1},{13,5},{2,10},{6,14},... | collective-permute-start | bytes 393224 | tf_op jit(solution)/shard_map/ppermute | solution.py:378
  68.7 3.0 %collective-permute-done.6.refs_2_ = bf16[256,256]{1,0:T(8,128)(2,1)S(1)} collective-permute-done((bf16[256,256]{1,0:T(8,128)(2,1)S(1)}, bf16[256,256]{1,0:T(8,128)(2,1)S(1)}, u32[]{:S(2)}, u32[]{:S(2)}) %collective-permute-start.6) | collective-permute-done | bytes 131104 | tf_op jit(solution)/shard_map/ppermute | solution.py:378
  71.7 2.3 %collective-permute-done.5.refs_1_ = bf16[256,256]{1,0:T(8,128)(2,1)S(1)} collective-permute-done((bf16[256,256]{1,0:T(8,128)(2,1)S(1)}, bf16[256,256]{1,0:T(8,128)(2,1)S(1)}, u32[]{:S(2)}, u32[]{:S(2)}) %collective-permute-start.5) | collective-permute-done | bytes 131104 | tf_op jit(solution)/shard_map/ppermute | solution.py:378
  74.0 2.1 %project.1 = (bf16[2,64,1024]{2,1,0:T(8,128)(2,1)S(1)}, f32[2,64,1024]{2,1,0:T(8,128)S(1)}) custom-call(s32[1]{0:T(128)} %bitcast.24.place, bf16[256,256]{1,0:T(8,128)(2,1)S(1)} %reduce_sum.19.refs_0_, bf16[256,256]{1,0:T(8,128)(2,1)S(1)} %collective-permute-done.5.refs_1_, bf16[256,256]{1,0:T(8,128)(2,1)S(1)} %collective-permute-done.6.refs_2_, ...), custom_call_target="tpu_custom_call" | custom-call | flops 1000000000 | bytes 4000000 | tf_op jit(solution)/shard_map/project/pallas_call | solution.py:126
  77.9 4.0 %copy-done = bf16[1,4096,1280]{2,1,0:T(8,128)(2,1)S(1)} copy-done((bf16[1,4096,1280]{2,1,0:T(8,128)(2,1)S(1)}, bf16[1,4096,1280]{2,1,0:T(8,128)(2,1)}, u32[]{:S(2)}) %copy-start) | copy-done | bytes 10485784
  82.7 3.6 %collective-permute-done.9.got_ref = bf16[2,64,1024]{2,1,0:T(8,128)(2,1)S(1)} collective-permute-done((bf16[2,64,1024]{2,1,0:T(8,128)(2,1)S(1)}, bf16[2,64,1024]{2,1,0:T(8,128)(2,1)S(1)}, u32[]{:S(2)}, u32[]{:S(2)}) %collective-permute-start.9) | collective-permute-done | bytes 262176 | tf_op jit(solution)/shard_map/ppermute | solution.py:385
  87.9 2.5 %collective-permute-start.13 = (bf16[2,48,1024]{2,1,0:T(8,128)(2,1)S(1)}, bf16[2,48,1024]{2,1,0:T(8,128)(2,1)S(1)}, u32[]{:S(2)}, u32[]{:S(2)}) collective-permute-start(bf16[2,48,1024]{2,1,0:T(8,128)(2,1)S(1)} %get-tuple-element.51), channel_id=1, source_target_pairs={{0,12},{4,0},{8,4},{12,8},{1,13},{5,1},{9,5},{13,9},{2,14},{6,2},{... | collective-permute-start | bytes 589832 | tf_op jit(solution)/shard_map/ppermute | solution.py:378
  91.3 7.0 %collective-permute-done.11.refs_1_ = bf16[2,48,1024]{2,1,0:T(8,128)(2,1)S(1)} collective-permute-done((bf16[2,48,1024]{2,1,0:T(8,128)(2,1)S(1)}, bf16[2,48,1024]{2,1,0:T(8,128)(2,1)S(1)}, u32[]{:S(2)}, u32[]{:S(2)}) %collective-permute-start.11) | collective-permute-done | bytes 196640 | tf_op jit(solution)/shard_map/ppermute | solution.py:378
  100.6 7.2 %expert.1 = (bf16[2,192,1024]{2,1,0:T(8,128)(2,1)}, f32[2,192,1024]{2,1,0:T(8,128)S(1)}) custom-call(s32[2]{0:T(128)S(1)} %pad_add_fusion.place, bf16[2,48,1024]{2,1,0:T(8,128)(2,1)S(1)} %get-tuple-element.47.refs_0_, bf16[2,48,1024]{2,1,0:T(8,128)(2,1)S(1)} %collective-permute-done.11.refs_1_, bf16[2,48,1024]{2,1,0:T(8,128)(2,1)S(1)} %collective-permute-done.12.refs_2_, ...), custom_call_target="tpu_custom_call" | custom-call | flops 4000000000 | bytes 24000000 | tf_op jit(solution)/shard_map/expert/pallas_call | solution.py:255
  108.0 2.3 %collective-permute-done.18.got_ref = bf16[2,192,1024]{2,1,0:T(8,128)(2,1)S(1)} collective-permute-done((bf16[2,192,1024]{2,1,0:T(8,128)(2,1)}, bf16[2,192,1024]{2,1,0:T(8,128)(2,1)S(1)}, u32[]{:S(2)}, u32[]{:S(2)}) %collective-permute-start.18) | collective-permute-done | bytes 786464 | tf_op jit(solution)/shard_map/ppermute | solution.py:382
  111.5 3.6 %collective-permute-start.20 = (bf16[2,48,1024]{2,1,0:T(8,128)(2,1)S(1)}, bf16[2,48,1024]{2,1,0:T(8,128)(2,1)S(1)}, u32[]{:S(2)}, u32[]{:S(2)}) collective-permute-start(bf16[2,48,1024]{2,1,0:T(8,128)(2,1)S(1)} %get-tuple-element.61), channel_id=1, source_target_pairs={{0,8},{4,12},{8,0},{12,4},{1,9},{5,13},{9,1},{13,5},{2,10},{6,14},... | collective-permute-start | bytes 589832 | tf_op jit(solution)/shard_map/ppermute | solution.py:378
  115.9 3.6 %collective-permute-done.19.refs_1_ = bf16[2,48,1024]{2,1,0:T(8,128)(2,1)S(1)} collective-permute-done((bf16[2,48,1024]{2,1,0:T(8,128)(2,1)}, bf16[2,48,1024]{2,1,0:T(8,128)(2,1)S(1)}, u32[]{:S(2)}, u32[]{:S(2)}) %collective-permute-start.19) | collective-permute-done | bytes 196640 | tf_op jit(solution)/shard_map/ppermute | solution.py:378
  119.5 5.0 %collective-permute-done.20.refs_2_ = bf16[2,48,1024]{2,1,0:T(8,128)(2,1)S(1)} collective-permute-done((bf16[2,48,1024]{2,1,0:T(8,128)(2,1)S(1)}, bf16[2,48,1024]{2,1,0:T(8,128)(2,1)S(1)}, u32[]{:S(2)}, u32[]{:S(2)}) %collective-permute-start.20) | collective-permute-done | bytes 196640 | tf_op jit(solution)/shard_map/ppermute | solution.py:378
  126.4 2.7 %collective-permute-start.22 = (bf16[64,1024]{1,0:T(8,128)(2,1)S(1)}, bf16[64,1024]{1,0:T(8,128)(2,1)S(1)}, u32[]{:S(2)}, u32[]{:S(2)}) collective-permute-start(bf16[64,1024]{1,0:T(8,128)(2,1)S(1)} %get-tuple-element.64), channel_id=1, source_target_pairs={{0,2},{1,3},{2,0},{3,1},{4,6},{5,7},{6,4},{7,5},{8,10},{9,11},{10,... | collective-permute-start | bytes 393224 | tf_op jit(solution)/shard_map/ppermute | solution.py:385
  129.2 3.7 %collective-permute-done.22 = bf16[64,1024]{1,0:T(8,128)(2,1)S(1)} collective-permute-done((bf16[64,1024]{1,0:T(8,128)(2,1)S(1)}, bf16[64,1024]{1,0:T(8,128)(2,1)S(1)}, u32[]{:S(2)}, u32[]{:S(2)}) %collective-permute-start.22) | collective-permute-done | bytes 131104 | tf_op jit(solution)/shard_map/ppermute | solution.py:385
  (99 shorter events, 29.7 us)
Async XLA Ops:
  0.0 52.1 %collective-permute-start.4 = (bf16[64,1024]{1,0:T(8,128)(2,1)}, bf16[64,1024]{1,0:T(8,128)(2,1)S(1)}, u32[]{:S(2)}, u32[]{:S(2)}) collective-permute-start(bf16[64,1024]{1,0:T(8,128)(2,1)} %param.11), channel_id=1, source_target_pairs={{0,2},{1,6},{2,10},{3,14},{4,3},{5,7},{6,11},{7,15},{8,0},{9,4},{1... | collective-permute-start | bytes 393224 | tf_op jit(solution)/shard_map/ppermute | solution.py:421
  1.6 50.5 %collective-permute-start.3 = (bf16[64,1024]{1,0:T(8,128)(2,1)}, bf16[64,1024]{1,0:T(8,128)(2,1)S(1)}, u32[]{:S(2)}, u32[]{:S(2)}) collective-permute-start(bf16[64,1024]{1,0:T(8,128)(2,1)} %param.11), channel_id=1, source_target_pairs={{0,0},{1,4},{2,8},{3,12},{4,1},{5,5},{6,9},{7,13},{8,2},{9,6},{10,... | collective-permute-start | bytes 393224 | tf_op jit(solution)/shard_map/ppermute | solution.py:421
  5.1 28.7 %all-to-all-start = ((bf16[8,256,256]{2,1,0:T(8,128)(2,1)}), bf16[8,256,256]{2,1,0:T(8,128)(2,1)S(1)}, u32[]{:S(2)}, u32[]{:S(2)}) async-start(bf16[8,256,256]{2,1,0:T(8,128)(2,1)} %broadcast_in_dim.60), calls=%async_computation | async-start | bytes 2097152 | tf_op jit(solution)/shard_map/all_to_all | solution.py:337
  18.5 33.7 %collective-permute-start.2 = (bf16[256,1024]{1,0:T(8,128)(2,1)}, bf16[256,1024]{1,0:T(8,128)(2,1)S(1)}, u32[]{:S(2)}, u32[]{:S(2)}) collective-permute-start(bf16[256,1024]{1,0:T(8,128)(2,1)} %get-tuple-element.65), channel_id=1, source_target_pairs={{0,12},{4,0},{8,4},{12,8},{1,13},{5,1},{9,5},{13,9},{2,14},{6,2},{... | collective-permute-start | bytes 1572872 | tf_op jit(solution)/shard_map/ppermute | solution.py:378
  24.2 27.9 %collective-permute-start = (bf16[256,1024]{1,0:T(8,128)(2,1)}, bf16[256,1024]{1,0:T(8,128)(2,1)}, u32[]{:S(2)}, u32[]{:S(2)}) collective-permute-start(bf16[256,1024]{1,0:T(8,128)(2,1)} %get-tuple-element.66), channel_id=1, source_target_pairs={{0,4},{4,8},{8,12},{12,0},{1,5},{5,9},{9,13},{13,1},{2,6},{6,10},{... | collective-permute-start | bytes 1572872 | tf_op jit(solution)/shard_map/ppermute | solution.py:378
  24.2 27.9 %collective-permute-start.1 = (bf16[256,1024]{1,0:T(8,128)(2,1)}, bf16[256,1024]{1,0:T(8,128)(2,1)}, u32[]{:S(2)}, u32[]{:S(2)}) collective-permute-start(bf16[256,1024]{1,0:T(8,128)(2,1)} %get-tuple-element.68), channel_id=1, source_target_pairs={{0,8},{4,12},{8,0},{12,4},{1,9},{5,13},{9,1},{13,5},{2,10},{6,14},... | collective-permute-start | bytes 1572872 | tf_op jit(solution)/shard_map/ppermute | solution.py:378
  38.5 23.5 %all-to-all-start.1 = ((bf16[8,256,256]{2,1,0:T(8,128)(2,1)}), bf16[8,256,256]{2,1,0:T(8,128)(2,1)}, u32[]{:S(2)}, u32[]{:S(2)}) async-start(bf16[8,256,256]{2,1,0:T(8,128)(2,1)} %attend.1), calls=%async_computation.1 | async-start | bytes 2097152 | tf_op jit(solution)/shard_map/all_to_all | solution.py:434
  63.4 5.4 %collective-permute-start.7 = (bf16[256,256]{1,0:T(8,128)(2,1)S(1)}, bf16[256,256]{1,0:T(8,128)(2,1)S(1)}, u32[]{:S(2)}, u32[]{:S(2)}) collective-permute-start(bf16[256,256]{1,0:T(8,128)(2,1)S(1)} %reduce_sum.19.refs_0_), channel_id=1, source_target_pairs={{0,12},{4,0},{8,4},{12,8},{1,13},{5,1},{9,5},{13,9},{2,14},{6,2},{... | collective-permute-start | bytes 393224 | tf_op jit(solution)/shard_map/ppermute | solution.py:378
  65.2 6.5 %collective-permute-start.6 = (bf16[256,256]{1,0:T(8,128)(2,1)S(1)}, bf16[256,256]{1,0:T(8,128)(2,1)S(1)}, u32[]{:S(2)}, u32[]{:S(2)}) collective-permute-start(bf16[256,256]{1,0:T(8,128)(2,1)S(1)} %reduce_sum.19.refs_0_), channel_id=1, source_target_pairs={{0,8},{4,12},{8,0},{12,4},{1,9},{5,13},{9,1},{13,5},{2,10},{6,14},... | collective-permute-start | bytes 393224 | tf_op jit(solution)/shard_map/ppermute | solution.py:378
  67.9 6.2 %collective-permute-start.5 = (bf16[256,256]{1,0:T(8,128)(2,1)S(1)}, bf16[256,256]{1,0:T(8,128)(2,1)S(1)}, u32[]{:S(2)}, u32[]{:S(2)}) collective-permute-start(bf16[256,256]{1,0:T(8,128)(2,1)S(1)} %reduce_sum.19.refs_0_), channel_id=1, source_target_pairs={{0,4},{4,8},{8,12},{12,0},{1,5},{5,9},{9,13},{13,1},{2,6},{6,10},{... | collective-permute-start | bytes 393224 | tf_op jit(solution)/shard_map/ppermute | solution.py:378
  76.2 1.6 %collective-permute-start.8 = (bf16[2,64,1024]{2,1,0:T(8,128)(2,1)S(1)}, bf16[2,64,1024]{2,1,0:T(8,128)(2,1)S(1)}, u32[]{:S(2)}, u32[]{:S(2)}) collective-permute-start(bf16[2,64,1024]{2,1,0:T(8,128)(2,1)S(1)} %get-tuple-element.42), channel_id=1, source_target_pairs={{0,1},{1,0},{2,3},{3,2},{4,5},{5,4},{6,7},{7,6},{8,9},{9,8},{10,11... | collective-permute-start | bytes 786440 | tf_op jit(solution)/shard_map/ppermute | solution.py:382
  77.8 8.4 %collective-permute-start.9 = (bf16[2,64,1024]{2,1,0:T(8,128)(2,1)S(1)}, bf16[2,64,1024]{2,1,0:T(8,128)(2,1)S(1)}, u32[]{:S(2)}, u32[]{:S(2)}) collective-permute-start(bf16[2,64,1024]{2,1,0:T(8,128)(2,1)S(1)} %add_convert_fusion.near_ref), channel_id=1, source_target_pairs={{0,2},{1,3},{2,0},{3,1},{4,6},{5,7},{6,4},{7,5},{8,10},{9,11},{10,... | collective-permute-start | bytes 786440 | tf_op jit(solution)/shard_map/ppermute | solution.py:385
  86.7 11.6 %collective-permute-start.11 = (bf16[2,48,1024]{2,1,0:T(8,128)(2,1)S(1)}, bf16[2,48,1024]{2,1,0:T(8,128)(2,1)S(1)}, u32[]{:S(2)}, u32[]{:S(2)}) collective-permute-start(bf16[2,48,1024]{2,1,0:T(8,128)(2,1)S(1)} %get-tuple-element.48), channel_id=1, source_target_pairs={{0,4},{4,8},{8,12},{12,0},{1,5},{5,9},{9,13},{13,1},{2,6},{6,10},{... | collective-permute-start | bytes 589832 | tf_op jit(solution)/shard_map/ppermute | solution.py:378
  87.0 11.3 %collective-permute-start.12 = (bf16[2,48,1024]{2,1,0:T(8,128)(2,1)S(1)}, bf16[2,48,1024]{2,1,0:T(8,128)(2,1)S(1)}, u32[]{:S(2)}, u32[]{:S(2)}) collective-permute-start(bf16[2,48,1024]{2,1,0:T(8,128)(2,1)S(1)} %get-tuple-element.50), channel_id=1, source_target_pairs={{0,8},{4,12},{8,0},{12,4},{1,9},{5,13},{9,1},{13,5},{2,10},{6,14},... | collective-permute-start | bytes 589832 | tf_op jit(solution)/shard_map/ppermute | solution.py:378
  87.9 11.0 %collective-permute-start.13 = (bf16[2,48,1024]{2,1,0:T(8,128)(2,1)S(1)}, bf16[2,48,1024]{2,1,0:T(8,128)(2,1)S(1)}, u32[]{:S(2)}, u32[]{:S(2)}) collective-permute-start(bf16[2,48,1024]{2,1,0:T(8,128)(2,1)S(1)} %get-tuple-element.51), channel_id=1, source_target_pairs={{0,12},{4,0},{8,4},{12,8},{1,13},{5,1},{9,5},{13,9},{2,14},{6,2},{... | collective-permute-start | bytes 589832 | tf_op jit(solution)/shard_map/ppermute | solution.py:378
  90.4 9.0 %collective-permute-start.14 = (bf16[2,48,1024]{2,1,0:T(8,128)(2,1)S(1)}, bf16[2,48,1024]{2,1,0:T(8,128)(2,1)S(1)}, u32[]{:S(2)}, u32[]{:S(2)}) collective-permute-start(bf16[2,48,1024]{2,1,0:T(8,128)(2,1)S(1)} %get-tuple-element.47.refs_0_), channel_id=1, source_target_pairs={{0,1},{1,0},{2,3},{3,2},{4,5},{5,4},{6,7},{7,6},{8,9},{9,8},{10,11... | collective-permute-start | bytes 589832 | tf_op jit(solution)/shard_map/ppermute | solution.py:382
  98.2 1.4 %collective-permute-start.16 = (bf16[2,48,1024]{2,1,0:T(8,128)(2,1)S(1)}, bf16[2,48,1024]{2,1,0:T(8,128)(2,1)S(1)}, u32[]{:S(2)}, u32[]{:S(2)}) collective-permute-start(bf16[2,48,1024]{2,1,0:T(8,128)(2,1)S(1)} %collective-permute-done.12.refs_2_), channel_id=1, source_target_pairs={{0,1},{1,0},{2,3},{3,2},{4,5},{5,4},{6,7},{7,6},{8,9},{9,8},{10,11... | collective-permute-start | bytes 589832 | tf_op jit(solution)/shard_map/ppermute | solution.py:382
  98.9 1.4 %collective-permute-start.17 = (bf16[2,48,1024]{2,1,0:T(8,128)(2,1)S(1)}, bf16[2,48,1024]{2,1,0:T(8,128)(2,1)S(1)}, u32[]{:S(2)}, u32[]{:S(2)}) collective-permute-start(bf16[2,48,1024]{2,1,0:T(8,128)(2,1)S(1)} %collective-permute-done.13.refs_3_), channel_id=1, source_target_pairs={{0,1},{1,0},{2,3},{3,2},{4,5},{5,4},{6,7},{7,6},{8,9},{9,8},{10,11... | collective-permute-start | bytes 589832 | tf_op jit(solution)/shard_map/ppermute | solution.py:382
  98.9 1.7 %collective-permute-start.15 = (bf16[2,48,1024]{2,1,0:T(8,128)(2,1)S(1)}, bf16[2,48,1024]{2,1,0:T(8,128)(2,1)S(1)}, u32[]{:S(2)}, u32[]{:S(2)}) collective-permute-start(bf16[2,48,1024]{2,1,0:T(8,128)(2,1)S(1)} %collective-permute-done.11.refs_1_), channel_id=1, source_target_pairs={{0,1},{1,0},{2,3},{3,2},{4,5},{5,4},{6,7},{7,6},{8,9},{9,8},{10,11... | collective-permute-start | bytes 589832 | tf_op jit(solution)/shard_map/ppermute | solution.py:382
  107.8 2.5 %collective-permute-start.18 = (bf16[2,192,1024]{2,1,0:T(8,128)(2,1)}, bf16[2,192,1024]{2,1,0:T(8,128)(2,1)S(1)}, u32[]{:S(2)}, u32[]{:S(2)}) collective-permute-start(bf16[2,192,1024]{2,1,0:T(8,128)(2,1)} %get-tuple-element.58), channel_id=1, source_target_pairs={{0,1},{1,0},{2,3},{3,2},{4,5},{5,4},{6,7},{7,6},{8,9},{9,8},{10,11... | collective-permute-start | bytes 2359304 | tf_op jit(solution)/shard_map/ppermute | solution.py:382
  111.1 8.4 %collective-permute-start.19 = (bf16[2,48,1024]{2,1,0:T(8,128)(2,1)}, bf16[2,48,1024]{2,1,0:T(8,128)(2,1)S(1)}, u32[]{:S(2)}, u32[]{:S(2)}) collective-permute-start(bf16[2,48,1024]{2,1,0:T(8,128)(2,1)} %get-tuple-element.60), channel_id=1, source_target_pairs={{0,4},{4,8},{8,12},{12,0},{1,5},{5,9},{9,13},{13,1},{2,6},{6,10},{... | collective-permute-start | bytes 589832 | tf_op jit(solution)/shard_map/ppermute | solution.py:378
  111.5 13.0 %collective-permute-start.20 = (bf16[2,48,1024]{2,1,0:T(8,128)(2,1)S(1)}, bf16[2,48,1024]{2,1,0:T(8,128)(2,1)S(1)}, u32[]{:S(2)}, u32[]{:S(2)}) collective-permute-start(bf16[2,48,1024]{2,1,0:T(8,128)(2,1)S(1)} %get-tuple-element.61), channel_id=1, source_target_pairs={{0,8},{4,12},{8,0},{12,4},{1,9},{5,13},{9,1},{13,5},{2,10},{6,14},... | collective-permute-start | bytes 589832 | tf_op jit(solution)/shard_map/ppermute | solution.py:378
  115.1 10.8 %collective-permute-start.21 = (bf16[2,48,1024]{2,1,0:T(8,128)(2,1)S(1)}, bf16[2,48,1024]{2,1,0:T(8,128)(2,1)S(1)}, u32[]{:S(2)}, u32[]{:S(2)}) collective-permute-start(bf16[2,48,1024]{2,1,0:T(8,128)(2,1)S(1)} %get-tuple-element.62), channel_id=1, source_target_pairs={{0,12},{4,0},{8,4},{12,8},{1,13},{5,1},{9,5},{13,9},{2,14},{6,2},{... | collective-permute-start | bytes 589832 | tf_op jit(solution)/shard_map/ppermute | solution.py:378
  126.4 6.5 %collective-permute-start.22 = (bf16[64,1024]{1,0:T(8,128)(2,1)S(1)}, bf16[64,1024]{1,0:T(8,128)(2,1)S(1)}, u32[]{:S(2)}, u32[]{:S(2)}) collective-permute-start(bf16[64,1024]{1,0:T(8,128)(2,1)S(1)} %get-tuple-element.64), channel_id=1, source_target_pairs={{0,2},{1,3},{2,0},{3,1},{4,6},{5,7},{6,4},{7,5},{8,10},{9,11},{10,... | collective-permute-start | bytes 393224 | tf_op jit(solution)/shard_map/ppermute | solution.py:385
  (7 other events, 82.1 us)

commit v2 on v1

--- a/solution.py
+++ b/solution.py
@@ -1,11 +1,11 @@
-import functools
-
 import jax
 import jax.numpy as jnp
 from jax import lax
 from jax.experimental import pallas as pl
+from jax.experimental.layout import Layout, with_layout_constraint
 from jax.experimental.pallas import tpu as pltpu
 from jax.sharding import PartitionSpec as P
+
 
 HEAD_DIM = 64
 CAP = 48
@@ -13,7 +13,6 @@
 F32 = jnp.float32
 BF16 = jnp.bfloat16
 ROWS_BLOCK = 256
-LIMIT = 60 * 1024 * 1024
 
 
 def dot(a, b):
@@ -28,20 +27,31 @@
     return jnp.where(flags, 1.0, 0.0).astype(BF16)
 
 
-def vmem(*shape_dtype):
-    return pltpu.VMEM(*shape_dtype)
-
-
-def attend_kernel(place, slot_of, lang_ref, q_ref, kt_ref, v_ref, out_ref, packed, attended):
+def attend_block(query, kv_ref):
+    width = query.shape[1]
+    head_of = iota((1, width), 1) // HEAD_DIM
+    total = jnp.zeros(query.shape, F32)
+    for head in range(width // HEAD_DIM):
+        mine = head_of == head
+        scores = lax.dot_general(
+            jnp.where(mine, query, jnp.zeros_like(query)),
+            kv_ref[0],
+            (((1,), (1,)), ((), ())),
+            preferred_element_type=F32,
+        )
+        weights = jnp.exp(scores - jnp.max(scores, axis=1, keepdims=True))
+        norm = jnp.sum(weights, axis=1, keepdims=True)
+        taken = dot(weights.astype(BF16), kv_ref[1])
+        total = jnp.where(mine, taken / norm, total)
+    return total
+
+
+def attend_kernel(place, holder_ref, q_ref, kv_from, out_ref, kv_ref, attended, kv_sem):
     sources, rows, width = q_ref.shape
-    heads = width // HEAD_DIM
-    span = rows + 16
     wide_span = rows + 128
-    langs = lang_ref[...]
-    holder = jnp.zeros_like(langs)
-    for lang in range(slot_of.shape[0]):
-        holder = jnp.where(langs == lang, slot_of[lang], holder)
-    mine = holder == place[0]
+    kv_copy = pltpu.make_async_copy(kv_from, kv_ref, kv_sem)
+    kv_copy.start()
+    mine = holder_ref[...] == place[0]
     upto = one_hot(iota((rows, rows), 0) <= iota((rows, rows), 1))
     within = dot(one_hot(mine), upto)
     counts = within[:, rows - 1 :]
@@ -54,52 +64,194 @@
     pos = jnp.where(mine, within - 1.0 + before, -1.0)
     pos_row = pos.astype(jnp.int32)
     pos_col = pos.T.astype(jnp.int32)
-    packed[...] = jnp.zeros_like(packed)
-    attended[...] = jnp.zeros_like(attended)
-    for source in range(sources):
-        at = pl.multiple_of((begins[source] // 16) * 16, 16)
-        pick = one_hot(iota((span, rows), 0) + at == pos_row[source : source + 1, :])
-        moved = dot(pick, q_ref[source]).astype(BF16)
-        packed[pl.ds(at, span), :] += moved
-
-    head_of = iota((1, width), 1) // HEAD_DIM
+    blocks = (begins[sources] + ROWS_BLOCK - 1) // ROWS_BLOCK
+    rest = pl.ds(pl.multiple_of(blocks * ROWS_BLOCK, ROWS_BLOCK), wide_span)
+    attended[rest, :] = jnp.zeros((wide_span, width), BF16)
+    kv_copy.wait()
 
     def block(index, _):
-        here = pl.ds(pl.multiple_of(index * ROWS_BLOCK, ROWS_BLOCK), ROWS_BLOCK)
-        query = packed[here, :] * jnp.asarray(HEAD_DIM**-0.5, BF16)
-        total = jnp.zeros((ROWS_BLOCK, width), F32)
-        for head in range(heads):
-            mine = head_of == head
-            scores = dot(jnp.where(mine, query, jnp.zeros_like(query)), kt_ref[...])
-            weights = jnp.exp(scores - jnp.max(scores, axis=1, keepdims=True))
-            norm = jnp.sum(weights, axis=1, keepdims=True)
-            taken = dot(weights.astype(BF16), v_ref[...])
-            total = jnp.where(mine, taken / norm, total)
-        attended[here, :] = total.astype(BF16)
+        begin = pl.multiple_of(index * ROWS_BLOCK, ROWS_BLOCK)
+        query = jnp.zeros((ROWS_BLOCK, width), F32)
+        for source in range(sources):
+            pick = one_hot(iota((ROWS_BLOCK, rows), 0) + begin == pos_row[source : source + 1, :])
+            query = query + dot(pick, q_ref[source])
+        total = attend_block((query * HEAD_DIM**-0.5).astype(BF16), kv_ref)
+        attended[pl.ds(begin, ROWS_BLOCK), :] = total.astype(BF16)
         return 0
 
-    lax.fori_loop(0, (begins[sources] + ROWS_BLOCK - 1) // ROWS_BLOCK, block, 0)
+    lax.fori_loop(0, blocks, block, 0)
     for source in range(sources):
         at = pl.multiple_of((begins[source] // 16) * 16, 16)
         put = one_hot(iota((rows, wide_span), 1) + at == pos_col[:, source : source + 1])
         out_ref[source] = dot(put, attended[pl.ds(at, wide_span), :]).astype(BF16)
 
 
-def attend(wide_at, owner_slot, langs, queries, keys_t, values):
+def attend(wide_at, holder, queries, keys_values):
     sources, rows, width = queries.shape
-    capacity = sources * rows + 2 * ROWS_BLOCK
-    in_vmem = pl.BlockSpec(memory_space=pltpu.VMEM)
-    in_smem = pl.BlockSpec(memory_space=pltpu.SMEM)
+    capacity = sources * rows + rows + 128
+    in_vmem = pl.BlockSpec(memory_space=pltpu.VMEM)
     return pl.pallas_call(
         attend_kernel,
         out_shape=jax.ShapeDtypeStruct(queries.shape, BF16),
-        in_specs=[in_smem] * 2 + [in_vmem] * 4,
+        in_specs=[
+            pl.BlockSpec(memory_space=pltpu.SMEM),
+            in_vmem,
+            in_vmem,
+            pl.BlockSpec(memory_space=pl.ANY),
+        ],
         out_specs=in_vmem,
-        scratch_shapes=[pltpu.VMEM((capacity, width), BF16)] * 2,
+        scratch_shapes=[
+            pltpu.VMEM(keys_values.shape, BF16),
+            pltpu.VMEM((capacity, width), BF16),
+            pltpu.SemaphoreType.DMA,
+        ],
         cost_estimate=pl.CostEstimate(flops=10**9, bytes_accessed=4 * 10**6, transcendentals=10**6),
         compiler_params=pltpu.CompilerParams(vmem_limit_bytes=32 * 1024 * 1024),
         name="attend",
-    )(wide_at, owner_slot, langs, queries, keys_t, values)
+    )(wide_at, holder, queries, keys_values)
+
+
+ROUTE = 128
+
+
+def route_kernel(place, slot_of, lang_ref, q_ref, box_ref, slot_ref, count_ref, fits_ref):
+    sources, _, _ = box_ref.shape
+    rows = q_ref.shape[0]
+    langs = lang_ref[...]
+    holder = jnp.zeros_like(langs)
+    for lang in range(slot_of.shape[0]):
+        holder = jnp.where(langs == lang, slot_of[lang], holder)
+    pieces = langs.shape[0] // sources
+    per_line = [
+        jnp.sum(jnp.where(holder == which, 1.0, 0.0), axis=1, keepdims=True)
+        for which in range(sources)
+    ]
+    per_line = jnp.concatenate(per_line, axis=1)
+    join = one_hot(iota((sources, langs.shape[0]), 1) // pieces == iota((sources, langs.shape[0]), 0))
+    counts = dot(join, per_line.astype(BF16))
+    fits_ref[0] = (jnp.max(counts) <= ROUTE).astype(jnp.int32)
+    here = jnp.sum(jnp.where(iota((1, sources), 1) == place[0], counts, 0.0), axis=1, keepdims=True)
+    for source in range(sources):
+        count_ref[source] = jnp.sum(here[source : source + 1, :]).astype(jnp.int32)
+    line_of = iota(holder.shape, 0) - place[0] * pieces
+    own = jnp.concatenate(
+        [
+            jnp.sum(jnp.where(line_of == piece, holder, 0), axis=0, keepdims=True)
+            for piece in range(pieces)
+        ],
+        axis=1,
+    )
+    goes = own == iota((sources, rows), 0)
+    upto = one_hot(iota((rows, rows), 0) <= iota((rows, rows), 1))
+    slots = jnp.where(goes, dot(one_hot(goes), upto) - 1.0, -1.0).astype(jnp.int32)
+    slot_ref[...] = slots
+    for which in range(sources):
+        pick = one_hot(iota((ROUTE, rows), 0) == slots[which : which + 1, :])
+        box_ref[which] = dot(pick, q_ref[...]).astype(BF16)
+
+
+def route(wide_at, owner_slot, lang_ids, queries, sources):
+    rows, width = queries.shape
+    in_vmem = pl.BlockSpec(memory_space=pltpu.VMEM)
+    in_smem = pl.BlockSpec(memory_space=pltpu.SMEM)
+    return pl.pallas_call(
+        route_kernel,
+        out_shape=(
+            jax.ShapeDtypeStruct((sources, ROUTE, width), BF16),
+            jax.ShapeDtypeStruct((sources, rows), jnp.int32),
+            jax.ShapeDtypeStruct((sources,), jnp.int32),
+            jax.ShapeDtypeStruct((1,), jnp.int32),
+        ),
+        in_specs=[in_smem, in_smem, in_vmem, in_vmem],
+        out_specs=(in_vmem, in_vmem, in_smem, in_smem),
+        cost_estimate=pl.CostEstimate(flops=10**8, bytes_accessed=10**6, transcendentals=0),
+        compiler_params=pltpu.CompilerParams(vmem_limit_bytes=16 * 1024 * 1024),
+        name="route",
+    )(wide_at, owner_slot, lang_ids.reshape(-1, 128), queries)
+
+
+def routed_kernel(counts, q_ref, kv_from, out_ref, kv_ref, attended, kv_sem):
+    sources, span, width = q_ref.shape
+    kv_copy = pltpu.make_async_copy(kv_from, kv_ref, kv_sem)
+    kv_copy.start()
+    begins = [0]
+    for source in range(sources):
+        begins.append(begins[-1] + counts[source])
+    blocks = (begins[sources] + ROWS_BLOCK - 1) // ROWS_BLOCK
+    rest = pl.ds(pl.multiple_of(blocks * ROWS_BLOCK, ROWS_BLOCK), 2 * span)
+    attended[rest, :] = jnp.zeros((2 * span, width), BF16)
+    lane = iota((1, 2 * span), 1)
+    ranks = []
+    for source in range(0, sources, 2):
+        first = jnp.where(lane < counts[source], begins[source] + lane, -1)
+        second = jnp.where(lane - span < counts[source + 1], begins[source + 1] + lane - span, -1)
+        ranks.append(jnp.where(lane < span, first, second))
+    kv_copy.wait()
+
+    def block(index, _):
+        begin = pl.multiple_of(index * ROWS_BLOCK, ROWS_BLOCK)
+        query = jnp.zeros((ROWS_BLOCK, width), F32)
+        for pair, rank in enumerate(ranks):
+            pick = one_hot(iota((ROWS_BLOCK, 2 * span), 0) + begin == rank)
+            query = query + dot(pick, q_ref[2 * pair : 2 * pair + 2].reshape(2 * span, width))
+        total = attend_block((query * HEAD_DIM**-0.5).astype(BF16), kv_ref)
+        attended[pl.ds(begin, ROWS_BLOCK), :] = total.astype(BF16)
+        return 0
+
+    lax.fori_loop(0, blocks, block, 0)
+    for source in range(sources):
+        at = pl.multiple_of((begins[source] // 16) * 16, 16)
+        shift = begins[source] - at
+        put = one_hot(iota((span, 2 * span), 1) == iota((span, 2 * span), 0) + shift)
+        out_ref[source] = dot(put, attended[pl.ds(at, 2 * span), :]).astype(BF16)
+
+
+def attend_routed(counts, queries, keys_values):
+    sources, span, width = queries.shape
+    capacity = sources * span + 2 * ROWS_BLOCK
+    in_vmem = pl.BlockSpec(memory_space=pltpu.VMEM)
+    return pl.pallas_call(
+        routed_kernel,
+        out_shape=jax.ShapeDtypeStruct(queries.shape, BF16),
+        in_specs=[
+            pl.BlockSpec(memory_space=pltpu.SMEM),
+            in_vmem,
+            pl.BlockSpec(memory_space=pl.ANY),
+        ],
+        out_specs=in_vmem,
+        scratch_shapes=[
+            pltpu.VMEM(keys_values.shape, BF16),
+            pltpu.VMEM((capacity, width), BF16),
+            pltpu.SemaphoreType.DMA,
+        ],
+        cost_estimate=pl.CostEstimate(flops=10**9, bytes_accessed=4 * 10**6, transcendentals=10**6),
+        compiler_params=pltpu.CompilerParams(vmem_limit_bytes=32 * 1024 * 1024),
+        name="attend",
+    )(counts, queries, keys_values)
+
+
+def gather_kernel(slot_ref, box_ref, out_ref):
+    sources, span, width = box_ref.shape
+    rows = out_ref.shape[0]
+    slot_col = slot_ref[...].astype(F32).T.astype(jnp.int32)
+    total = jnp.zeros((rows, width), F32)
+    for which in range(sources):
+        pick = one_hot(iota((rows, span), 1) == slot_col[:, which : which + 1])
+        total = total + dot(pick, box_ref[which])
+    out_ref[...] = total.astype(BF16)
+
+
+def gather_rows(slots, boxes):
+    in_vmem = pl.BlockSpec(memory_space=pltpu.VMEM)
+    return pl.pallas_call(
+        gather_kernel,
+        out_shape=jax.ShapeDtypeStruct((slots.shape[1], boxes.shape[2]), BF16),
+        in_specs=[in_vmem, in_vmem],
+        out_specs=in_vmem,
+        cost_estimate=pl.CostEstimate(flops=10**8, bytes_accessed=10**6, transcendentals=0),
+        compiler_params=pltpu.CompilerParams(vmem_limit_bytes=16 * 1024 * 1024),
+        name="gather",
+    )(slots, boxes)
 
 
 def project_kernel(place, *refs):
@@ -120,7 +272,7 @@
 
 
 def project(core, contexts, projs):
-    rows, width = contexts[0].shape
+    rows, _ = contexts[0].shape
     cols = projs[0].shape[1]
     in_vmem = pl.BlockSpec(memory_space=pltpu.VMEM)
     return pl.pallas_call(
@@ -138,7 +290,8 @@
     )(core, *contexts, *projs)
 
 
-def dispatch_kernel(near_ref, got_ref, hidden_ref, slot_ref, resid_ref, *box_refs):
+def dispatch_kernel(place, near_ref, got_ref, hidden_ref, slot_ref, own_ref, *refs):
+    box_refs, resid_ref = refs[:-1], refs[-1]
     for far in range(2):
         summed = near_ref[far].astype(F32) + got_ref[far].astype(F32)
         residual = (hidden_ref[far].astype(F32) + summed).astype(BF16)
@@ -147,22 +300,24 @@
             index = step * 2 + far
             pick = one_hot(iota((CAP, residual.shape[0]), 0) == slot_ref[index : index + 1, :])
             box_ref[far] = dot(pick, residual).astype(BF16)
-
-
-def dispatch(near, got, hidden, slots):
-    _, rows, cols = near.shape
+    own_ref[...] = resid_ref[place[0]]
+
+
+def dispatch(far, near, got, hidden, slots):
+    _, _, cols = near.shape
     steps = slots.shape[0] // 2
     in_vmem = pl.BlockSpec(memory_space=pltpu.VMEM)
     return pl.pallas_call(
         dispatch_kernel,
-        out_shape=(jax.ShapeDtypeStruct(near.shape, BF16),)
+        out_shape=(jax.ShapeDtypeStruct(near.shape[1:], BF16),)
         + (jax.ShapeDtypeStruct((2, CAP, cols), BF16),) * steps,
-        in_specs=[in_vmem] * 4,
+        in_specs=[pl.BlockSpec(memory_space=pltpu.SMEM)] + [in_vmem] * 4,
         out_specs=(in_vmem,) * (1 + steps),
+        scratch_shapes=[pltpu.VMEM(near.shape, BF16)],
         cost_estimate=pl.CostEstimate(flops=10**8, bytes_accessed=2 * 10**6, transcendentals=0),
-        compiler_params=pltpu.CompilerParams(vmem_limit_bytes=16 * 1024 * 1024),
+        compiler_params=pltpu.CompilerParams(vmem_limit_bytes=8 * 1024 * 1024),
         name="dispatch",
-    )(near, got, hidden, slots)
+    )(far, near, got, hidden, slots)
 
 
 def hold_kernel(from_ref, _, held_ref, sems):
@@ -185,7 +340,7 @@
     return pl.pallas_call(
         hold_kernel,
         out_shape=jax.ShapeDtypeStruct(weight.shape, weight.dtype),
-        in_specs=[pl.BlockSpec(memory_space=pltpu.HBM), in_vmem],
+        in_specs=[pl.BlockSpec(memory_space=pltpu.HBM), pl.BlockSpec(memory_space=pl.ANY)],
         out_specs=in_vmem,
         scratch_shapes=[pltpu.SemaphoreType.DMA((8,))],
         cost_estimate=pl.CostEstimate(flops=4 * 10**9, bytes_accessed=10**7, transcendentals=0),
@@ -220,10 +375,21 @@
                 rows = row_refs[which * parts + part][far].astype(F32)
                 normed = rows * inverse * gain_ref[blocks[part]]
                 rows_all[part, pl.ds(at, slots), :] = normed.astype(BF16)
-    logits = dot(rows_all[0], router_ref[blocks[0]])
-    for part in range(1, parts):
-        logits = logits + dot(rows_all[part], router_ref[blocks[part]])
-    differ = jnp.sum(logits * choose_ref[...], axis=1, keepdims=True)
+    logits = jnp.zeros((4 * slots, 3 * router_ref.shape[0]), F32)
+    for part in range(parts):
+        exact = router_ref[:, pl.ds(pl.multiple_of(blocks[part] * quarter, quarter), quarter)]
+        high = exact.astype(BF16)
+        rest = exact - high.astype(F32)
+        middle = rest.astype(BF16)
+        low = (rest - middle.astype(F32)).astype(BF16)
+        pieces = jnp.concatenate([high.astype(F32), middle.astype(F32), low.astype(F32)], axis=0)
+        logits = logits + lax.dot_general(
+            rows_all[part],
+            pieces.astype(BF16),
+            (((1,), (1,)), ((), ())),
+            preferred_element_type=F32,
+        )
+    differ = jnp.sum(logits * choose_ref[:, : logits.shape[1]], axis=1, keepdims=True)
     gate = 1.0 / (1.0 + jnp.exp(-differ))
     for step in range(hidden_units // IN_COLS):
         cols = slice(step * IN_COLS, (step + 1) * IN_COLS)
@@ -250,7 +416,7 @@
     _, slots, quarter = own[0].shape
     parts = len(own)
     rows = 4 * slots
-    features, units = w_in.shape
+    _, units = w_in.shape
     in_vmem = pl.BlockSpec(memory_space=pltpu.VMEM)
     return pl.pallas_call(
         expert_kernel,
@@ -289,7 +455,7 @@
         in_specs=[pl.BlockSpec(memory_space=pltpu.SMEM), in_vmem, in_vmem],
         out_specs=(in_vmem,) * peers,
         cost_estimate=pl.CostEstimate(flops=10**7, bytes_accessed=4 * 10**6, transcendentals=0),
-        compiler_params=pltpu.CompilerParams(vmem_limit_bytes=16 * 1024 * 1024),
+        compiler_params=pltpu.CompilerParams(vmem_limit_bytes=8 * 1024 * 1024),
         name="share",
     )(place, keep, got)
 
@@ -300,8 +466,10 @@
     for far in range(2):
         acc = jnp.zeros(both.shape[1:], F32)
         for step, box_ref in enumerate(box_refs):
-            pick = one_hot(iota((tokens, CAP), 1) == slot_ref[step])
-            acc = acc + dot(pick, box_ref[far])
+            pick = one_hot(iota((CAP, tokens), 0) == slot_ref[step : step + 1, :])
+            acc = acc + lax.dot_general(
+                pick, box_ref[far], (((0,), (0,)), ((), ())), preferred_element_type=F32
+            )
         both[far] = acc
     send_ref[...] = both[1 - place[0]].astype(BF16)
     keep_ref[...] = both[place[0]] + resid_ref[...].astype(F32)
@@ -319,7 +487,7 @@
         out_specs=(in_vmem, in_vmem),
         scratch_shapes=[pltpu.VMEM((2, *resid.shape), F32)],
         cost_estimate=pl.CostEstimate(flops=10**8, bytes_accessed=2 * 10**6, transcendentals=0),
-        compiler_params=pltpu.CompilerParams(vmem_limit_bytes=16 * 1024 * 1024),
+        compiler_params=pltpu.CompilerParams(vmem_limit_bytes=8 * 1024 * 1024),
         name="combine",
     )(place, slots, resid, *boxes)
 
@@ -332,14 +500,7 @@
     return lax.dynamic_index_in_dim(values, index, axis, keepdims=False)
 
 
-def to_all(value, axis):
-    peers = lax.axis_size(axis)
-    return lax.all_to_all(
-        jnp.broadcast_to(value[None], (peers, *value.shape)), axis, 0, 0, tiled=True
-    )
-
-
-def shards(
+def body(
     hidden_in,
     queries,
     lang_ids,
@@ -356,7 +517,7 @@
     depth_count = lax.axis_size("depth")
     wide_count = lax.axis_size("wide")
     tok_rows, quarter = hidden_in.shape
-    seg_rows, width = queries.shape
+    seg_rows, _ = queries.shape
     experts = narrow_count
     peers = range(narrow_count)
     wide_at = lax.axis_index("wide")
@@ -375,7 +536,9 @@
 
     def around(values):
         return [values[0]] + [
-            lax.ppermute(values[step], "narrow", ring(narrow_count, step)) for step in peers if step
+            lax.ppermute(values[step], "narrow", ring(narrow_count, step))
+            for step in peers
+            if step
         ]
 
     def to_core(value):
@@ -384,79 +547,94 @@
     def to_far(value):
         return lax.ppermute(value, "depth", far_perm)
 
-    segment = to_all(queries, "wide")
-
-    id_blocks = expert_ids.reshape(-1, tok_rows, 2)
-    names = id_blocks[:, :, :, None] == jnp.arange(experts, dtype=jnp.int32)
-    named = jnp.any(names, axis=2)
-    ranks = jnp.where(named, jnp.cumsum(named.astype(jnp.int32), axis=1) - 1, -1)
-    ranks = jnp.moveaxis(ranks, 2, 0)
-    my_blocks = jnp.stack([core, 2 + core])
     around_to = (narrow_at + jnp.arange(narrow_count)) % narrow_count
-    around_from = (narrow_at - jnp.arange(narrow_count)) % narrow_count
-    send_slots = ranks[around_to][:, my_blocks].reshape(2 * narrow_count, tok_rows)
-    get_slots = pick_at(ranks, narrow_at, 1)[around_from][:, :, None]
-    my_ranks = pick_at(ranks, narrow_at)
-    filled = my_ranks[:, None, :] == jnp.arange(CAP, dtype=jnp.int32)[None, :, None]
-    here = jnp.arange(experts, dtype=jnp.int32) == narrow_at
-    weigh = jnp.where(here[None, None, :], 1.0, -1.0) * named
-    choose = jnp.sum(jnp.where(filled[:, :, :, None], weigh[:, None, :, :], 0.0), axis=2)
-    choose = choose.reshape(-1, experts)
-    choose = jnp.pad(jnp.concatenate([choose] * 3, axis=1), ((0, 0), (0, 128 - 3 * experts)))
-    high = router_proj.astype(BF16)
-    rest = router_proj - high.astype(F32)
-    middle = rest.astype(BF16)
-    low = (rest - middle.astype(F32)).astype(BF16)
-    router = jnp.pad(
-        jnp.concatenate([high, middle, low], axis=1), ((0, 0), (0, 128 - 3 * experts))
-    )
-
-    projs = around(
-        [
-            lax.dynamic_slice_in_dim(attn_proj, around_to[step] * quarter, quarter, 1)
-            for step in peers
+
+    def prepared(hidden_in, expert_ids):
+        id_blocks = expert_ids.reshape(-1, tok_rows, 2)
+        names = id_blocks[:, :, :, None] == jnp.arange(experts, dtype=jnp.int32)
+        named = jnp.any(names, axis=2)
+        ranks = jnp.where(named, jnp.cumsum(named.astype(jnp.int32), axis=1) - 1, -1)
+        ranks = jnp.moveaxis(ranks, 2, 0)
+        my_blocks = jnp.stack([core, 2 + core])
+        around_from = (narrow_at - jnp.arange(narrow_count)) % narrow_count
+        send_slots = ranks[around_to][:, my_blocks].reshape(2 * narrow_count, tok_rows)
+        get_slots = pick_at(ranks, narrow_at, 1)[around_from]
+        my_ranks = pick_at(ranks, narrow_at)
+        filled = my_ranks[:, None, :] == jnp.arange(CAP, dtype=jnp.int32)[None, :, None]
+        here = jnp.arange(experts, dtype=jnp.int32) == narrow_at
+        weigh = jnp.where(here[None, None, :], 1.0, -1.0) * named
+        choose = jnp.sum(jnp.where(filled[:, :, :, None], weigh[:, None, :, :], 0.0), axis=2)
+        choose = choose.reshape(-1, experts)
+        choose = jnp.pad(jnp.concatenate([choose] * 3, axis=1), ((0, 0), (0, 128 - 3 * experts)))
+        hidden_blocks = [
+            lax.ppermute(hidden_in, ("narrow", "depth"), swap_perm(flip)) for flip in (0, 2)
         ]
-    )
-    hidden_blocks = [
-        lax.ppermute(hidden_in, ("narrow", "depth"), swap_perm(flip)) for flip in (0, 2)
-    ]
-    near_hidden = jnp.where(far == 0, hidden_blocks[0], hidden_blocks[1])
-    far_hidden = jnp.where(far == 0, hidden_blocks[1], hidden_blocks[0])
-    hidden_swapped = jnp.stack([near_hidden, far_hidden])
-    router = router.reshape(narrow_count, quarter, 128)
-    gain = norm_gain.reshape(narrow_count, 1, quarter)
-    keys_t = enc_kv[0, 0].T
-    values = enc_kv[0, 1]
-
-    partial = attend(
-        wide_at[None], owner_slot, lang_ids.reshape(wide_count, seg_rows), segment, keys_t, values
-    )
-    returned = lax.all_to_all(partial, "wide", split_axis=0, concat_axis=0, tiled=True)
-    returned, projs, hidden_swapped, send_slots, get_slots, choose, router, gain = (
-        lax.optimization_barrier(
-            (returned, projs, hidden_swapped, send_slots, get_slots, choose, router, gain)
-        )
-    )
-    context = jnp.sum(returned, axis=0, dtype=BF16)
+        near_hidden = jnp.where(far == 0, hidden_blocks[0], hidden_blocks[1])
+        far_hidden = jnp.where(far == 0, hidden_blocks[1], hidden_blocks[0])
+        hidden_swapped = jnp.stack([near_hidden, far_hidden])
+        return tuple(
+            with_layout_constraint(value, Layout(tuple(range(value.ndim))))
+            for value in (hidden_swapped, send_slots, get_slots, choose)
+        )
+
+    def spread():
+        projs = around(
+            [
+                lax.dynamic_slice_in_dim(attn_proj, around_to[step] * quarter, quarter, 1)
+                for step in peers
+            ],
+        )
+        return tuple(projs)
+
+    def exchanged(boxes, attend_to, gathered):
+        segment = lax.all_to_all(boxes, "wide", split_axis=0, concat_axis=0, tiled=True)
+        projs = spread()
+        partial, *late = lax.optimization_barrier(
+            (attend_to(segment), hidden_in, expert_ids)
+        )
+        returned = lax.all_to_all(partial, "wide", split_axis=0, concat_axis=0, tiled=True)
+        returned, projs, ready = lax.optimization_barrier((returned, projs, prepared(*late)))
+        return gathered(returned), projs, ready
+
+    def routed(boxes):
+        return exchanged(
+            boxes,
+            lambda segment: attend_routed(counts, segment, enc_kv[0]),
+            lambda returned: gather_rows(slots, returned),
+        )
+
+    def general(_):
+        langs = lang_ids.reshape(wide_count, seg_rows)
+        match = langs[:, :, None] == jnp.arange(owner_slot.shape[0], dtype=jnp.int32)
+        holder = jnp.sum(jnp.where(match, owner_slot, 0), axis=2)
+        return exchanged(
+            jnp.broadcast_to(queries[None], (wide_count, *queries.shape)),
+            lambda segment: attend(wide_at[None], holder, segment, enc_kv[0]),
+            lambda returned: jnp.sum(returned, axis=0, dtype=BF16),
+        )
+
+    boxes, slots, counts, fits = route(wide_at[None], owner_slot, lang_ids, queries, wide_count)
+    context, projs, ready = lax.cond(fits[0] == 1, routed, general, boxes)
+    hidden_swapped, send_slots, get_slots, choose = ready
     contexts = around([context] * narrow_count)
 
     send, keep = project(core[None], contexts, projs)
     near = (keep + to_core(send).astype(F32)).astype(BF16)
-    w_in = hold(proj_in[0], send[0, :16, :128], 2)
+    w_in = hold(proj_in[0], send, 2)
     got, w_in = lax.optimization_barrier((to_far(near), w_in))
-    residual, *boxes = dispatch(near, got, hidden_swapped, send_slots)
+    residual, *boxes = dispatch(far[None], near, got, hidden_swapped, send_slots)
     own_rows = around(boxes)
-    w_out = hold(proj_out[0], residual[0, :16, :128], 2)
-    own_rows[1], w_out = lax.optimization_barrier((own_rows[1], w_out))
+    w_out = hold(proj_out[0], residual, 2)
+    own_resid = lax.ppermute(residual, ("narrow", "depth"), swap_perm(0))
+    own_rows[1], w_out, own_resid = lax.optimization_barrier((own_rows[1], w_out, own_resid))
     other_rows = [to_core(part) for part in own_rows]
-    own_resid = lax.ppermute(pick_at(residual, far), ("narrow", "depth"), swap_perm(0))
 
     out_send, out_keep = expert(
         jnp.stack([narrow_at, core]),
         own_rows,
         other_rows,
-        gain,
-        router,
+        norm_gain.reshape(narrow_count, 1, quarter),
+        router_proj.T,
         choose,
         w_in,
         w_out,
@@ -468,7 +646,7 @@
 
 def solution(mesh):
     return jax.shard_map(
-        shards,
+        body,
         mesh=mesh,
         in_specs=(
             P(("wide", "narrow"), "depth"),

time: 134 us -> 124 us (0.925)
  local copies, waits for them, and re-layouts: 19.5 us -> 9.89 us
  loops' own time: 0 us -> 2.67 us
  other arithmetic: 3.84 us -> 1.47 us
  between operations: 2.85 us -> 0.82 us
  Pallas kernels: 17.3 us -> 19 us
    ppermute x3, waiting for transfers between devices: 0.01 us -> 6.43 us  [the longest x2 6.43 us: prepared(): lax.ppermute(hidden_in, ('narrow', 'depth'), swap_perm(flip))]
    all_to_all x2, waiting for transfers between devices: 9.81 us -> 5.66 us  [the longest x1 3.79 us: exchanged(): lax.all_to_all(partial, 'wide', split_axis=0, concat_axis=0, tiled=True)]
    pallas_call x1 -> x3, Pallas kernels: 4.68 us -> 7.47 us  [the longest x1 4.57 us: attend_routed(): pl.pallas_call(routed_kernel, out_shape=jax.ShapeDtypeStruct(queries.shap...]
    another operation x0 -> x1, loops' own time: none -> 2.67 us  [body(): context, projs, ready = lax.cond(fits[0] == 1, routed, general, boxes)]
    unnamed x14 -> x12, local copies, waits for them, and re-layouts: 6.57 us -> 4.15 us
    broadcast_in_dim x1 -> x0, local copies, waits for them, and re-layouts: 1.95 us -> none  [to_all(): jnp.broadcast_to(value[None], (peers, *value.shape))]
    squeeze x3 -> x0, local copies, waits for them, and re-layouts: 1.91 us -> none  [the longest x1 1.91 us: shards(): values = enc_kv[0, 1]]
    pad x2 -> x1, local copies, waits for them, and re-layouts: 1.44 us -> 0.01 us  [prepared(): jnp.pad(jnp.concatenate([choose] * 3, axis=1), ((0, 0), (0, 128 - 3 * exp...]
  transfers between devices with their start and end apart: 25 -> 25, of which waited for: 16 -> 17; matrix products, arithmetic and copies ran while one was open for 13% -> 5% of each run, Pallas kernels for 5% -> 5%
where the time goes in v2:
time: 124 us; the launch traced here: 123 us
  waiting for transfers between devices  45.9 us (37%)
  starting transfers between devices  43.2 us (35%)
  Pallas kernels  19 us (15%)
  local copies, waits for them, and re-layouts  9.89 us (8%)
  loops' own time  2.67 us (2%)
  other arithmetic  1.47 us (1%)
    ppermute x12, waiting for transfers between devices, around(): lax.ppermute(values[step], 'narrow', ring(narrow_count, step))  22.8 us
    ppermute x12, starting transfers between devices, around(): lax.ppermute(values[step], 'narrow', ring(narrow_count, step))  20.9 us
    all_to_all x1, starting transfers between devices, exchanged(): lax.all_to_all(partial, 'wide', split_axis=0, concat_axis=0, tiled=True)  7.96 us
    all_to_all x1, starting transfers between devices, exchanged(): lax.all_to_all(boxes, 'wide', split_axis=0, concat_axis=0, tiled=True)  7.91 us
    pallas_call x1, Pallas kernels, expert(): pl.pallas_call(expert_kernel, out_shape=(jax.ShapeDtypeStruct((2, rows, q...  6.82 us
    ppermute x2, waiting for transfers between devices, prepared(): lax.ppermute(hidden_in, ('narrow', 'depth'), swap_perm(flip))  6.43 us
    ppermute x2, waiting for transfers between devices, to_far(): return lax.ppermute(value, 'depth', far_perm)  6.26 us
    ppermute x6, waiting for transfers between devices, to_core(): return lax.ppermute(value, 'depth', core_perm)  4.72 us
  transfers between devices with their start and end apart: 25, of which 17 were waited for; matrix products, arithmetic and copies ran while one was open for 5% of the time, Pallas kernels for 5%

profile of v2, /device:TPU:0, one launch (start us, length us, event | category | flops | bytes accessed | tf_op | source)
XLA Modules:
  0.0 122.9 jit_solution(423407202006087318)
XLA Ops:
  0.0 2.2 %route.1 = (bf16[8,128,256]{2,1,0:T(8,128)(2,1)}, s32[8,256]{1,0:T(8,128)S(1)}, s32[8]{0:T(128)S(1)}, s32[1]{0:T(128)}) custom-call(s32[1]{0:T(128)} %bitcast.36.place, s32[8]{0:T(128)} %slot_of.1, s32[16,128]{1,0:T(8,128)} %bitcast.75, bf16[256,256]{1,0:T(8,128)(2,1)} %q_ref.1), custom_call_target="tpu_custom_call" | custom-call | flops 100000000 | bytes 1000000 | tf_op jit(solution)/shard_map/route/pallas_call | solution.py:157
  2.9 49.2 %conditional.1 = (bf16[256,256]{1,0:T(8,128)(2,1)S(1)}, bf16[256,1024]{1,0:T(8,128)(2,1)S(1)}, bf16[256,1024]{1,0:T(8,128)(2,1)}, bf16[256,1024]{1,0:T(8,128)(2,...) conditional(s32[]{:T(128)} %bitcast.38, (s32[]{:T(128)}, ...), branch_computations={%region_0.6_spmd, %region_6.10_spmd} | conditional | flops 1100451328 | bytes 25561204 | solution.py:617
  2.9 7.9 %all-to-all-start.2 = ((bf16[8,128,256]{2,1,0:T(8,128)(2,1)}), bf16[8,128,256]{2,1,0:T(8,128)(2,1)S(1)}, u32[]{:S(2)}, u32[]{:S(2)}) async-start(bf16[8,128,256]{2,1,0:T(8,128)(2,1)} %get-tuple-element.77), calls=%async_computation.2 | async-start | bytes 1048576 | tf_op jit(solution)/shard_map/cond/branch_1_fun/all_to_all | solution.py:590
  15.7 3.1 %collective-permute-start.7 = (bf16[256,1024]{1,0:T(8,128)(2,1)S(1)}, bf16[256,1024]{1,0:T(8,128)(2,1)}, u32[]{:S(2)}, u32[]{:S(2)}) collective-permute-start(bf16[256,1024]{1,0:T(8,128)(2,1)S(1)} %get-tuple-element.174), channel_id=1, source_target_pairs={{0,12},{4,0},{8,4},{12,8},{1,13},{5,1},{9,5},{13,9},{2,14},{6,2},{... | collective-permute-start | bytes 1572872 | tf_op jit(solution)/shard_map/cond/branch_1_fun/ppermute | solution.py:539
  22.4 4.6 %attend.3 = bf16[8,128,256]{2,1,0:T(8,128)(2,1)} custom-call(s32[8]{0:T(128)S(1)} %get-tuple-element.76.counts, bf16[8,128,256]{2,1,0:T(8,128)(2,1)S(1)} %all-to-all-done.2.q_ref, bf16[2,768,256]{2,1,0:T(8,128)(2,1)} %bitcast.77), custom_call_target="tpu_custom_call" | custom-call | flops 1000000000 | bytes 4000000 | tf_op jit(solution)/shard_map/cond/branch_1_fun/attend/pallas_call | solution.py:213
  31.0 8.0 %all-to-all-start.3 = ((bf16[8,128,256]{2,1,0:T(8,128)(2,1)}), bf16[8,128,256]{2,1,0:T(8,128)(2,1)S(1)}, u32[]{:S(2)}, u32[]{:S(2)}) async-start(bf16[8,128,256]{2,1,0:T(8,128)(2,1)} %attend.3), calls=%async_computation.3 | async-start | bytes 1048576 | tf_op jit(solution)/shard_map/cond/branch_1_fun/all_to_all | solution.py:595
  41.1 6.4 %collective-permute-done.9 = bf16[64,1024]{1,0:T(8,128)(2,1)S(1)} collective-permute-done((bf16[64,1024]{1,0:T(8,128)(2,1)}, bf16[64,1024]{1,0:T(8,128)(2,1)S(1)}, u32[]{:S(2)}, u32[]{:S(2)}) %collective-permute-start.9) | collective-permute-done | bytes 131104 | tf_op jit(solution)/shard_map/cond/branch_1_fun/ppermute | solution.py:570
  47.6 3.8 %all-to-all-done.3.box_ref = bf16[8,128,256]{2,1,0:T(8,128)(2,1)S(1)} async-done(((bf16[8,128,256]{2,1,0:T(8,128)(2,1)}), bf16[8,128,256]{2,1,0:T(8,128)(2,1)S(1)}, u32[]{:S(2)}, u32[]{:S(2)}) %all-to-all-start.3) | async-done | bytes 524320 | tf_op jit(solution)/shard_map/cond/branch_1_fun/all_to_all | solution.py:595
  52.1 3.0 %collective-permute-start.12 = (bf16[256,256]{1,0:T(8,128)(2,1)S(1)}, bf16[256,256]{1,0:T(8,128)(2,1)S(1)}, u32[]{:S(2)}, u32[]{:S(2)}) collective-permute-start(bf16[256,256]{1,0:T(8,128)(2,1)S(1)} %get-tuple-element.136.refs_0_), channel_id=1, source_target_pairs={{0,12},{4,0},{8,4},{12,8},{1,13},{5,1},{9,5},{13,9},{2,14},{6,2},{... | collective-permute-start | bytes 393224 | tf_op jit(solution)/shard_map/ppermute | solution.py:539
  57.0 3.5 %collective-permute-done.12.refs_3_ = bf16[256,256]{1,0:T(8,128)(2,1)S(1)} collective-permute-done((bf16[256,256]{1,0:T(8,128)(2,1)S(1)}, bf16[256,256]{1,0:T(8,128)(2,1)S(1)}, u32[]{:S(2)}, u32[]{:S(2)}) %collective-permute-start.12) | collective-permute-done | bytes 131104 | tf_op jit(solution)/shard_map/ppermute | solution.py:539
  67.1 4.1 %copy-done = bf16[1,4096,1280]{2,1,0:T(8,128)(2,1)S(1)} copy-done((bf16[1,4096,1280]{2,1,0:T(8,128)(2,1)S(1)}, bf16[1,4096,1280]{2,1,0:T(8,128)(2,1)}, u32[]{:S(2)}) %copy-start) | copy-done | bytes 10485784
  72.0 3.3 %collective-permute-done.14.got_ref = bf16[2,64,1024]{2,1,0:T(8,128)(2,1)S(1)} collective-permute-done((bf16[2,64,1024]{2,1,0:T(8,128)(2,1)S(1)}, bf16[2,64,1024]{2,1,0:T(8,128)(2,1)S(1)}, u32[]{:S(2)}, u32[]{:S(2)}) %collective-permute-start.14) | collective-permute-done | bytes 262176 | tf_op jit(solution)/shard_map/ppermute | solution.py:548
  76.4 2.2 %collective-permute-start.15 = (bf16[2,48,1024]{2,1,0:T(8,128)(2,1)S(1)}, bf16[2,48,1024]{2,1,0:T(8,128)(2,1)S(1)}, u32[]{:S(2)}, u32[]{:S(2)}) collective-permute-start(bf16[2,48,1024]{2,1,0:T(8,128)(2,1)S(1)} %get-tuple-element.146), channel_id=1, source_target_pairs={{0,4},{4,8},{8,12},{12,0},{1,5},{5,9},{9,13},{13,1},{2,6},{6,10},{... | collective-permute-start | bytes 589832 | tf_op jit(solution)/shard_map/ppermute | solution.py:539
  78.6 2.6 %collective-permute-start.17 = (bf16[2,48,1024]{2,1,0:T(8,128)(2,1)S(1)}, bf16[2,48,1024]{2,1,0:T(8,128)(2,1)S(1)}, u32[]{:S(2)}, u32[]{:S(2)}) collective-permute-start(bf16[2,48,1024]{2,1,0:T(8,128)(2,1)S(1)} %get-tuple-element.151), channel_id=1, source_target_pairs={{0,8},{4,12},{8,0},{12,4},{1,9},{5,13},{9,1},{13,5},{2,10},{6,14},... | collective-permute-start | bytes 589832 | tf_op jit(solution)/shard_map/ppermute | solution.py:539
  81.2 2.4 %collective-permute-start.18 = (bf16[2,48,1024]{2,1,0:T(8,128)(2,1)S(1)}, bf16[2,48,1024]{2,1,0:T(8,128)(2,1)S(1)}, u32[]{:S(2)}, u32[]{:S(2)}) collective-permute-start(bf16[2,48,1024]{2,1,0:T(8,128)(2,1)S(1)} %get-tuple-element.152), channel_id=1, source_target_pairs={{0,12},{4,0},{8,4},{12,8},{1,13},{5,1},{9,5},{13,9},{2,14},{6,2},{... | collective-permute-start | bytes 589832 | tf_op jit(solution)/shard_map/ppermute | solution.py:539
  84.4 2.3 %collective-permute-done.15.refs_1_ = bf16[2,48,1024]{2,1,0:T(8,128)(2,1)S(1)} collective-permute-done((bf16[2,48,1024]{2,1,0:T(8,128)(2,1)S(1)}, bf16[2,48,1024]{2,1,0:T(8,128)(2,1)S(1)}, u32[]{:S(2)}, u32[]{:S(2)}) %collective-permute-start.15) | collective-permute-done | bytes 196640 | tf_op jit(solution)/shard_map/ppermute | solution.py:539
  86.8 3.0 %collective-permute-done.17.refs_2_ = bf16[2,48,1024]{2,1,0:T(8,128)(2,1)S(1)} collective-permute-done((bf16[2,48,1024]{2,1,0:T(8,128)(2,1)S(1)}, bf16[2,48,1024]{2,1,0:T(8,128)(2,1)S(1)}, u32[]{:S(2)}, u32[]{:S(2)}) %collective-permute-start.17) | collective-permute-done | bytes 196640 | tf_op jit(solution)/shard_map/ppermute | solution.py:539
  89.7 2.2 %collective-permute-done.18.refs_3_ = bf16[2,48,1024]{2,1,0:T(8,128)(2,1)S(1)} collective-permute-done((bf16[2,48,1024]{2,1,0:T(8,128)(2,1)S(1)}, bf16[2,48,1024]{2,1,0:T(8,128)(2,1)S(1)}, u32[]{:S(2)}, u32[]{:S(2)}) %collective-permute-start.18) | collective-permute-done | bytes 196640 | tf_op jit(solution)/shard_map/ppermute | solution.py:539
  93.6 6.8 %expert.1 = (bf16[2,192,1024]{2,1,0:T(8,128)(2,1)S(1)}, f32[2,192,1024]{2,1,0:T(8,128)S(1)}) custom-call(s32[2]{0:T(128)S(1)} %pad_add_fusion.place, bf16[2,48,1024]{2,1,0:T(8,128)(2,1)S(1)} %get-tuple-element.149.refs_0_, bf16[2,48,1024]{2,1,0:T(8,128)(2,1)S(1)} %collective-permute-done.15.refs_1_, ...), custom_call_target="tpu_custom_call" | custom-call | flops 4000000000 | bytes 24000000 | tf_op jit(solution)/shard_map/expert/pallas_call | solution.py:421
  103.1 4.0 %collective-permute-start.25 = (bf16[2,48,1024]{2,1,0:T(8,128)(2,1)S(1)}, bf16[2,48,1024]{2,1,0:T(8,128)(2,1)S(1)}, u32[]{:S(2)}, u32[]{:S(2)}) collective-permute-start(bf16[2,48,1024]{2,1,0:T(8,128)(2,1)S(1)} %get-tuple-element.160), channel_id=1, source_target_pairs={{0,8},{4,12},{8,0},{12,4},{1,9},{5,13},{9,1},{13,5},{2,10},{6,14},... | collective-permute-start | bytes 589832 | tf_op jit(solution)/shard_map/ppermute | solution.py:539
  107.2 4.1 %collective-permute-done.24.refs_1_ = bf16[2,48,1024]{2,1,0:T(8,128)(2,1)S(1)} collective-permute-done((bf16[2,48,1024]{2,1,0:T(8,128)(2,1)S(1)}, bf16[2,48,1024]{2,1,0:T(8,128)(2,1)S(1)}, u32[]{:S(2)}, u32[]{:S(2)}) %collective-permute-start.24) | collective-permute-done | bytes 196640 | tf_op jit(solution)/shard_map/ppermute | solution.py:539
  111.3 5.1 %collective-permute-done.25.refs_2_ = bf16[2,48,1024]{2,1,0:T(8,128)(2,1)S(1)} collective-permute-done((bf16[2,48,1024]{2,1,0:T(8,128)(2,1)S(1)}, bf16[2,48,1024]{2,1,0:T(8,128)(2,1)S(1)}, u32[]{:S(2)}, u32[]{:S(2)}) %collective-permute-start.25) | collective-permute-done | bytes 196640 | tf_op jit(solution)/shard_map/ppermute | solution.py:539
  116.9 2.4 %collective-permute-start.27 = (bf16[64,1024]{1,0:T(8,128)(2,1)S(1)}, bf16[64,1024]{1,0:T(8,128)(2,1)S(1)}, u32[]{:S(2)}, u32[]{:S(2)}) collective-permute-start(bf16[64,1024]{1,0:T(8,128)(2,1)S(1)} %get-tuple-element.163), channel_id=1, source_target_pairs={{0,2},{1,3},{2,0},{3,1},{4,6},{5,7},{6,4},{7,5},{8,10},{9,11},{10,... | collective-permute-start | bytes 393224 | tf_op jit(solution)/shard_map/ppermute | solution.py:548
  119.3 2.9 %collective-permute-done.27 = bf16[64,1024]{1,0:T(8,128)(2,1)S(1)} collective-permute-done((bf16[64,1024]{1,0:T(8,128)(2,1)S(1)}, bf16[64,1024]{1,0:T(8,128)(2,1)S(1)}, u32[]{:S(2)}, u32[]{:S(2)}) %collective-permute-start.27) | collective-permute-done | bytes 131104 | tf_op jit(solution)/shard_map/ppermute | solution.py:548
  (90 shorter events, 29.5 us)
Async XLA Ops:
  2.9 19.5 %all-to-all-start.2 = ((bf16[8,128,256]{2,1,0:T(8,128)(2,1)}), bf16[8,128,256]{2,1,0:T(8,128)(2,1)S(1)}, u32[]{:S(2)}, u32[]{:S(2)}) async-start(bf16[8,128,256]{2,1,0:T(8,128)(2,1)} %get-tuple-element.77), calls=%async_computation.2 | async-start | bytes 1048576 | tf_op jit(solution)/shard_map/cond/branch_1_fun/all_to_all | solution.py:590
  15.7 31.8 %collective-permute-start.7 = (bf16[256,1024]{1,0:T(8,128)(2,1)S(1)}, bf16[256,1024]{1,0:T(8,128)(2,1)}, u32[]{:S(2)}, u32[]{:S(2)}) collective-permute-start(bf16[256,1024]{1,0:T(8,128)(2,1)S(1)} %get-tuple-element.174), channel_id=1, source_target_pairs={{0,12},{4,0},{8,4},{12,8},{1,13},{5,1},{9,5},{13,9},{2,14},{6,2},{... | collective-permute-start | bytes 1572872 | tf_op jit(solution)/shard_map/cond/branch_1_fun/ppermute | solution.py:539
  18.8 28.8 %collective-permute-start.6 = (bf16[256,1024]{1,0:T(8,128)(2,1)S(1)}, bf16[256,1024]{1,0:T(8,128)(2,1)}, u32[]{:S(2)}, u32[]{:S(2)}) collective-permute-start(bf16[256,1024]{1,0:T(8,128)(2,1)S(1)} %get-tuple-element.175), channel_id=1, source_target_pairs={{0,8},{4,12},{8,0},{12,4},{1,9},{5,13},{9,1},{13,5},{2,10},{6,14},... | collective-permute-start | bytes 1572872 | tf_op jit(solution)/shard_map/cond/branch_1_fun/ppermute | solution.py:539
  19.4 28.2 %collective-permute-start.5 = (bf16[256,1024]{1,0:T(8,128)(2,1)S(1)}, bf16[256,1024]{1,0:T(8,128)(2,1)}, u32[]{:S(2)}, u32[]{:S(2)}) collective-permute-start(bf16[256,1024]{1,0:T(8,128)(2,1)S(1)} %get-tuple-element.176), channel_id=1, source_target_pairs={{0,4},{4,8},{8,12},{12,0},{1,5},{5,9},{9,13},{13,1},{2,6},{6,10},{... | collective-permute-start | bytes 1572872 | tf_op jit(solution)/shard_map/cond/branch_1_fun/ppermute | solution.py:539
  27.9 19.6 %collective-permute-start.9 = (bf16[64,1024]{1,0:T(8,128)(2,1)}, bf16[64,1024]{1,0:T(8,128)(2,1)S(1)}, u32[]{:S(2)}, u32[]{:S(2)}) collective-permute-start(bf16[64,1024]{1,0:T(8,128)(2,1)} %get-tuple-element.85), channel_id=1, source_target_pairs={{0,2},{1,6},{2,10},{3,14},{4,3},{5,7},{6,11},{7,15},{8,0},{9,4},{1... | collective-permute-start | bytes 393224 | tf_op jit(solution)/shard_map/cond/branch_1_fun/ppermute | solution.py:570
  28.6 18.9 %collective-permute-start.8 = (bf16[64,1024]{1,0:T(8,128)(2,1)}, bf16[64,1024]{1,0:T(8,128)(2,1)S(1)}, u32[]{:S(2)}, u32[]{:S(2)}) collective-permute-start(bf16[64,1024]{1,0:T(8,128)(2,1)} %get-tuple-element.85), channel_id=1, source_target_pairs={{0,0},{1,4},{2,8},{3,12},{4,1},{5,5},{6,9},{7,13},{8,2},{9,6},{10,... | collective-permute-start | bytes 393224 | tf_op jit(solution)/shard_map/cond/branch_1_fun/ppermute | solution.py:570
  31.0 20.4 %all-to-all-start.3 = ((bf16[8,128,256]{2,1,0:T(8,128)(2,1)}), bf16[8,128,256]{2,1,0:T(8,128)(2,1)S(1)}, u32[]{:S(2)}, u32[]{:S(2)}) async-start(bf16[8,128,256]{2,1,0:T(8,128)(2,1)} %attend.3), calls=%async_computation.3 | async-start | bytes 1048576 | tf_op jit(solution)/shard_map/cond/branch_1_fun/all_to_all | solution.py:595
  52.1 8.4 %collective-permute-start.12 = (bf16[256,256]{1,0:T(8,128)(2,1)S(1)}, bf16[256,256]{1,0:T(8,128)(2,1)S(1)}, u32[]{:S(2)}, u32[]{:S(2)}) collective-permute-start(bf16[256,256]{1,0:T(8,128)(2,1)S(1)} %get-tuple-element.136.refs_0_), channel_id=1, source_target_pairs={{0,12},{4,0},{8,4},{12,8},{1,13},{5,1},{9,5},{13,9},{2,14},{6,2},{... | collective-permute-start | bytes 393224 | tf_op jit(solution)/shard_map/ppermute | solution.py:539
  55.1 6.7 %collective-permute-start.11 = (bf16[256,256]{1,0:T(8,128)(2,1)S(1)}, bf16[256,256]{1,0:T(8,128)(2,1)S(1)}, u32[]{:S(2)}, u32[]{:S(2)}) collective-permute-start(bf16[256,256]{1,0:T(8,128)(2,1)S(1)} %get-tuple-element.136.refs_0_), channel_id=1, source_target_pairs={{0,8},{4,12},{8,0},{12,4},{1,9},{5,13},{9,1},{13,5},{2,10},{6,14},... | collective-permute-start | bytes 393224 | tf_op jit(solution)/shard_map/ppermute | solution.py:539
  55.6 7.5 %collective-permute-start.10 = (bf16[256,256]{1,0:T(8,128)(2,1)S(1)}, bf16[256,256]{1,0:T(8,128)(2,1)S(1)}, u32[]{:S(2)}, u32[]{:S(2)}) collective-permute-start(bf16[256,256]{1,0:T(8,128)(2,1)S(1)} %get-tuple-element.136.refs_0_), channel_id=1, source_target_pairs={{0,4},{4,8},{8,12},{12,0},{1,5},{5,9},{9,13},{13,1},{2,6},{6,10},{... | collective-permute-start | bytes 393224 | tf_op jit(solution)/shard_map/ppermute | solution.py:539
  65.2 1.6 %collective-permute-start.13 = (bf16[2,64,1024]{2,1,0:T(8,128)(2,1)S(1)}, bf16[2,64,1024]{2,1,0:T(8,128)(2,1)S(1)}, u32[]{:S(2)}, u32[]{:S(2)}) collective-permute-start(bf16[2,64,1024]{2,1,0:T(8,128)(2,1)S(1)} %get-tuple-element.142._), channel_id=1, source_target_pairs={{0,1},{1,0},{2,3},{3,2},{4,5},{5,4},{6,7},{7,6},{8,9},{9,8},{10,11... | collective-permute-start | bytes 786440 | tf_op jit(solution)/shard_map/ppermute | solution.py:545
  66.9 8.4 %collective-permute-start.14 = (bf16[2,64,1024]{2,1,0:T(8,128)(2,1)S(1)}, bf16[2,64,1024]{2,1,0:T(8,128)(2,1)S(1)}, u32[]{:S(2)}, u32[]{:S(2)}) collective-permute-start(bf16[2,64,1024]{2,1,0:T(8,128)(2,1)S(1)} %add_convert_fusion.near_ref), channel_id=1, source_target_pairs={{0,2},{1,3},{2,0},{3,1},{4,6},{5,7},{6,4},{7,5},{8,10},{9,11},{10,... | collective-permute-start | bytes 786440 | tf_op jit(solution)/shard_map/ppermute | solution.py:548
  75.7 8.7 %collective-permute-start.16 = (bf16[64,1024]{1,0:T(8,128)(2,1)S(1)}, bf16[64,1024]{1,0:T(8,128)(2,1)S(1)}, u32[]{:S(2)}, u32[]{:S(2)}) collective-permute-start(bf16[64,1024]{1,0:T(8,128)(2,1)S(1)} %get-tuple-element.147._), channel_id=1, source_target_pairs={{0,0},{1,4},{2,8},{3,12},{4,1},{5,5},{6,9},{7,13},{8,2},{9,6},{10,... | collective-permute-start | bytes 393224 | tf_op jit(solution)/shard_map/ppermute | solution.py:628
  76.4 10.4 %collective-permute-start.15 = (bf16[2,48,1024]{2,1,0:T(8,128)(2,1)S(1)}, bf16[2,48,1024]{2,1,0:T(8,128)(2,1)S(1)}, u32[]{:S(2)}, u32[]{:S(2)}) collective-permute-start(bf16[2,48,1024]{2,1,0:T(8,128)(2,1)S(1)} %get-tuple-element.146), channel_id=1, source_target_pairs={{0,4},{4,8},{8,12},{12,0},{1,5},{5,9},{9,13},{13,1},{2,6},{6,10},{... | collective-permute-start | bytes 589832 | tf_op jit(solution)/shard_map/ppermute | solution.py:539
  78.6 11.1 %collective-permute-start.17 = (bf16[2,48,1024]{2,1,0:T(8,128)(2,1)S(1)}, bf16[2,48,1024]{2,1,0:T(8,128)(2,1)S(1)}, u32[]{:S(2)}, u32[]{:S(2)}) collective-permute-start(bf16[2,48,1024]{2,1,0:T(8,128)(2,1)S(1)} %get-tuple-element.151), channel_id=1, source_target_pairs={{0,8},{4,12},{8,0},{12,4},{1,9},{5,13},{9,1},{13,5},{2,10},{6,14},... | collective-permute-start | bytes 589832 | tf_op jit(solution)/shard_map/ppermute | solution.py:539
  81.2 10.7 %collective-permute-start.18 = (bf16[2,48,1024]{2,1,0:T(8,128)(2,1)S(1)}, bf16[2,48,1024]{2,1,0:T(8,128)(2,1)S(1)}, u32[]{:S(2)}, u32[]{:S(2)}) collective-permute-start(bf16[2,48,1024]{2,1,0:T(8,128)(2,1)S(1)} %get-tuple-element.152), channel_id=1, source_target_pairs={{0,12},{4,0},{8,4},{12,8},{1,13},{5,1},{9,5},{13,9},{2,14},{6,2},{... | collective-permute-start | bytes 589832 | tf_op jit(solution)/shard_map/ppermute | solution.py:539
  83.6 8.9 %collective-permute-start.19 = (bf16[2,48,1024]{2,1,0:T(8,128)(2,1)S(1)}, bf16[2,48,1024]{2,1,0:T(8,128)(2,1)S(1)}, u32[]{:S(2)}, u32[]{:S(2)}) collective-permute-start(bf16[2,48,1024]{2,1,0:T(8,128)(2,1)S(1)} %get-tuple-element.149.refs_0_), channel_id=1, source_target_pairs={{0,1},{1,0},{2,3},{3,2},{4,5},{5,4},{6,7},{7,6},{8,9},{9,8},{10,11... | collective-permute-start | bytes 589832 | tf_op jit(solution)/shard_map/ppermute | solution.py:545
  89.7 2.8 %collective-permute-start.21 = (bf16[2,48,1024]{2,1,0:T(8,128)(2,1)S(1)}, bf16[2,48,1024]{2,1,0:T(8,128)(2,1)S(1)}, u32[]{:S(2)}, u32[]{:S(2)}) collective-permute-start(bf16[2,48,1024]{2,1,0:T(8,128)(2,1)S(1)} %collective-permute-done.17.refs_2_), channel_id=1, source_target_pairs={{0,1},{1,0},{2,3},{3,2},{4,5},{5,4},{6,7},{7,6},{8,9},{9,8},{10,11... | collective-permute-start | bytes 589832 | tf_op jit(solution)/shard_map/ppermute | solution.py:545
  91.9 1.7 %collective-permute-start.20 = (bf16[2,48,1024]{2,1,0:T(8,128)(2,1)S(1)}, bf16[2,48,1024]{2,1,0:T(8,128)(2,1)S(1)}, u32[]{:S(2)}, u32[]{:S(2)}) collective-permute-start(bf16[2,48,1024]{2,1,0:T(8,128)(2,1)S(1)} %collective-permute-done.15.refs_1_), channel_id=1, source_target_pairs={{0,1},{1,0},{2,3},{3,2},{4,5},{5,4},{6,7},{7,6},{8,9},{9,8},{10,11... | collective-permute-start | bytes 589832 | tf_op jit(solution)/shard_map/ppermute | solution.py:545
  100.5 2.4 %collective-permute-start.23 = (bf16[2,192,1024]{2,1,0:T(8,128)(2,1)S(1)}, bf16[2,192,1024]{2,1,0:T(8,128)(2,1)S(1)}, u32[]{:S(2)}, u32[]{:S(2)}) collective-permute-start(bf16[2,192,1024]{2,1,0:T(8,128)(2,1)S(1)} %get-tuple-element.157), channel_id=1, source_target_pairs={{0,1},{1,0},{2,3},{3,2},{4,5},{5,4},{6,7},{7,6},{8,9},{9,8},{10,11... | collective-permute-start | bytes 2359304 | tf_op jit(solution)/shard_map/ppermute | solution.py:545
  103.0 8.3 %collective-permute-start.24 = (bf16[2,48,1024]{2,1,0:T(8,128)(2,1)S(1)}, bf16[2,48,1024]{2,1,0:T(8,128)(2,1)S(1)}, u32[]{:S(2)}, u32[]{:S(2)}) collective-permute-start(bf16[2,48,1024]{2,1,0:T(8,128)(2,1)S(1)} %get-tuple-element.159), channel_id=1, source_target_pairs={{0,4},{4,8},{8,12},{12,0},{1,5},{5,9},{9,13},{13,1},{2,6},{6,10},{... | collective-permute-start | bytes 589832 | tf_op jit(solution)/shard_map/ppermute | solution.py:539
  103.1 13.3 %collective-permute-start.25 = (bf16[2,48,1024]{2,1,0:T(8,128)(2,1)S(1)}, bf16[2,48,1024]{2,1,0:T(8,128)(2,1)S(1)}, u32[]{:S(2)}, u32[]{:S(2)}) collective-permute-start(bf16[2,48,1024]{2,1,0:T(8,128)(2,1)S(1)} %get-tuple-element.160), channel_id=1, source_target_pairs={{0,8},{4,12},{8,0},{12,4},{1,9},{5,13},{9,1},{13,5},{2,10},{6,14},... | collective-permute-start | bytes 589832 | tf_op jit(solution)/shard_map/ppermute | solution.py:539
  107.2 9.2 %collective-permute-start.26 = (bf16[2,48,1024]{2,1,0:T(8,128)(2,1)S(1)}, bf16[2,48,1024]{2,1,0:T(8,128)(2,1)S(1)}, u32[]{:S(2)}, u32[]{:S(2)}) collective-permute-start(bf16[2,48,1024]{2,1,0:T(8,128)(2,1)S(1)} %get-tuple-element.161), channel_id=1, source_target_pairs={{0,12},{4,0},{8,4},{12,8},{1,13},{5,1},{9,5},{13,9},{2,14},{6,2},{... | collective-permute-start | bytes 589832 | tf_op jit(solution)/shard_map/ppermute | solution.py:539
  116.9 5.3 %collective-permute-start.27 = (bf16[64,1024]{1,0:T(8,128)(2,1)S(1)}, bf16[64,1024]{1,0:T(8,128)(2,1)S(1)}, u32[]{:S(2)}, u32[]{:S(2)}) collective-permute-start(bf16[64,1024]{1,0:T(8,128)(2,1)S(1)} %get-tuple-element.163), channel_id=1, source_target_pairs={{0,2},{1,3},{2,0},{3,1},{4,6},{5,7},{6,4},{7,5},{8,10},{9,11},{10,... | collective-permute-start | bytes 393224 | tf_op jit(solution)/shard_map/ppermute | solution.py:548
  (7 other events, 67.1 us)

commit v3 on v2

--- a/solution.py
+++ b/solution.py
@@ -254,13 +254,29 @@
     )(slots, boxes)
 
 
-def project_kernel(place, *refs):
+def begin_kernel(*refs):
+    parts = (len(refs) - 2) // 4
+    late_from, late_to, sems = refs[2 * parts : 3 * parts], refs[3 * parts + 1 : 4 * parts + 1], refs[-1]
+    copies = [
+        pltpu.make_async_copy(late_from[part], late_to[part], sems.at[part]) for part in range(parts)
+    ]
+    for copy in copies:
+        copy.start()
+    acc = dot(refs[0][...], refs[parts][...])
+    for part in range(1, parts):
+        acc = acc + dot(refs[part][...], refs[parts + part][...])
+    refs[3 * parts][...] = acc
+    for copy in copies:
+        copy.wait()
+
+
+def project_kernel(place, begun_ref, *refs):
     parts = (len(refs) - 3) // 2
     ctx_refs, proj_refs = refs[:parts], refs[parts : 2 * parts]
     send_ref, keep_ref, full = refs[2 * parts :]
     rows = send_ref.shape[1]
-    acc = dot(ctx_refs[0][...], proj_refs[0][...])
-    for part in range(1, parts):
+    acc = begun_ref[...]
+    for part in range(parts):
         acc = acc + dot(ctx_refs[part][...], proj_refs[part][...])
     full[...] = acc
     core = place[0]
@@ -272,29 +288,45 @@
 
 
 def project(core, contexts, projs):
-    rows, _ = contexts[0].shape
+    rows, width = contexts[0].shape
     cols = projs[0].shape[1]
-    in_vmem = pl.BlockSpec(memory_space=pltpu.VMEM)
+    early, late = (0, 3), (1, 2)
+    in_vmem = pl.BlockSpec(memory_space=pltpu.VMEM)
+    in_any = pl.BlockSpec(memory_space=pl.ANY)
+    begun, *late_projs = pl.pallas_call(
+        begin_kernel,
+        out_shape=(jax.ShapeDtypeStruct((rows, cols), F32),)
+        + (jax.ShapeDtypeStruct((width, cols), BF16),) * len(late),
+        in_specs=[in_vmem] * 4 + [in_any] * len(late),
+        out_specs=(in_vmem,) * (1 + len(late)),
+        scratch_shapes=[pltpu.SemaphoreType.DMA((len(late),))],
+        cost_estimate=pl.CostEstimate(flops=5 * 10**8, bytes_accessed=2 * 10**6, transcendentals=0),
+        compiler_params=pltpu.CompilerParams(vmem_limit_bytes=24 * 1024 * 1024),
+        name="begin",
+    )(
+        *[contexts[part] for part in early],
+        *[projs[part] for part in early],
+        *[projs[part] for part in late],
+    )
     return pl.pallas_call(
         project_kernel,
         out_shape=(
             jax.ShapeDtypeStruct((2, rows // 4, cols), BF16),
             jax.ShapeDtypeStruct((2, rows // 4, cols), F32),
         ),
-        in_specs=[pl.BlockSpec(memory_space=pltpu.SMEM)] + [in_vmem] * (len(contexts) + len(projs)),
+        in_specs=[pl.BlockSpec(memory_space=pltpu.SMEM)] + [in_vmem] * 5,
         out_specs=(in_vmem, in_vmem),
         scratch_shapes=[pltpu.VMEM((rows, cols), F32)],
-        cost_estimate=pl.CostEstimate(flops=10**9, bytes_accessed=4 * 10**6, transcendentals=0),
+        cost_estimate=pl.CostEstimate(flops=5 * 10**8, bytes_accessed=2 * 10**6, transcendentals=0),
         compiler_params=pltpu.CompilerParams(vmem_limit_bytes=24 * 1024 * 1024),
         name="project",
-    )(core, *contexts, *projs)
-
-
-def dispatch_kernel(place, near_ref, got_ref, hidden_ref, slot_ref, own_ref, *refs):
+    )(core, begun, *[contexts[part] for part in late], *late_projs)
+
+
+def dispatch_kernel(place, near_ref, got_ref, slot_ref, own_ref, *refs):
     box_refs, resid_ref = refs[:-1], refs[-1]
     for far in range(2):
-        summed = near_ref[far].astype(F32) + got_ref[far].astype(F32)
-        residual = (hidden_ref[far].astype(F32) + summed).astype(BF16)
+        residual = (near_ref[far].astype(F32) + got_ref[far].astype(F32)).astype(BF16)
         resid_ref[far] = residual
         for step, box_ref in enumerate(box_refs):
             index = step * 2 + far
@@ -303,7 +335,7 @@
     own_ref[...] = resid_ref[place[0]]
 
 
-def dispatch(far, near, got, hidden, slots):
+def dispatch(far, near, got, slots):
     _, _, cols = near.shape
     steps = slots.shape[0] // 2
     in_vmem = pl.BlockSpec(memory_space=pltpu.VMEM)
@@ -311,13 +343,13 @@
         dispatch_kernel,
         out_shape=(jax.ShapeDtypeStruct(near.shape[1:], BF16),)
         + (jax.ShapeDtypeStruct((2, CAP, cols), BF16),) * steps,
-        in_specs=[pl.BlockSpec(memory_space=pltpu.SMEM)] + [in_vmem] * 4,
+        in_specs=[pl.BlockSpec(memory_space=pltpu.SMEM)] + [in_vmem] * 3,
         out_specs=(in_vmem,) * (1 + steps),
         scratch_shapes=[pltpu.VMEM(near.shape, BF16)],
         cost_estimate=pl.CostEstimate(flops=10**8, bytes_accessed=2 * 10**6, transcendentals=0),
         compiler_params=pltpu.CompilerParams(vmem_limit_bytes=8 * 1024 * 1024),
         name="dispatch",
-    )(far, near, got, hidden, slots)
+    )(far, near, got, slots)
 
 
 def hold_kernel(from_ref, _, held_ref, sems):
@@ -350,14 +382,13 @@
 
 
 IN_COLS = 640
-OUT_COLS = 1024
 
 
 def expert_kernel(place, *refs):
     parts = 4
     row_refs = refs[: 2 * parts]
-    gain_ref, router_ref, choose_ref, w_in, w_out, send_ref, keep_ref = refs[2 * parts : 2 * parts + 7]
-    rows_all, hidden = refs[2 * parts + 7 :]
+    gain_ref, router_ref, choose_ref, w_in, w_out, send_ref, hidden, gate_ref = refs[2 * parts : 2 * parts + 8]
+    (rows_all,) = refs[2 * parts + 8 :]
     narrow_at, core = place[0], place[1]
     features, hidden_units = w_in.shape
     _, slots, quarter = row_refs[0].shape
@@ -399,17 +430,31 @@
             term = dot(rows_all[part], w_in[pl.ds(at, quarter), cols])
             acc = term if acc is None else acc + term
         hidden[:, cols] = jax.nn.gelu(acc, approximate=True).astype(BF16)
-    for kept in range(2):
-        side = core if kept else 1 - core
-        for far in range(2):
-            for step in range(quarter // OUT_COLS):
-                at = pl.multiple_of((far * 2 + side) * quarter + step * OUT_COLS, OUT_COLS)
-                acc = dot(hidden[...], w_out[:, pl.ds(at, OUT_COLS)]) * gate
-                cols = slice(step * OUT_COLS, (step + 1) * OUT_COLS)
-                if kept:
-                    keep_ref[far, :, cols] = acc
-                else:
-                    send_ref[far, :, cols] = acc.astype(BF16)
+    gate_ref[...] = jnp.broadcast_to(gate, gate_ref.shape)
+    for far in range(2):
+        at = pl.multiple_of((far * 2 + 1 - core) * quarter, quarter)
+        send_ref[far] = (dot(hidden[...], w_out[:, pl.ds(at, quarter)]) * gate).astype(BF16)
+
+
+def finish_kernel(place, hidden, gate_ref, w_out, keep_ref):
+    quarter = keep_ref.shape[2]
+    gate = gate_ref[:, :1]
+    for far in range(2):
+        at = pl.multiple_of((far * 2 + place[1]) * quarter, quarter)
+        keep_ref[far] = dot(hidden[...], w_out[:, pl.ds(at, quarter)]) * gate
+
+
+def finish(place, hidden, gate, w_out):
+    in_vmem = pl.BlockSpec(memory_space=pltpu.VMEM)
+    return pl.pallas_call(
+        finish_kernel,
+        out_shape=jax.ShapeDtypeStruct((2, hidden.shape[0], w_out.shape[1] // 4), F32),
+        in_specs=[pl.BlockSpec(memory_space=pltpu.SMEM)] + [in_vmem] * 3,
+        out_specs=in_vmem,
+        cost_estimate=pl.CostEstimate(flops=10**9, bytes_accessed=8 * 10**6, transcendentals=0),
+        compiler_params=pltpu.CompilerParams(vmem_limit_bytes=8 * 1024 * 1024),
+        name="finish",
+    )(place, hidden, gate, w_out)
 
 
 def expert(place, own, other, gain, router, choose, w_in, w_out):
@@ -422,14 +467,14 @@
         expert_kernel,
         out_shape=(
             jax.ShapeDtypeStruct((2, rows, quarter), BF16),
-            jax.ShapeDtypeStruct((2, rows, quarter), F32),
+            jax.ShapeDtypeStruct((rows, units), BF16),
+            jax.ShapeDtypeStruct((rows, 128), F32),
         ),
         in_specs=[pl.BlockSpec(memory_space=pltpu.SMEM)]
         + [in_vmem] * (2 * parts + 5),
-        out_specs=(in_vmem, in_vmem),
+        out_specs=(in_vmem,) * 3,
         scratch_shapes=[
             pltpu.VMEM((parts, rows, quarter), BF16),
-            pltpu.VMEM((rows, units), BF16),
         ],
         cost_estimate=pl.CostEstimate(flops=4 * 10**9, bytes_accessed=24 * 10**6, transcendentals=10**5),
         compiler_params=pltpu.CompilerParams(vmem_limit_bytes=12 * 1024 * 1024),
@@ -497,7 +542,9 @@
 
 
 def pick_at(values, index, axis=0):
-    return lax.dynamic_index_in_dim(values, index, axis, keepdims=False)
+    return lax.dynamic_index_in_dim(
+        values, index, axis, keepdims=False, allow_negative_indices=False
+    )
 
 
 def body(
@@ -523,16 +570,15 @@
     wide_at = lax.axis_index("wide")
     narrow_at = lax.axis_index("narrow")
     depth_at = lax.axis_index("depth")
-    core, far = depth_at % 2, depth_at // 2
+    core, far = depth_at & 1, depth_at >> 1
     core_perm = [(i, i ^ 1) for i in range(depth_count)]
     far_perm = [(i, i ^ 2) for i in range(depth_count)]
 
-    def swap_perm(flip):
-        return [
-            (n * depth_count + d, d * narrow_count + (n ^ flip))
-            for n in range(narrow_count)
-            for d in range(depth_count)
-        ]
+    swap_perm = [
+        (n * depth_count + d, d * narrow_count + n)
+        for n in range(narrow_count)
+        for d in range(depth_count)
+    ]
 
     def around(values):
         return [values[0]] + [
@@ -547,17 +593,17 @@
     def to_far(value):
         return lax.ppermute(value, "depth", far_perm)
 
-    around_to = (narrow_at + jnp.arange(narrow_count)) % narrow_count
-
-    def prepared(hidden_in, expert_ids):
-        id_blocks = expert_ids.reshape(-1, tok_rows, 2)
+    last = narrow_count - 1
+    around_to = [(narrow_at + step) & last for step in peers]
+
+    def prepared(id_blocks):
         names = id_blocks[:, :, :, None] == jnp.arange(experts, dtype=jnp.int32)
         named = jnp.any(names, axis=2)
         ranks = jnp.where(named, jnp.cumsum(named.astype(jnp.int32), axis=1) - 1, -1)
         ranks = jnp.moveaxis(ranks, 2, 0)
         my_blocks = jnp.stack([core, 2 + core])
-        around_from = (narrow_at - jnp.arange(narrow_count)) % narrow_count
-        send_slots = ranks[around_to][:, my_blocks].reshape(2 * narrow_count, tok_rows)
+        around_from = (narrow_at - jnp.arange(narrow_count, dtype=jnp.int32)) & last
+        send_slots = ranks[jnp.stack(around_to)][:, my_blocks].reshape(2 * narrow_count, tok_rows)
         get_slots = pick_at(ranks, narrow_at, 1)[around_from]
         my_ranks = pick_at(ranks, narrow_at)
         filled = my_ranks[:, None, :] == jnp.arange(CAP, dtype=jnp.int32)[None, :, None]
@@ -566,21 +612,23 @@
         choose = jnp.sum(jnp.where(filled[:, :, :, None], weigh[:, None, :, :], 0.0), axis=2)
         choose = choose.reshape(-1, experts)
         choose = jnp.pad(jnp.concatenate([choose] * 3, axis=1), ((0, 0), (0, 128 - 3 * experts)))
-        hidden_blocks = [
-            lax.ppermute(hidden_in, ("narrow", "depth"), swap_perm(flip)) for flip in (0, 2)
-        ]
-        near_hidden = jnp.where(far == 0, hidden_blocks[0], hidden_blocks[1])
-        far_hidden = jnp.where(far == 0, hidden_blocks[1], hidden_blocks[0])
-        hidden_swapped = jnp.stack([near_hidden, far_hidden])
         return tuple(
             with_layout_constraint(value, Layout(tuple(range(value.ndim))))
-            for value in (hidden_swapped, send_slots, get_slots, choose)
-        )
+            for value in (send_slots, get_slots, choose)
+        )
+
+    def swapped(value):
+        return lax.ppermute(value, ("narrow", "depth"), swap_perm)
 
     def spread():
         projs = around(
             [
-                lax.dynamic_slice_in_dim(attn_proj, around_to[step] * quarter, quarter, 1)
+                lax.dynamic_slice(
+                    attn_proj,
+                    (0, around_to[step] * quarter),
+                    (attn_proj.shape[0], quarter),
+                    allow_negative_indices=False,
+                )
                 for step in peers
             ],
         )
@@ -589,12 +637,14 @@
     def exchanged(boxes, attend_to, gathered):
         segment = lax.all_to_all(boxes, "wide", split_axis=0, concat_axis=0, tiled=True)
         projs = spread()
-        partial, *late = lax.optimization_barrier(
-            (attend_to(segment), hidden_in, expert_ids)
+        partial, id_blocks, hidden = lax.optimization_barrier(
+            (attend_to(segment), expert_ids.reshape(-1, tok_rows, 2), hidden_in)
         )
         returned = lax.all_to_all(partial, "wide", split_axis=0, concat_axis=0, tiled=True)
-        returned, projs, ready = lax.optimization_barrier((returned, projs, prepared(*late)))
-        return gathered(returned), projs, ready
+        returned, projs, hidden, ready = lax.optimization_barrier(
+            (returned, projs, swapped(hidden), prepared(id_blocks))
+        )
+        return gathered(returned), projs, (hidden, *ready)
 
     def routed(boxes):
         return exchanged(
@@ -619,18 +669,20 @@
     contexts = around([context] * narrow_count)
 
     send, keep = project(core[None], contexts, projs)
-    near = (keep + to_core(send).astype(F32)).astype(BF16)
+    own_block = jnp.where(jnp.arange(2)[:, None, None] == far, hidden_swapped.astype(F32), 0.0)
+    near = (keep + to_core(send).astype(F32) + own_block).astype(BF16)
     w_in = hold(proj_in[0], send, 2)
     got, w_in = lax.optimization_barrier((to_far(near), w_in))
-    residual, *boxes = dispatch(far[None], near, got, hidden_swapped, send_slots)
+    residual, *boxes = dispatch(far[None], near, got, send_slots)
     own_rows = around(boxes)
     w_out = hold(proj_out[0], residual, 2)
-    own_resid = lax.ppermute(residual, ("narrow", "depth"), swap_perm(0))
+    own_resid = lax.ppermute(residual, ("narrow", "depth"), swap_perm)
     own_rows[1], w_out, own_resid = lax.optimization_barrier((own_rows[1], w_out, own_resid))
     other_rows = [to_core(part) for part in own_rows]
 
-    out_send, out_keep = expert(
-        jnp.stack([narrow_at, core]),
+    place = jnp.stack([narrow_at, core])
+    out_send, hidden, gate = expert(
+        place,
         own_rows,
         other_rows,
         norm_gain.reshape(narrow_count, 1, quarter),
@@ -639,6 +691,7 @@
         w_in,
         w_out,
     )
+    out_keep = finish(place, hidden, gate, w_out)
     arrived = around(share(narrow_at[None], out_keep, to_core(out_send), narrow_count))
     far_send, own_sum = combine(far[None], get_slots, own_resid, arrived)
     return (own_sum + to_far(far_send).astype(F32)).astype(BF16)

time: 124 us -> 115 us (0.927)
  waiting for transfers between devices: 45.9 us -> 38.7 us
  loops' own time: 2.67 us -> 0.16 us
  Pallas kernels: 19 us -> 20.5 us
    ppermute x3 -> x2, waiting for transfers between devices: 6.43 us -> 0.01 us  [the longest x1 0.01 us: swapped(): return lax.ppermute(value, ('narrow', 'depth'), swap_perm)]
    pallas_call x0 -> x2, Pallas kernels: none -> 4.09 us  [the longest x1 2.35 us: project(): pl.pallas_call(begin_kernel, out_shape=(jax.ShapeDtypeStruct((rows, cols)...]
    ppermute x6, waiting for transfers between devices: 4.72 us -> 2.01 us  [to_core(): return lax.ppermute(value, 'depth', core_perm)]
    another operation x1, loops' own time: 2.67 us -> 0.16 us  [body(): context, projs, ready = lax.cond(fits[0] == 1, routed, general, boxes)]
    all_to_all x1, waiting for transfers between devices: 1.87 us -> 4.21 us  [exchanged(): lax.all_to_all(boxes, 'wide', split_axis=0, concat_axis=0, tiled=True)]
    all_to_all x1, starting transfers between devices: 7.96 us -> 5.66 us  [exchanged(): lax.all_to_all(partial, 'wide', split_axis=0, concat_axis=0, tiled=True)]
    all_to_all x1, waiting for transfers between devices: 3.79 us -> 1.71 us  [exchanged(): lax.all_to_all(partial, 'wide', split_axis=0, concat_axis=0, tiled=True)]
    ppermute x12, waiting for transfers between devices: 22.8 us -> 24.8 us  [around(): lax.ppermute(values[step], 'narrow', ring(narrow_count, step))]
  transfers between devices with their start and end apart: 25 -> 24, of which waited for: 17 -> 17; matrix products, arithmetic and copies ran while one was open for 5% -> 6% of each run, Pallas kernels for 5% -> 9%
where the time goes in v3:
time: 115 us; the launch traced here: 114 us
  starting transfers between devices  42.1 us (37%)
  waiting for transfers between devices  38.7 us (34%)
  Pallas kernels  20.5 us (18%)
  local copies, waits for them, and re-layouts  9.26 us (8%)
  other arithmetic  2.47 us (2%)
    ppermute x12, waiting for transfers between devices, around(): lax.ppermute(values[step], 'narrow', ring(narrow_count, step))  24.8 us
    ppermute x12, starting transfers between devices, around(): lax.ppermute(values[step], 'narrow', ring(narrow_count, step))  22.1 us
    all_to_all x1, starting transfers between devices, exchanged(): lax.all_to_all(boxes, 'wide', split_axis=0, concat_axis=0, tiled=True)  7.9 us
    pallas_call x1, Pallas kernels, expert(): pl.pallas_call(expert_kernel, out_shape=(jax.ShapeDtypeStruct((2, rows, q...  5.91 us
    ppermute x2, waiting for transfers between devices, to_far(): return lax.ppermute(value, 'depth', far_perm)  5.88 us
    all_to_all x1, starting transfers between devices, exchanged(): lax.all_to_all(partial, 'wide', split_axis=0, concat_axis=0, tiled=True)  5.66 us
    pallas_call x1, Pallas kernels, attend_routed(): pl.pallas_call(routed_kernel, out_shape=jax.ShapeDtypeStruct(queries.shap...  4.56 us
    all_to_all x1, waiting for transfers between devices, exchanged(): lax.all_to_all(boxes, 'wide', split_axis=0, concat_axis=0, tiled=True)  4.21 us
  transfers between devices with their start and end apart: 24, of which 17 were waited for; matrix products, arithmetic and copies ran while one was open for 6% of the time, Pallas kernels for 9%

profile of v3, /device:TPU:0, one launch (start us, length us, event | category | flops | bytes accessed | tf_op | source)
XLA Modules:
  0.0 114.0 jit_solution(13250836678609240812)
XLA Ops:
  0.0 2.2 %route.1 = (bf16[8,128,256]{2,1,0:T(8,128)(2,1)}, s32[8,256]{1,0:T(8,128)S(1)}, s32[8]{0:T(128)S(1)}, s32[1]{0:T(128)}) custom-call(s32[1]{0:T(128)} %bitcast.34.place, s32[8]{0:T(128)} %slot_of.1, s32[16,128]{1,0:T(8,128)} %bitcast.71, bf16[256,256]{1,0:T(8,128)(2,1)} %q_ref.1), custom_call_target="tpu_custom_call" | custom-call | flops 100000000 | bytes 1000000 | tf_op jit(solution)/shard_map/route/pallas_call | solution.py:157
  2.9 41.1 %conditional.1 = (bf16[256,256]{1,0:T(8,128)(2,1)S(1)}, bf16[256,1024]{1,0:T(8,128)(2,1)S(1)}, bf16[256,1024]{1,0:T(8,128)(2,1)}, bf16[256,1024]{1,0:T(8,128)(2,...) conditional(s32[]{:T(128)} %bitcast.36, (s32[]{:T(128)}, ...), branch_computations={%region_0.6_spmd, %region_6.10_spmd} | conditional | flops 1100189184 | bytes 23979870 | solution.py:667
  2.9 7.9 %all-to-all-start.2 = ((bf16[8,128,256]{2,1,0:T(8,128)(2,1)}), bf16[8,128,256]{2,1,0:T(8,128)(2,1)S(1)}, u32[]{:S(2)}, u32[]{:S(2)}) async-start(bf16[8,128,256]{2,1,0:T(8,128)(2,1)} %get-tuple-element.87), calls=%async_computation.2 | async-start | bytes 1048576 | tf_op jit(solution)/shard_map/cond/branch_1_fun/all_to_all | solution.py:638
  12.5 3.1 %collective-permute-start.6 = (bf16[256,1024]{1,0:T(8,128)(2,1)S(1)}, bf16[256,1024]{1,0:T(8,128)(2,1)}, u32[]{:S(2)}, u32[]{:S(2)}) collective-permute-start(bf16[256,1024]{1,0:T(8,128)(2,1)S(1)} %get-tuple-element.188), channel_id=1, source_target_pairs={{0,12},{4,0},{8,4},{12,8},{1,13},{5,1},{9,5},{13,9},{2,14},{6,2},{... | collective-permute-start | bytes 1572872 | tf_op jit(solution)/shard_map/cond/branch_1_fun/ppermute | solution.py:585
  18.2 4.2 %all-to-all-done.2.q_ref = bf16[8,128,256]{2,1,0:T(8,128)(2,1)S(1)} async-done(((bf16[8,128,256]{2,1,0:T(8,128)(2,1)}), bf16[8,128,256]{2,1,0:T(8,128)(2,1)S(1)}, u32[]{:S(2)}, u32[]{:S(2)}) %all-to-all-start.2) | async-done | bytes 524320 | tf_op jit(solution)/shard_map/cond/branch_1_fun/all_to_all | solution.py:638
  22.4 4.6 %attend.3 = bf16[8,128,256]{2,1,0:T(8,128)(2,1)} custom-call(s32[8]{0:T(128)S(1)} %get-tuple-element.86.counts, bf16[8,128,256]{2,1,0:T(8,128)(2,1)S(1)} %all-to-all-done.2.q_ref, bf16[2,768,256]{2,1,0:T(8,128)(2,1)} %bitcast.73), custom_call_target="tpu_custom_call" | custom-call | flops 1000000000 | bytes 4000000 | tf_op jit(solution)/shard_map/cond/branch_1_fun/attend/pallas_call | solution.py:213
  27.2 5.7 %all-to-all-start.3 = ((bf16[8,128,256]{2,1,0:T(8,128)(2,1)}), bf16[8,128,256]{2,1,0:T(8,128)(2,1)S(1)}, u32[]{:S(2)}, u32[]{:S(2)}) async-start(bf16[8,128,256]{2,1,0:T(8,128)(2,1)} %attend.3), calls=%async_computation.3 | async-start | bytes 1048576 | tf_op jit(solution)/shard_map/cond/branch_1_fun/all_to_all | solution.py:643
  33.4 2.1 %collective-permute-start.7 = (bf16[64,1024]{1,0:T(8,128)(2,1)}, bf16[64,1024]{1,0:T(8,128)(2,1)}, u32[]{:S(2)}, u32[]{:S(2)}) collective-permute-start(bf16[64,1024]{1,0:T(8,128)(2,1)} %get-tuple-element.97), channel_id=1, source_target_pairs={{0,0},{1,4},{2,8},{3,12},{4,1},{5,5},{6,9},{7,13},{8,2},{9,6},{10,... | collective-permute-start | bytes 393224 | tf_op jit(solution)/shard_map/cond/branch_1_fun/ppermute | solution.py:621
  37.9 3.6 %collective-permute-done.4 = bf16[256,1024]{1,0:T(8,128)(2,1)} collective-permute-done((bf16[256,1024]{1,0:T(8,128)(2,1)S(1)}, bf16[256,1024]{1,0:T(8,128)(2,1)}, u32[]{:S(2)}, u32[]{:S(2)}) %collective-permute-start.4) | collective-permute-done | bytes 524320 | tf_op jit(solution)/shard_map/cond/branch_1_fun/ppermute | solution.py:585
  44.0 4.6 %collective-permute-start.8 = (bf16[256,256]{1,0:T(8,128)(2,1)S(1)}, bf16[256,256]{1,0:T(8,128)(2,1)S(1)}, u32[]{:S(2)}, u32[]{:S(2)}) collective-permute-start(bf16[256,256]{1,0:T(8,128)(2,1)S(1)} %get-tuple-element.152.refs_0_), channel_id=1, source_target_pairs={{0,12},{4,0},{8,4},{12,8},{1,13},{5,1},{9,5},{13,9},{2,14},{6,2},{... | collective-permute-start | bytes 393224 | tf_op jit(solution)/shard_map/ppermute | solution.py:585
  49.5 3.0 %collective-permute-done.8.refs_1_ = bf16[256,256]{1,0:T(8,128)(2,1)S(1)} collective-permute-done((bf16[256,256]{1,0:T(8,128)(2,1)S(1)}, bf16[256,256]{1,0:T(8,128)(2,1)S(1)}, u32[]{:S(2)}, u32[]{:S(2)}) %collective-permute-start.8) | collective-permute-done | bytes 131104 | tf_op jit(solution)/shard_map/ppermute | solution.py:585
  52.5 2.4 %begin.1 = (f32[256,1024]{1,0:T(8,128)S(1)}, bf16[256,1024]{1,0:T(8,128)(2,1)S(1)}, bf16[256,1024]{1,0:T(8,128)(2,1)S(1)}) custom-call(bf16[256,256]{1,0:T(8,128)(2,1)S(1)} %get-tuple-element.152.refs_0_, bf16[256,256]{1,0:T(8,128)(2,1)S(1)} %collective-permute-done.8.refs_1_, bf16[256,1024]{1,0:T(8,128)(2,1)S(1)} %get-tuple-element.153.refs_2_, ...), custom_call_target="tpu_custom_call" | custom-call | flops 500000000 | bytes 2000000 | tf_op jit(solution)/shard_map/begin/pallas_call | solution.py:296
  59.4 4.2 %copy-done = bf16[1,4096,1280]{2,1,0:T(8,128)(2,1)S(1)} copy-done((bf16[1,4096,1280]{2,1,0:T(8,128)(2,1)S(1)}, bf16[1,4096,1280]{2,1,0:T(8,128)(2,1)}, u32[]{:S(2)}) %copy-start) | copy-done | bytes 10485784
  64.3 2.5 %collective-permute-done.12.got_ref = bf16[2,64,1024]{2,1,0:T(8,128)(2,1)S(1)} collective-permute-done((bf16[2,64,1024]{2,1,0:T(8,128)(2,1)S(1)}, bf16[2,64,1024]{2,1,0:T(8,128)(2,1)S(1)}, u32[]{:S(2)}, u32[]{:S(2)}) %collective-permute-start.12) | collective-permute-done | bytes 262176 | tf_op jit(solution)/shard_map/ppermute | solution.py:594
  67.9 2.2 %collective-permute-start.13 = (bf16[2,48,1024]{2,1,0:T(8,128)(2,1)S(1)}, bf16[2,48,1024]{2,1,0:T(8,128)(2,1)S(1)}, u32[]{:S(2)}, u32[]{:S(2)}) collective-permute-start(bf16[2,48,1024]{2,1,0:T(8,128)(2,1)S(1)} %get-tuple-element.165), channel_id=1, source_target_pairs={{0,4},{4,8},{8,12},{12,0},{1,5},{5,9},{9,13},{13,1},{2,6},{6,10},{... | collective-permute-start | bytes 589832 | tf_op jit(solution)/shard_map/ppermute | solution.py:585
  70.1 3.0 %collective-permute-start.15 = (bf16[2,48,1024]{2,1,0:T(8,128)(2,1)S(1)}, bf16[2,48,1024]{2,1,0:T(8,128)(2,1)S(1)}, u32[]{:S(2)}, u32[]{:S(2)}) collective-permute-start(bf16[2,48,1024]{2,1,0:T(8,128)(2,1)S(1)} %get-tuple-element.170), channel_id=1, source_target_pairs={{0,8},{4,12},{8,0},{12,4},{1,9},{5,13},{9,1},{13,5},{2,10},{6,14},... | collective-permute-start | bytes 589832 | tf_op jit(solution)/shard_map/ppermute | solution.py:585
  73.1 2.5 %collective-permute-start.16 = (bf16[2,48,1024]{2,1,0:T(8,128)(2,1)S(1)}, bf16[2,48,1024]{2,1,0:T(8,128)(2,1)S(1)}, u32[]{:S(2)}, u32[]{:S(2)}) collective-permute-start(bf16[2,48,1024]{2,1,0:T(8,128)(2,1)S(1)} %get-tuple-element.171), channel_id=1, source_target_pairs={{0,12},{4,0},{8,4},{12,8},{1,13},{5,1},{9,5},{13,9},{2,14},{6,2},{... | collective-permute-start | bytes 589832 | tf_op jit(solution)/shard_map/ppermute | solution.py:585
  77.6 3.7 %collective-permute-done.15.refs_2_ = bf16[2,48,1024]{2,1,0:T(8,128)(2,1)S(1)} collective-permute-done((bf16[2,48,1024]{2,1,0:T(8,128)(2,1)S(1)}, bf16[2,48,1024]{2,1,0:T(8,128)(2,1)S(1)}, u32[]{:S(2)}, u32[]{:S(2)}) %collective-permute-start.15) | collective-permute-done | bytes 196640 | tf_op jit(solution)/shard_map/ppermute | solution.py:585
  81.3 2.9 %collective-permute-done.16.refs_3_ = bf16[2,48,1024]{2,1,0:T(8,128)(2,1)S(1)} collective-permute-done((bf16[2,48,1024]{2,1,0:T(8,128)(2,1)S(1)}, bf16[2,48,1024]{2,1,0:T(8,128)(2,1)S(1)}, u32[]{:S(2)}, u32[]{:S(2)}) %collective-permute-start.16) | collective-permute-done | bytes 196640 | tf_op jit(solution)/shard_map/ppermute | solution.py:585
  86.0 5.9 %expert.1 = (bf16[2,192,1024]{2,1,0:T(8,128)(2,1)S(1)}, bf16[192,1280]{1,0:T(8,128)(2,1)S(1)}, f32[192,128]{1,0:T(8,128)S(1)}) custom-call(s32[2]{0:T(128)S(1)} %pad_add_fusion.place, bf16[2,48,1024]{2,1,0:T(8,128)(2,1)S(1)} %get-tuple-element.168.refs_0_, bf16[2,48,1024]{2,1,0:T(8,128)(2,1)S(1)} %collective-permute-done.13.refs_1_, ...), custom_call_target="tpu_custom_call" | custom-call | flops 4000000000 | bytes 24000000 | tf_op jit(solution)/shard_map/expert/pallas_call | solution.py:466
  94.5 4.1 %collective-permute-start.23 = (bf16[2,48,1024]{2,1,0:T(8,128)(2,1)S(1)}, bf16[2,48,1024]{2,1,0:T(8,128)(2,1)S(1)}, u32[]{:S(2)}, u32[]{:S(2)}) collective-permute-start(bf16[2,48,1024]{2,1,0:T(8,128)(2,1)S(1)} %get-tuple-element.180), channel_id=1, source_target_pairs={{0,8},{4,12},{8,0},{12,4},{1,9},{5,13},{9,1},{13,5},{2,10},{6,14},... | collective-permute-start | bytes 589832 | tf_op jit(solution)/shard_map/ppermute | solution.py:585
  98.6 4.2 %collective-permute-done.22.refs_1_ = bf16[2,48,1024]{2,1,0:T(8,128)(2,1)S(1)} collective-permute-done((bf16[2,48,1024]{2,1,0:T(8,128)(2,1)S(1)}, bf16[2,48,1024]{2,1,0:T(8,128)(2,1)S(1)}, u32[]{:S(2)}, u32[]{:S(2)}) %collective-permute-start.22) | collective-permute-done | bytes 196640 | tf_op jit(solution)/shard_map/ppermute | solution.py:585
  102.7 5.1 %collective-permute-done.23.refs_2_ = bf16[2,48,1024]{2,1,0:T(8,128)(2,1)S(1)} collective-permute-done((bf16[2,48,1024]{2,1,0:T(8,128)(2,1)S(1)}, bf16[2,48,1024]{2,1,0:T(8,128)(2,1)S(1)}, u32[]{:S(2)}, u32[]{:S(2)}) %collective-permute-start.23) | collective-permute-done | bytes 196640 | tf_op jit(solution)/shard_map/ppermute | solution.py:585
  110.0 3.4 %collective-permute-done.25 = bf16[64,1024]{1,0:T(8,128)(2,1)S(1)} collective-permute-done((bf16[64,1024]{1,0:T(8,128)(2,1)S(1)}, bf16[64,1024]{1,0:T(8,128)(2,1)S(1)}, u32[]{:S(2)}, u32[]{:S(2)}) %collective-permute-start.25) | collective-permute-done | bytes 131104 | tf_op jit(solution)/shard_map/ppermute | solution.py:594
  (88 shorter events, 26.0 us)
Async XLA Ops:
  2.9 19.5 %all-to-all-start.2 = ((bf16[8,128,256]{2,1,0:T(8,128)(2,1)}), bf16[8,128,256]{2,1,0:T(8,128)(2,1)S(1)}, u32[]{:S(2)}, u32[]{:S(2)}) async-start(bf16[8,128,256]{2,1,0:T(8,128)(2,1)} %get-tuple-element.87), calls=%async_computation.2 | async-start | bytes 1048576 | tf_op jit(solution)/shard_map/cond/branch_1_fun/all_to_all | solution.py:638
  12.5 25.4 %collective-permute-start.6 = (bf16[256,1024]{1,0:T(8,128)(2,1)S(1)}, bf16[256,1024]{1,0:T(8,128)(2,1)}, u32[]{:S(2)}, u32[]{:S(2)}) collective-permute-start(bf16[256,1024]{1,0:T(8,128)(2,1)S(1)} %get-tuple-element.188), channel_id=1, source_target_pairs={{0,12},{4,0},{8,4},{12,8},{1,13},{5,1},{9,5},{13,9},{2,14},{6,2},{... | collective-permute-start | bytes 1572872 | tf_op jit(solution)/shard_map/cond/branch_1_fun/ppermute | solution.py:585
  15.6 22.3 %collective-permute-start.5 = (bf16[256,1024]{1,0:T(8,128)(2,1)S(1)}, bf16[256,1024]{1,0:T(8,128)(2,1)}, u32[]{:S(2)}, u32[]{:S(2)}) collective-permute-start(bf16[256,1024]{1,0:T(8,128)(2,1)S(1)} %get-tuple-element.189), channel_id=1, source_target_pairs={{0,8},{4,12},{8,0},{12,4},{1,9},{5,13},{9,1},{13,5},{2,10},{6,14},... | collective-permute-start | bytes 1572872 | tf_op jit(solution)/shard_map/cond/branch_1_fun/ppermute | solution.py:585
  16.2 25.3 %collective-permute-start.4 = (bf16[256,1024]{1,0:T(8,128)(2,1)S(1)}, bf16[256,1024]{1,0:T(8,128)(2,1)}, u32[]{:S(2)}, u32[]{:S(2)}) collective-permute-start(bf16[256,1024]{1,0:T(8,128)(2,1)S(1)} %get-tuple-element.190), channel_id=1, source_target_pairs={{0,4},{4,8},{8,12},{12,0},{1,5},{5,9},{9,13},{13,1},{2,6},{6,10},{... | collective-permute-start | bytes 1572872 | tf_op jit(solution)/shard_map/cond/branch_1_fun/ppermute | solution.py:585
  27.2 16.1 %all-to-all-start.3 = ((bf16[8,128,256]{2,1,0:T(8,128)(2,1)}), bf16[8,128,256]{2,1,0:T(8,128)(2,1)S(1)}, u32[]{:S(2)}, u32[]{:S(2)}) async-start(bf16[8,128,256]{2,1,0:T(8,128)(2,1)} %attend.3), calls=%async_computation.3 | async-start | bytes 1048576 | tf_op jit(solution)/shard_map/cond/branch_1_fun/all_to_all | solution.py:643
  33.4 8.1 %collective-permute-start.7 = (bf16[64,1024]{1,0:T(8,128)(2,1)}, bf16[64,1024]{1,0:T(8,128)(2,1)}, u32[]{:S(2)}, u32[]{:S(2)}) collective-permute-start(bf16[64,1024]{1,0:T(8,128)(2,1)} %get-tuple-element.97), channel_id=1, source_target_pairs={{0,0},{1,4},{2,8},{3,12},{4,1},{5,5},{6,9},{7,13},{8,2},{9,6},{10,... | collective-permute-start | bytes 393224 | tf_op jit(solution)/shard_map/cond/branch_1_fun/ppermute | solution.py:621
  44.0 8.5 %collective-permute-start.8 = (bf16[256,256]{1,0:T(8,128)(2,1)S(1)}, bf16[256,256]{1,0:T(8,128)(2,1)S(1)}, u32[]{:S(2)}, u32[]{:S(2)}) collective-permute-start(bf16[256,256]{1,0:T(8,128)(2,1)S(1)} %get-tuple-element.152.refs_0_), channel_id=1, source_target_pairs={{0,12},{4,0},{8,4},{12,8},{1,13},{5,1},{9,5},{13,9},{2,14},{6,2},{... | collective-permute-start | bytes 393224 | tf_op jit(solution)/shard_map/ppermute | solution.py:585
  48.6 6.6 %collective-permute-start.10 = (bf16[256,256]{1,0:T(8,128)(2,1)S(1)}, bf16[256,256]{1,0:T(8,128)(2,1)S(1)}, u32[]{:S(2)}, u32[]{:S(2)}) collective-permute-start(bf16[256,256]{1,0:T(8,128)(2,1)S(1)} %get-tuple-element.152.refs_0_), channel_id=1, source_target_pairs={{0,8},{4,12},{8,0},{12,4},{1,9},{5,13},{9,1},{13,5},{2,10},{6,14},... | collective-permute-start | bytes 393224 | tf_op jit(solution)/shard_map/ppermute | solution.py:585
  48.6 7.6 %collective-permute-start.9 = (bf16[256,256]{1,0:T(8,128)(2,1)S(1)}, bf16[256,256]{1,0:T(8,128)(2,1)S(1)}, u32[]{:S(2)}, u32[]{:S(2)}) collective-permute-start(bf16[256,256]{1,0:T(8,128)(2,1)S(1)} %get-tuple-element.152.refs_0_), channel_id=1, source_target_pairs={{0,4},{4,8},{8,12},{12,0},{1,5},{5,9},{9,13},{13,1},{2,6},{6,10},{... | collective-permute-start | bytes 393224 | tf_op jit(solution)/shard_map/ppermute | solution.py:585
  56.7 1.6 %collective-permute-start.11 = (bf16[2,64,1024]{2,1,0:T(8,128)(2,1)S(1)}, bf16[2,64,1024]{2,1,0:T(8,128)(2,1)S(1)}, u32[]{:S(2)}, u32[]{:S(2)}) collective-permute-start(bf16[2,64,1024]{2,1,0:T(8,128)(2,1)S(1)} %get-tuple-element.161._), channel_id=1, source_target_pairs={{0,1},{1,0},{2,3},{3,2},{4,5},{5,4},{6,7},{7,6},{8,9},{9,8},{10,11... | collective-permute-start | bytes 786440 | tf_op jit(solution)/shard_map/ppermute | solution.py:591
  58.4 8.4 %collective-permute-start.12 = (bf16[2,64,1024]{2,1,0:T(8,128)(2,1)S(1)}, bf16[2,64,1024]{2,1,0:T(8,128)(2,1)S(1)}, u32[]{:S(2)}, u32[]{:S(2)}) collective-permute-start(bf16[2,64,1024]{2,1,0:T(8,128)(2,1)S(1)} %add_convert_fusion.near_ref), channel_id=1, source_target_pairs={{0,2},{1,3},{2,0},{3,1},{4,6},{5,7},{6,4},{7,5},{8,10},{9,11},{10,... | collective-permute-start | bytes 786440 | tf_op jit(solution)/shard_map/ppermute | solution.py:594
  67.2 9.3 %collective-permute-start.14 = (bf16[64,1024]{1,0:T(8,128)(2,1)S(1)}, bf16[64,1024]{1,0:T(8,128)(2,1)S(1)}, u32[]{:S(2)}, u32[]{:S(2)}) collective-permute-start(bf16[64,1024]{1,0:T(8,128)(2,1)S(1)} %get-tuple-element.166._), channel_id=1, source_target_pairs={{0,0},{1,4},{2,8},{3,12},{4,1},{5,5},{6,9},{7,13},{8,2},{9,6},{10,... | collective-permute-start | bytes 393224 | tf_op jit(solution)/shard_map/ppermute | solution.py:679
  67.9 9.7 %collective-permute-start.13 = (bf16[2,48,1024]{2,1,0:T(8,128)(2,1)S(1)}, bf16[2,48,1024]{2,1,0:T(8,128)(2,1)S(1)}, u32[]{:S(2)}, u32[]{:S(2)}) collective-permute-start(bf16[2,48,1024]{2,1,0:T(8,128)(2,1)S(1)} %get-tuple-element.165), channel_id=1, source_target_pairs={{0,4},{4,8},{8,12},{12,0},{1,5},{5,9},{9,13},{13,1},{2,6},{6,10},{... | collective-permute-start | bytes 589832 | tf_op jit(solution)/shard_map/ppermute | solution.py:585
  70.1 11.2 %collective-permute-start.15 = (bf16[2,48,1024]{2,1,0:T(8,128)(2,1)S(1)}, bf16[2,48,1024]{2,1,0:T(8,128)(2,1)S(1)}, u32[]{:S(2)}, u32[]{:S(2)}) collective-permute-start(bf16[2,48,1024]{2,1,0:T(8,128)(2,1)S(1)} %get-tuple-element.170), channel_id=1, source_target_pairs={{0,8},{4,12},{8,0},{12,4},{1,9},{5,13},{9,1},{13,5},{2,10},{6,14},... | collective-permute-start | bytes 589832 | tf_op jit(solution)/shard_map/ppermute | solution.py:585
  73.1 11.1 %collective-permute-start.16 = (bf16[2,48,1024]{2,1,0:T(8,128)(2,1)S(1)}, bf16[2,48,1024]{2,1,0:T(8,128)(2,1)S(1)}, u32[]{:S(2)}, u32[]{:S(2)}) collective-permute-start(bf16[2,48,1024]{2,1,0:T(8,128)(2,1)S(1)} %get-tuple-element.171), channel_id=1, source_target_pairs={{0,12},{4,0},{8,4},{12,8},{1,13},{5,1},{9,5},{13,9},{2,14},{6,2},{... | collective-permute-start | bytes 589832 | tf_op jit(solution)/shard_map/ppermute | solution.py:585
  75.7 9.2 %collective-permute-start.17 = (bf16[2,48,1024]{2,1,0:T(8,128)(2,1)S(1)}, bf16[2,48,1024]{2,1,0:T(8,128)(2,1)S(1)}, u32[]{:S(2)}, u32[]{:S(2)}) collective-permute-start(bf16[2,48,1024]{2,1,0:T(8,128)(2,1)S(1)} %get-tuple-element.168.refs_0_), channel_id=1, source_target_pairs={{0,1},{1,0},{2,3},{3,2},{4,5},{5,4},{6,7},{7,6},{8,9},{9,8},{10,11... | collective-permute-start | bytes 589832 | tf_op jit(solution)/shard_map/ppermute | solution.py:591
  81.3 3.5 %collective-permute-start.19 = (bf16[2,48,1024]{2,1,0:T(8,128)(2,1)S(1)}, bf16[2,48,1024]{2,1,0:T(8,128)(2,1)S(1)}, u32[]{:S(2)}, u32[]{:S(2)}) collective-permute-start(bf16[2,48,1024]{2,1,0:T(8,128)(2,1)S(1)} %collective-permute-done.15.refs_2_), channel_id=1, source_target_pairs={{0,1},{1,0},{2,3},{3,2},{4,5},{5,4},{6,7},{7,6},{8,9},{9,8},{10,11... | collective-permute-start | bytes 589832 | tf_op jit(solution)/shard_map/ppermute | solution.py:591
  84.2 1.4 %collective-permute-start.20 = (bf16[2,48,1024]{2,1,0:T(8,128)(2,1)S(1)}, bf16[2,48,1024]{2,1,0:T(8,128)(2,1)S(1)}, u32[]{:S(2)}, u32[]{:S(2)}) collective-permute-start(bf16[2,48,1024]{2,1,0:T(8,128)(2,1)S(1)} %collective-permute-done.16.refs_3_), channel_id=1, source_target_pairs={{0,1},{1,0},{2,3},{3,2},{4,5},{5,4},{6,7},{7,6},{8,9},{9,8},{10,11... | collective-permute-start | bytes 589832 | tf_op jit(solution)/shard_map/ppermute | solution.py:591
  84.2 1.7 %collective-permute-start.18 = (bf16[2,48,1024]{2,1,0:T(8,128)(2,1)S(1)}, bf16[2,48,1024]{2,1,0:T(8,128)(2,1)S(1)}, u32[]{:S(2)}, u32[]{:S(2)}) collective-permute-start(bf16[2,48,1024]{2,1,0:T(8,128)(2,1)S(1)} %collective-permute-done.13.refs_1_), channel_id=1, source_target_pairs={{0,1},{1,0},{2,3},{3,2},{4,5},{5,4},{6,7},{7,6},{8,9},{9,8},{10,11... | collective-permute-start | bytes 589832 | tf_op jit(solution)/shard_map/ppermute | solution.py:591
  91.9 2.4 %collective-permute-start.21 = (bf16[2,192,1024]{2,1,0:T(8,128)(2,1)S(1)}, bf16[2,192,1024]{2,1,0:T(8,128)(2,1)S(1)}, u32[]{:S(2)}, u32[]{:S(2)}) collective-permute-start(bf16[2,192,1024]{2,1,0:T(8,128)(2,1)S(1)} %get-tuple-element.177), channel_id=1, source_target_pairs={{0,1},{1,0},{2,3},{3,2},{4,5},{5,4},{6,7},{7,6},{8,9},{9,8},{10,11... | collective-permute-start | bytes 2359304 | tf_op jit(solution)/shard_map/ppermute | solution.py:591
  94.4 8.3 %collective-permute-start.22 = (bf16[2,48,1024]{2,1,0:T(8,128)(2,1)S(1)}, bf16[2,48,1024]{2,1,0:T(8,128)(2,1)S(1)}, u32[]{:S(2)}, u32[]{:S(2)}) collective-permute-start(bf16[2,48,1024]{2,1,0:T(8,128)(2,1)S(1)} %get-tuple-element.179), channel_id=1, source_target_pairs={{0,4},{4,8},{8,12},{12,0},{1,5},{5,9},{9,13},{13,1},{2,6},{6,10},{... | collective-permute-start | bytes 589832 | tf_op jit(solution)/shard_map/ppermute | solution.py:585
  94.5 13.3 %collective-permute-start.23 = (bf16[2,48,1024]{2,1,0:T(8,128)(2,1)S(1)}, bf16[2,48,1024]{2,1,0:T(8,128)(2,1)S(1)}, u32[]{:S(2)}, u32[]{:S(2)}) collective-permute-start(bf16[2,48,1024]{2,1,0:T(8,128)(2,1)S(1)} %get-tuple-element.180), channel_id=1, source_target_pairs={{0,8},{4,12},{8,0},{12,4},{1,9},{5,13},{9,1},{13,5},{2,10},{6,14},... | collective-permute-start | bytes 589832 | tf_op jit(solution)/shard_map/ppermute | solution.py:585
  98.6 9.2 %collective-permute-start.24 = (bf16[2,48,1024]{2,1,0:T(8,128)(2,1)S(1)}, bf16[2,48,1024]{2,1,0:T(8,128)(2,1)S(1)}, u32[]{:S(2)}, u32[]{:S(2)}) collective-permute-start(bf16[2,48,1024]{2,1,0:T(8,128)(2,1)S(1)} %get-tuple-element.181), channel_id=1, source_target_pairs={{0,12},{4,0},{8,4},{12,8},{1,13},{5,1},{9,5},{13,9},{2,14},{6,2},{... | collective-permute-start | bytes 589832 | tf_op jit(solution)/shard_map/ppermute | solution.py:585
  108.3 5.0 %collective-permute-start.25 = (bf16[64,1024]{1,0:T(8,128)(2,1)S(1)}, bf16[64,1024]{1,0:T(8,128)(2,1)S(1)}, u32[]{:S(2)}, u32[]{:S(2)}) collective-permute-start(bf16[64,1024]{1,0:T(8,128)(2,1)S(1)} %get-tuple-element.183), channel_id=1, source_target_pairs={{0,2},{1,3},{2,0},{3,1},{4,6},{5,7},{6,4},{7,5},{8,10},{9,11},{10,... | collective-permute-start | bytes 393224 | tf_op jit(solution)/shard_map/ppermute | solution.py:594
  (6 other events, 66.4 us)

commit v4 on v3

--- a/solution.py
+++ b/solution.py
@@ -170,7 +170,7 @@
     )(wide_at, owner_slot, lang_ids.reshape(-1, 128), queries)
 
 
-def routed_kernel(counts, q_ref, kv_from, out_ref, kv_ref, attended, kv_sem):
+def routed_kernel(counts, q_ref, kv_from, out_ref, kv_ref, lined, attended, kv_sem):
     sources, span, width = q_ref.shape
     kv_copy = pltpu.make_async_copy(kv_from, kv_ref, kv_sem)
     kv_copy.start()
@@ -186,16 +186,22 @@
         first = jnp.where(lane < counts[source], begins[source] + lane, -1)
         second = jnp.where(lane - span < counts[source + 1], begins[source + 1] + lane - span, -1)
         ranks.append(jnp.where(lane < span, first, second))
-    kv_copy.wait()
-
-    def block(index, _):
+
+    def pack(index, _):
         begin = pl.multiple_of(index * ROWS_BLOCK, ROWS_BLOCK)
         query = jnp.zeros((ROWS_BLOCK, width), F32)
         for pair, rank in enumerate(ranks):
             pick = one_hot(iota((ROWS_BLOCK, 2 * span), 0) + begin == rank)
             query = query + dot(pick, q_ref[2 * pair : 2 * pair + 2].reshape(2 * span, width))
-        total = attend_block((query * HEAD_DIM**-0.5).astype(BF16), kv_ref)
-        attended[pl.ds(begin, ROWS_BLOCK), :] = total.astype(BF16)
+        lined[pl.ds(begin, ROWS_BLOCK), :] = (query * HEAD_DIM**-0.5).astype(BF16)
+        return 0
+
+    lax.fori_loop(0, blocks, pack, 0)
+    kv_copy.wait()
+
+    def block(index, _):
+        here = pl.ds(pl.multiple_of(index * ROWS_BLOCK, ROWS_BLOCK), ROWS_BLOCK)
+        attended[here, :] = attend_block(lined[here, :], kv_ref).astype(BF16)
         return 0
 
     lax.fori_loop(0, blocks, block, 0)
@@ -221,6 +227,7 @@
         out_specs=in_vmem,
         scratch_shapes=[
             pltpu.VMEM(keys_values.shape, BF16),
+            pltpu.VMEM((capacity, width), BF16),
             pltpu.VMEM((capacity, width), BF16),
             pltpu.SemaphoreType.DMA,
         ],

time: 115 us -> 114 us (level)
  transfers between devices with their start and end apart: 24 -> 24, of which waited for: 17 -> 18; matrix products, arithmetic and copies ran while one was open for 6% -> 6% of each run, Pallas kernels for 9% -> 9%
where the time goes in v4:
time: 114 us; the launch traced here: 113 us
  starting transfers between devices  41.6 us (36%)
  waiting for transfers between devices  38.7 us (34%)
  Pallas kernels  20.3 us (18%)
  local copies, waits for them, and re-layouts  9.25 us (8%)
  other arithmetic  2.47 us (2%)
    ppermute x12, waiting for transfers between devices, around(): lax.ppermute(values[step], 'narrow', ring(narrow_count, step))  25.6 us
    ppermute x12, starting transfers between devices, around(): lax.ppermute(values[step], 'narrow', ring(narrow_count, step))  22.2 us
    all_to_all x1, starting transfers between devices, exchanged(): lax.all_to_all(boxes, 'wide', split_axis=0, concat_axis=0, tiled=True)  7.9 us
    pallas_call x1, Pallas kernels, expert(): pl.pallas_call(expert_kernel, out_shape=(jax.ShapeDtypeStruct((2, rows, q...  5.92 us
    ppermute x2, waiting for transfers between devices, to_far(): return lax.ppermute(value, 'depth', far_perm)  5.87 us
    all_to_all x1, starting transfers between devices, exchanged(): lax.all_to_all(partial, 'wide', split_axis=0, concat_axis=0, tiled=True)  5.15 us
    pallas_call x1, Pallas kernels, attend_routed(): pl.pallas_call(routed_kernel, out_shape=jax.ShapeDtypeStruct(queries.shap...  4.31 us
    all_to_all x1, waiting for transfers between devices, exchanged(): lax.all_to_all(boxes, 'wide', split_axis=0, concat_axis=0, tiled=True)  4.21 us
  transfers between devices with their start and end apart: 24, of which 18 were waited for; matrix products, arithmetic and copies ran while one was open for 6% of the time, Pallas kernels for 9%

profile of v4, /device:TPU:0, one launch (start us, length us, event | category | flops | bytes accessed | tf_op | source)
XLA Modules:
  0.0 113.3 jit_solution(12793984173371971035)
XLA Ops:
  0.0 2.2 %route.1 = (bf16[8,128,256]{2,1,0:T(8,128)(2,1)}, s32[8,256]{1,0:T(8,128)S(1)}, s32[8]{0:T(128)S(1)}, s32[1]{0:T(128)}) custom-call(s32[1]{0:T(128)} %bitcast.34.place, s32[8]{0:T(128)} %slot_of.1, s32[16,128]{1,0:T(8,128)} %bitcast.71, bf16[256,256]{1,0:T(8,128)(2,1)} %q_ref.1), custom_call_target="tpu_custom_call" | custom-call | flops 100000000 | bytes 1000000 | tf_op jit(solution)/shard_map/route/pallas_call | solution.py:157
  2.9 40.3 %conditional.1 = (bf16[256,256]{1,0:T(8,128)(2,1)S(1)}, bf16[256,1024]{1,0:T(8,128)(2,1)S(1)}, bf16[256,1024]{1,0:T(8,128)(2,1)}, bf16[256,1024]{1,0:T(8,128)(2,...) conditional(s32[]{:T(128)} %bitcast.36, (s32[]{:T(128)}, ...), branch_computations={%region_0.6_spmd, %region_6.10_spmd} | conditional | flops 1100189184 | bytes 23979870 | solution.py:674
  2.9 7.9 %all-to-all-start.2 = ((bf16[8,128,256]{2,1,0:T(8,128)(2,1)}), bf16[8,128,256]{2,1,0:T(8,128)(2,1)S(1)}, u32[]{:S(2)}, u32[]{:S(2)}) async-start(bf16[8,128,256]{2,1,0:T(8,128)(2,1)} %get-tuple-element.87), calls=%async_computation.2 | async-start | bytes 1048576 | tf_op jit(solution)/shard_map/cond/branch_1_fun/all_to_all | solution.py:645
  12.5 3.1 %collective-permute-start.6 = (bf16[256,1024]{1,0:T(8,128)(2,1)S(1)}, bf16[256,1024]{1,0:T(8,128)(2,1)}, u32[]{:S(2)}, u32[]{:S(2)}) collective-permute-start(bf16[256,1024]{1,0:T(8,128)(2,1)S(1)} %get-tuple-element.188), channel_id=1, source_target_pairs={{0,12},{4,0},{8,4},{12,8},{1,13},{5,1},{9,5},{13,9},{2,14},{6,2},{... | collective-permute-start | bytes 1572872 | tf_op jit(solution)/shard_map/cond/branch_1_fun/ppermute | solution.py:592
  18.2 4.2 %all-to-all-done.2.q_ref = bf16[8,128,256]{2,1,0:T(8,128)(2,1)S(1)} async-done(((bf16[8,128,256]{2,1,0:T(8,128)(2,1)}), bf16[8,128,256]{2,1,0:T(8,128)(2,1)S(1)}, u32[]{:S(2)}, u32[]{:S(2)}) %all-to-all-start.2) | async-done | bytes 524320 | tf_op jit(solution)/shard_map/cond/branch_1_fun/all_to_all | solution.py:645
  22.4 4.3 %attend.3 = bf16[8,128,256]{2,1,0:T(8,128)(2,1)} custom-call(s32[8]{0:T(128)S(1)} %get-tuple-element.86.counts, bf16[8,128,256]{2,1,0:T(8,128)(2,1)S(1)} %all-to-all-done.2.q_ref, bf16[2,768,256]{2,1,0:T(8,128)(2,1)} %bitcast.73), custom_call_target="tpu_custom_call" | custom-call | flops 1000000000 | bytes 4000000 | tf_op jit(solution)/shard_map/cond/branch_1_fun/attend/pallas_call | solution.py:219
  26.9 5.1 %all-to-all-start.3 = ((bf16[8,128,256]{2,1,0:T(8,128)(2,1)}), bf16[8,128,256]{2,1,0:T(8,128)(2,1)S(1)}, u32[]{:S(2)}, u32[]{:S(2)}) async-start(bf16[8,128,256]{2,1,0:T(8,128)(2,1)} %attend.3), calls=%async_computation.3 | async-start | bytes 1048576 | tf_op jit(solution)/shard_map/cond/branch_1_fun/all_to_all | solution.py:650
  32.7 2.1 %collective-permute-start.7 = (bf16[64,1024]{1,0:T(8,128)(2,1)}, bf16[64,1024]{1,0:T(8,128)(2,1)}, u32[]{:S(2)}, u32[]{:S(2)}) collective-permute-start(bf16[64,1024]{1,0:T(8,128)(2,1)} %get-tuple-element.97), channel_id=1, source_target_pairs={{0,0},{1,4},{2,8},{3,12},{4,1},{5,5},{6,9},{7,13},{8,2},{9,6},{10,... | collective-permute-start | bytes 393224 | tf_op jit(solution)/shard_map/cond/branch_1_fun/ppermute | solution.py:628
  37.8 3.7 %collective-permute-done.4 = bf16[256,1024]{1,0:T(8,128)(2,1)} collective-permute-done((bf16[256,1024]{1,0:T(8,128)(2,1)S(1)}, bf16[256,1024]{1,0:T(8,128)(2,1)}, u32[]{:S(2)}, u32[]{:S(2)}) %collective-permute-start.4) | collective-permute-done | bytes 524320 | tf_op jit(solution)/shard_map/cond/branch_1_fun/ppermute | solution.py:592
  43.2 4.6 %collective-permute-start.8 = (bf16[256,256]{1,0:T(8,128)(2,1)S(1)}, bf16[256,256]{1,0:T(8,128)(2,1)S(1)}, u32[]{:S(2)}, u32[]{:S(2)}) collective-permute-start(bf16[256,256]{1,0:T(8,128)(2,1)S(1)} %get-tuple-element.152.refs_0_), channel_id=1, source_target_pairs={{0,12},{4,0},{8,4},{12,8},{1,13},{5,1},{9,5},{13,9},{2,14},{6,2},{... | collective-permute-start | bytes 393224 | tf_op jit(solution)/shard_map/ppermute | solution.py:592
  48.8 3.0 %collective-permute-done.8.refs_1_ = bf16[256,256]{1,0:T(8,128)(2,1)S(1)} collective-permute-done((bf16[256,256]{1,0:T(8,128)(2,1)S(1)}, bf16[256,256]{1,0:T(8,128)(2,1)S(1)}, u32[]{:S(2)}, u32[]{:S(2)}) %collective-permute-start.8) | collective-permute-done | bytes 131104 | tf_op jit(solution)/shard_map/ppermute | solution.py:592
  51.7 2.4 %begin.1 = (f32[256,1024]{1,0:T(8,128)S(1)}, bf16[256,1024]{1,0:T(8,128)(2,1)S(1)}, bf16[256,1024]{1,0:T(8,128)(2,1)S(1)}) custom-call(bf16[256,256]{1,0:T(8,128)(2,1)S(1)} %get-tuple-element.152.refs_0_, bf16[256,256]{1,0:T(8,128)(2,1)S(1)} %collective-permute-done.8.refs_1_, bf16[256,1024]{1,0:T(8,128)(2,1)S(1)} %get-tuple-element.153.refs_2_, ...), custom_call_target="tpu_custom_call" | custom-call | flops 500000000 | bytes 2000000 | tf_op jit(solution)/shard_map/begin/pallas_call | solution.py:303
  58.6 4.2 %copy-done = bf16[1,4096,1280]{2,1,0:T(8,128)(2,1)S(1)} copy-done((bf16[1,4096,1280]{2,1,0:T(8,128)(2,1)S(1)}, bf16[1,4096,1280]{2,1,0:T(8,128)(2,1)}, u32[]{:S(2)}) %copy-start) | copy-done | bytes 10485784
  63.6 2.5 %collective-permute-done.12.got_ref = bf16[2,64,1024]{2,1,0:T(8,128)(2,1)S(1)} collective-permute-done((bf16[2,64,1024]{2,1,0:T(8,128)(2,1)S(1)}, bf16[2,64,1024]{2,1,0:T(8,128)(2,1)S(1)}, u32[]{:S(2)}, u32[]{:S(2)}) %collective-permute-start.12) | collective-permute-done | bytes 262176 | tf_op jit(solution)/shard_map/ppermute | solution.py:601
  67.1 2.2 %collective-permute-start.13 = (bf16[2,48,1024]{2,1,0:T(8,128)(2,1)S(1)}, bf16[2,48,1024]{2,1,0:T(8,128)(2,1)S(1)}, u32[]{:S(2)}, u32[]{:S(2)}) collective-permute-start(bf16[2,48,1024]{2,1,0:T(8,128)(2,1)S(1)} %get-tuple-element.165), channel_id=1, source_target_pairs={{0,4},{4,8},{8,12},{12,0},{1,5},{5,9},{9,13},{13,1},{2,6},{6,10},{... | collective-permute-start | bytes 589832 | tf_op jit(solution)/shard_map/ppermute | solution.py:592
  69.3 3.0 %collective-permute-start.15 = (bf16[2,48,1024]{2,1,0:T(8,128)(2,1)S(1)}, bf16[2,48,1024]{2,1,0:T(8,128)(2,1)S(1)}, u32[]{:S(2)}, u32[]{:S(2)}) collective-permute-start(bf16[2,48,1024]{2,1,0:T(8,128)(2,1)S(1)} %get-tuple-element.170), channel_id=1, source_target_pairs={{0,8},{4,12},{8,0},{12,4},{1,9},{5,13},{9,1},{13,5},{2,10},{6,14},... | collective-permute-start | bytes 589832 | tf_op jit(solution)/shard_map/ppermute | solution.py:592
  72.4 2.5 %collective-permute-start.16 = (bf16[2,48,1024]{2,1,0:T(8,128)(2,1)S(1)}, bf16[2,48,1024]{2,1,0:T(8,128)(2,1)S(1)}, u32[]{:S(2)}, u32[]{:S(2)}) collective-permute-start(bf16[2,48,1024]{2,1,0:T(8,128)(2,1)S(1)} %get-tuple-element.171), channel_id=1, source_target_pairs={{0,12},{4,0},{8,4},{12,8},{1,13},{5,1},{9,5},{13,9},{2,14},{6,2},{... | collective-permute-start | bytes 589832 | tf_op jit(solution)/shard_map/ppermute | solution.py:592
  76.9 3.7 %collective-permute-done.15.refs_2_ = bf16[2,48,1024]{2,1,0:T(8,128)(2,1)S(1)} collective-permute-done((bf16[2,48,1024]{2,1,0:T(8,128)(2,1)S(1)}, bf16[2,48,1024]{2,1,0:T(8,128)(2,1)S(1)}, u32[]{:S(2)}, u32[]{:S(2)}) %collective-permute-start.15) | collective-permute-done | bytes 196640 | tf_op jit(solution)/shard_map/ppermute | solution.py:592
  80.6 2.9 %collective-permute-done.16.refs_3_ = bf16[2,48,1024]{2,1,0:T(8,128)(2,1)S(1)} collective-permute-done((bf16[2,48,1024]{2,1,0:T(8,128)(2,1)S(1)}, bf16[2,48,1024]{2,1,0:T(8,128)(2,1)S(1)}, u32[]{:S(2)}, u32[]{:S(2)}) %collective-permute-start.16) | collective-permute-done | bytes 196640 | tf_op jit(solution)/shard_map/ppermute | solution.py:592
  85.2 5.9 %expert.1 = (bf16[2,192,1024]{2,1,0:T(8,128)(2,1)S(1)}, bf16[192,1280]{1,0:T(8,128)(2,1)S(1)}, f32[192,128]{1,0:T(8,128)S(1)}) custom-call(s32[2]{0:T(128)S(1)} %pad_add_fusion.place, bf16[2,48,1024]{2,1,0:T(8,128)(2,1)S(1)} %get-tuple-element.168.refs_0_, bf16[2,48,1024]{2,1,0:T(8,128)(2,1)S(1)} %collective-permute-done.13.refs_1_, ...), custom_call_target="tpu_custom_call" | custom-call | flops 4000000000 | bytes 24000000 | tf_op jit(solution)/shard_map/expert/pallas_call | solution.py:473
  93.7 4.1 %collective-permute-start.23 = (bf16[2,48,1024]{2,1,0:T(8,128)(2,1)S(1)}, bf16[2,48,1024]{2,1,0:T(8,128)(2,1)S(1)}, u32[]{:S(2)}, u32[]{:S(2)}) collective-permute-start(bf16[2,48,1024]{2,1,0:T(8,128)(2,1)S(1)} %get-tuple-element.180), channel_id=1, source_target_pairs={{0,8},{4,12},{8,0},{12,4},{1,9},{5,13},{9,1},{13,5},{2,10},{6,14},... | collective-permute-start | bytes 589832 | tf_op jit(solution)/shard_map/ppermute | solution.py:592
  97.8 4.2 %collective-permute-done.22.refs_1_ = bf16[2,48,1024]{2,1,0:T(8,128)(2,1)S(1)} collective-permute-done((bf16[2,48,1024]{2,1,0:T(8,128)(2,1)S(1)}, bf16[2,48,1024]{2,1,0:T(8,128)(2,1)S(1)}, u32[]{:S(2)}, u32[]{:S(2)}) %collective-permute-start.22) | collective-permute-done | bytes 196640 | tf_op jit(solution)/shard_map/ppermute | solution.py:592
  102.0 5.1 %collective-permute-done.23.refs_2_ = bf16[2,48,1024]{2,1,0:T(8,128)(2,1)S(1)} collective-permute-done((bf16[2,48,1024]{2,1,0:T(8,128)(2,1)S(1)}, bf16[2,48,1024]{2,1,0:T(8,128)(2,1)S(1)}, u32[]{:S(2)}, u32[]{:S(2)}) %collective-permute-start.23) | collective-permute-done | bytes 196640 | tf_op jit(solution)/shard_map/ppermute | solution.py:592
  109.2 3.3 %collective-permute-done.25 = bf16[64,1024]{1,0:T(8,128)(2,1)S(1)} collective-permute-done((bf16[64,1024]{1,0:T(8,128)(2,1)S(1)}, bf16[64,1024]{1,0:T(8,128)(2,1)S(1)}, u32[]{:S(2)}, u32[]{:S(2)}) %collective-permute-start.25) | collective-permute-done | bytes 131104 | tf_op jit(solution)/shard_map/ppermute | solution.py:601
  (88 shorter events, 26.0 us)
Async XLA Ops:
  2.9 19.5 %all-to-all-start.2 = ((bf16[8,128,256]{2,1,0:T(8,128)(2,1)}), bf16[8,128,256]{2,1,0:T(8,128)(2,1)S(1)}, u32[]{:S(2)}, u32[]{:S(2)}) async-start(bf16[8,128,256]{2,1,0:T(8,128)(2,1)} %get-tuple-element.87), calls=%async_computation.2 | async-start | bytes 1048576 | tf_op jit(solution)/shard_map/cond/branch_1_fun/all_to_all | solution.py:645
  12.5 25.3 %collective-permute-start.6 = (bf16[256,1024]{1,0:T(8,128)(2,1)S(1)}, bf16[256,1024]{1,0:T(8,128)(2,1)}, u32[]{:S(2)}, u32[]{:S(2)}) collective-permute-start(bf16[256,1024]{1,0:T(8,128)(2,1)S(1)} %get-tuple-element.188), channel_id=1, source_target_pairs={{0,12},{4,0},{8,4},{12,8},{1,13},{5,1},{9,5},{13,9},{2,14},{6,2},{... | collective-permute-start | bytes 1572872 | tf_op jit(solution)/shard_map/cond/branch_1_fun/ppermute | solution.py:592
  15.6 22.2 %collective-permute-start.5 = (bf16[256,1024]{1,0:T(8,128)(2,1)S(1)}, bf16[256,1024]{1,0:T(8,128)(2,1)}, u32[]{:S(2)}, u32[]{:S(2)}) collective-permute-start(bf16[256,1024]{1,0:T(8,128)(2,1)S(1)} %get-tuple-element.189), channel_id=1, source_target_pairs={{0,8},{4,12},{8,0},{12,4},{1,9},{5,13},{9,1},{13,5},{2,10},{6,14},... | collective-permute-start | bytes 1572872 | tf_op jit(solution)/shard_map/cond/branch_1_fun/ppermute | solution.py:592
  16.2 25.3 %collective-permute-start.4 = (bf16[256,1024]{1,0:T(8,128)(2,1)S(1)}, bf16[256,1024]{1,0:T(8,128)(2,1)}, u32[]{:S(2)}, u32[]{:S(2)}) collective-permute-start(bf16[256,1024]{1,0:T(8,128)(2,1)S(1)} %get-tuple-element.190), channel_id=1, source_target_pairs={{0,4},{4,8},{8,12},{12,0},{1,5},{5,9},{9,13},{13,1},{2,6},{6,10},{... | collective-permute-start | bytes 1572872 | tf_op jit(solution)/shard_map/cond/branch_1_fun/ppermute | solution.py:592
  26.9 15.6 %all-to-all-start.3 = ((bf16[8,128,256]{2,1,0:T(8,128)(2,1)}), bf16[8,128,256]{2,1,0:T(8,128)(2,1)S(1)}, u32[]{:S(2)}, u32[]{:S(2)}) async-start(bf16[8,128,256]{2,1,0:T(8,128)(2,1)} %attend.3), calls=%async_computation.3 | async-start | bytes 1048576 | tf_op jit(solution)/shard_map/cond/branch_1_fun/all_to_all | solution.py:650
  32.7 8.9 %collective-permute-start.7 = (bf16[64,1024]{1,0:T(8,128)(2,1)}, bf16[64,1024]{1,0:T(8,128)(2,1)}, u32[]{:S(2)}, u32[]{:S(2)}) collective-permute-start(bf16[64,1024]{1,0:T(8,128)(2,1)} %get-tuple-element.97), channel_id=1, source_target_pairs={{0,0},{1,4},{2,8},{3,12},{4,1},{5,5},{6,9},{7,13},{8,2},{9,6},{10,... | collective-permute-start | bytes 393224 | tf_op jit(solution)/shard_map/cond/branch_1_fun/ppermute | solution.py:628
  43.2 8.5 %collective-permute-start.8 = (bf16[256,256]{1,0:T(8,128)(2,1)S(1)}, bf16[256,256]{1,0:T(8,128)(2,1)S(1)}, u32[]{:S(2)}, u32[]{:S(2)}) collective-permute-start(bf16[256,256]{1,0:T(8,128)(2,1)S(1)} %get-tuple-element.152.refs_0_), channel_id=1, source_target_pairs={{0,12},{4,0},{8,4},{12,8},{1,13},{5,1},{9,5},{13,9},{2,14},{6,2},{... | collective-permute-start | bytes 393224 | tf_op jit(solution)/shard_map/ppermute | solution.py:592
  47.8 6.6 %collective-permute-start.10 = (bf16[256,256]{1,0:T(8,128)(2,1)S(1)}, bf16[256,256]{1,0:T(8,128)(2,1)S(1)}, u32[]{:S(2)}, u32[]{:S(2)}) collective-permute-start(bf16[256,256]{1,0:T(8,128)(2,1)S(1)} %get-tuple-element.152.refs_0_), channel_id=1, source_target_pairs={{0,8},{4,12},{8,0},{12,4},{1,9},{5,13},{9,1},{13,5},{2,10},{6,14},... | collective-permute-start | bytes 393224 | tf_op jit(solution)/shard_map/ppermute | solution.py:592
  47.8 7.6 %collective-permute-start.9 = (bf16[256,256]{1,0:T(8,128)(2,1)S(1)}, bf16[256,256]{1,0:T(8,128)(2,1)S(1)}, u32[]{:S(2)}, u32[]{:S(2)}) collective-permute-start(bf16[256,256]{1,0:T(8,128)(2,1)S(1)} %get-tuple-element.152.refs_0_), channel_id=1, source_target_pairs={{0,4},{4,8},{8,12},{12,0},{1,5},{5,9},{9,13},{13,1},{2,6},{6,10},{... | collective-permute-start | bytes 393224 | tf_op jit(solution)/shard_map/ppermute | solution.py:592
  55.9 1.6 %collective-permute-start.11 = (bf16[2,64,1024]{2,1,0:T(8,128)(2,1)S(1)}, bf16[2,64,1024]{2,1,0:T(8,128)(2,1)S(1)}, u32[]{:S(2)}, u32[]{:S(2)}) collective-permute-start(bf16[2,64,1024]{2,1,0:T(8,128)(2,1)S(1)} %get-tuple-element.161._), channel_id=1, source_target_pairs={{0,1},{1,0},{2,3},{3,2},{4,5},{5,4},{6,7},{7,6},{8,9},{9,8},{10,11... | collective-permute-start | bytes 786440 | tf_op jit(solution)/shard_map/ppermute | solution.py:598
  57.7 8.4 %collective-permute-start.12 = (bf16[2,64,1024]{2,1,0:T(8,128)(2,1)S(1)}, bf16[2,64,1024]{2,1,0:T(8,128)(2,1)S(1)}, u32[]{:S(2)}, u32[]{:S(2)}) collective-permute-start(bf16[2,64,1024]{2,1,0:T(8,128)(2,1)S(1)} %add_convert_fusion.near_ref), channel_id=1, source_target_pairs={{0,2},{1,3},{2,0},{3,1},{4,6},{5,7},{6,4},{7,5},{8,10},{9,11},{10,... | collective-permute-start | bytes 786440 | tf_op jit(solution)/shard_map/ppermute | solution.py:601
  66.5 9.3 %collective-permute-start.14 = (bf16[64,1024]{1,0:T(8,128)(2,1)S(1)}, bf16[64,1024]{1,0:T(8,128)(2,1)S(1)}, u32[]{:S(2)}, u32[]{:S(2)}) collective-permute-start(bf16[64,1024]{1,0:T(8,128)(2,1)S(1)} %get-tuple-element.166._), channel_id=1, source_target_pairs={{0,0},{1,4},{2,8},{3,12},{4,1},{5,5},{6,9},{7,13},{8,2},{9,6},{10,... | collective-permute-start | bytes 393224 | tf_op jit(solution)/shard_map/ppermute | solution.py:686
  67.1 9.7 %collective-permute-start.13 = (bf16[2,48,1024]{2,1,0:T(8,128)(2,1)S(1)}, bf16[2,48,1024]{2,1,0:T(8,128)(2,1)S(1)}, u32[]{:S(2)}, u32[]{:S(2)}) collective-permute-start(bf16[2,48,1024]{2,1,0:T(8,128)(2,1)S(1)} %get-tuple-element.165), channel_id=1, source_target_pairs={{0,4},{4,8},{8,12},{12,0},{1,5},{5,9},{9,13},{13,1},{2,6},{6,10},{... | collective-permute-start | bytes 589832 | tf_op jit(solution)/shard_map/ppermute | solution.py:592
  69.3 11.2 %collective-permute-start.15 = (bf16[2,48,1024]{2,1,0:T(8,128)(2,1)S(1)}, bf16[2,48,1024]{2,1,0:T(8,128)(2,1)S(1)}, u32[]{:S(2)}, u32[]{:S(2)}) collective-permute-start(bf16[2,48,1024]{2,1,0:T(8,128)(2,1)S(1)} %get-tuple-element.170), channel_id=1, source_target_pairs={{0,8},{4,12},{8,0},{12,4},{1,9},{5,13},{9,1},{13,5},{2,10},{6,14},... | collective-permute-start | bytes 589832 | tf_op jit(solution)/shard_map/ppermute | solution.py:592
  72.4 11.1 %collective-permute-start.16 = (bf16[2,48,1024]{2,1,0:T(8,128)(2,1)S(1)}, bf16[2,48,1024]{2,1,0:T(8,128)(2,1)S(1)}, u32[]{:S(2)}, u32[]{:S(2)}) collective-permute-start(bf16[2,48,1024]{2,1,0:T(8,128)(2,1)S(1)} %get-tuple-element.171), channel_id=1, source_target_pairs={{0,12},{4,0},{8,4},{12,8},{1,13},{5,1},{9,5},{13,9},{2,14},{6,2},{... | collective-permute-start | bytes 589832 | tf_op jit(solution)/shard_map/ppermute | solution.py:592
  74.9 9.2 %collective-permute-start.17 = (bf16[2,48,1024]{2,1,0:T(8,128)(2,1)S(1)}, bf16[2,48,1024]{2,1,0:T(8,128)(2,1)S(1)}, u32[]{:S(2)}, u32[]{:S(2)}) collective-permute-start(bf16[2,48,1024]{2,1,0:T(8,128)(2,1)S(1)} %get-tuple-element.168.refs_0_), channel_id=1, source_target_pairs={{0,1},{1,0},{2,3},{3,2},{4,5},{5,4},{6,7},{7,6},{8,9},{9,8},{10,11... | collective-permute-start | bytes 589832 | tf_op jit(solution)/shard_map/ppermute | solution.py:598
  80.6 3.5 %collective-permute-start.19 = (bf16[2,48,1024]{2,1,0:T(8,128)(2,1)S(1)}, bf16[2,48,1024]{2,1,0:T(8,128)(2,1)S(1)}, u32[]{:S(2)}, u32[]{:S(2)}) collective-permute-start(bf16[2,48,1024]{2,1,0:T(8,128)(2,1)S(1)} %collective-permute-done.15.refs_2_), channel_id=1, source_target_pairs={{0,1},{1,0},{2,3},{3,2},{4,5},{5,4},{6,7},{7,6},{8,9},{9,8},{10,11... | collective-permute-start | bytes 589832 | tf_op jit(solution)/shard_map/ppermute | solution.py:598
  83.5 1.4 %collective-permute-start.20 = (bf16[2,48,1024]{2,1,0:T(8,128)(2,1)S(1)}, bf16[2,48,1024]{2,1,0:T(8,128)(2,1)S(1)}, u32[]{:S(2)}, u32[]{:S(2)}) collective-permute-start(bf16[2,48,1024]{2,1,0:T(8,128)(2,1)S(1)} %collective-permute-done.16.refs_3_), channel_id=1, source_target_pairs={{0,1},{1,0},{2,3},{3,2},{4,5},{5,4},{6,7},{7,6},{8,9},{9,8},{10,11... | collective-permute-start | bytes 589832 | tf_op jit(solution)/shard_map/ppermute | solution.py:598
  83.5 1.7 %collective-permute-start.18 = (bf16[2,48,1024]{2,1,0:T(8,128)(2,1)S(1)}, bf16[2,48,1024]{2,1,0:T(8,128)(2,1)S(1)}, u32[]{:S(2)}, u32[]{:S(2)}) collective-permute-start(bf16[2,48,1024]{2,1,0:T(8,128)(2,1)S(1)} %collective-permute-done.13.refs_1_), channel_id=1, source_target_pairs={{0,1},{1,0},{2,3},{3,2},{4,5},{5,4},{6,7},{7,6},{8,9},{9,8},{10,11... | collective-permute-start | bytes 589832 | tf_op jit(solution)/shard_map/ppermute | solution.py:598
  91.1 2.4 %collective-permute-start.21 = (bf16[2,192,1024]{2,1,0:T(8,128)(2,1)S(1)}, bf16[2,192,1024]{2,1,0:T(8,128)(2,1)S(1)}, u32[]{:S(2)}, u32[]{:S(2)}) collective-permute-start(bf16[2,192,1024]{2,1,0:T(8,128)(2,1)S(1)} %get-tuple-element.177), channel_id=1, source_target_pairs={{0,1},{1,0},{2,3},{3,2},{4,5},{5,4},{6,7},{7,6},{8,9},{9,8},{10,11... | collective-permute-start | bytes 2359304 | tf_op jit(solution)/shard_map/ppermute | solution.py:598
  93.6 8.3 %collective-permute-start.22 = (bf16[2,48,1024]{2,1,0:T(8,128)(2,1)S(1)}, bf16[2,48,1024]{2,1,0:T(8,128)(2,1)S(1)}, u32[]{:S(2)}, u32[]{:S(2)}) collective-permute-start(bf16[2,48,1024]{2,1,0:T(8,128)(2,1)S(1)} %get-tuple-element.179), channel_id=1, source_target_pairs={{0,4},{4,8},{8,12},{12,0},{1,5},{5,9},{9,13},{13,1},{2,6},{6,10},{... | collective-permute-start | bytes 589832 | tf_op jit(solution)/shard_map/ppermute | solution.py:592
  93.7 13.3 %collective-permute-start.23 = (bf16[2,48,1024]{2,1,0:T(8,128)(2,1)S(1)}, bf16[2,48,1024]{2,1,0:T(8,128)(2,1)S(1)}, u32[]{:S(2)}, u32[]{:S(2)}) collective-permute-start(bf16[2,48,1024]{2,1,0:T(8,128)(2,1)S(1)} %get-tuple-element.180), channel_id=1, source_target_pairs={{0,8},{4,12},{8,0},{12,4},{1,9},{5,13},{9,1},{13,5},{2,10},{6,14},... | collective-permute-start | bytes 589832 | tf_op jit(solution)/shard_map/ppermute | solution.py:592
  97.8 9.2 %collective-permute-start.24 = (bf16[2,48,1024]{2,1,0:T(8,128)(2,1)S(1)}, bf16[2,48,1024]{2,1,0:T(8,128)(2,1)S(1)}, u32[]{:S(2)}, u32[]{:S(2)}) collective-permute-start(bf16[2,48,1024]{2,1,0:T(8,128)(2,1)S(1)} %get-tuple-element.181), channel_id=1, source_target_pairs={{0,12},{4,0},{8,4},{12,8},{1,13},{5,1},{9,5},{13,9},{2,14},{6,2},{... | collective-permute-start | bytes 589832 | tf_op jit(solution)/shard_map/ppermute | solution.py:592
  107.5 5.0 %collective-permute-start.25 = (bf16[64,1024]{1,0:T(8,128)(2,1)S(1)}, bf16[64,1024]{1,0:T(8,128)(2,1)S(1)}, u32[]{:S(2)}, u32[]{:S(2)}) collective-permute-start(bf16[64,1024]{1,0:T(8,128)(2,1)S(1)} %get-tuple-element.183), channel_id=1, source_target_pairs={{0,2},{1,3},{2,0},{3,1},{4,6},{5,7},{6,4},{7,5},{8,10},{9,11},{10,... | collective-permute-start | bytes 393224 | tf_op jit(solution)/shard_map/ppermute | solution.py:601
  (6 other events, 66.4 us)
